TPU v7x, 8 devices: a whole 2x2x1 slice. The times are simulated.
8 devices in a mesh: model: 8 (over z, y, x, core).
Axes of the slice: x: 2, y: 2, z: 1, core: 2. Of those that a mesh axis runs over, the one named last changes fastest.
Arguments:
- act_in: bfloat16 [2048, 18432], P('model')
- ln_gain: float32 [18432], replicated
- w_q: bfloat16 [18432, 12288], P(None, 'model')
- w_kv: bfloat16 [18432, 512], replicated
- w_o: bfloat16 [12288, 18432], P('model')
- positions: int32 [2048], replicated
Outputs:
- output 1: bfloat16 [2048, 18432], P('model')
- output 2: bfloat16 [2048, 256], replicated
- output 3: bfloat16 [2048, 256], replicated
All inputs are finite; a program needn't handle non-finite values.
Results may differ from a plain program's by a relative error of at most 0.0120546.
Values are sent between devices in bfloat16 or wider.
A program may use at most 1 GiB of HBM per device.

v0:
```python
import functools
import math

import jax
import jax.numpy as jnp
from jax import lax
from jax.experimental import pallas as pl
from jax.experimental.pallas import tpu as pltpu
from jax.sharding import PartitionSpec as P


NORM_EPS = 1e-6
LOG2E = math.log2(math.e)
VMEM_BYTES = 67043328
NORM_BYTES = 56 << 20
AXIS = "model"
CORE, XN, YN, DIAG = 1, 2, 4, 6
BF16, F32 = jnp.bfloat16, jnp.float32


def _norm_kernel(chunk, steps, x_ref, g_ref, *out_refs):
    rows, width = x_ref.shape
    n_chunks = width // chunk

    def cols(c):
        return pl.ds(pl.multiple_of(c * chunk, chunk), chunk)

    def load(c):
        return x_ref[:, cols(c)].astype(F32)

    def fold(v):
        acc = v[:, :128]
        for i in range(1, chunk // 128):
            acc = acc + v[:, i * 128:(i + 1) * 128]
        return acc

    def square(c, acc):
        d = load(c) - mean
        return acc + fold(d * d)

    zero = jnp.zeros((rows, 128), F32)
    mean = jnp.sum(lax.fori_loop(0, n_chunks, lambda c, acc: acc + fold(load(c)), zero), axis=1, keepdims=True) / width
    rstd = lax.rsqrt(jnp.sum(lax.fori_loop(0, n_chunks, square, zero), axis=1, keepdims=True) / width + NORM_EPS)
    for i, out_ref in enumerate(out_refs):
        @pl.when(pl.program_id(0) // steps == i)
        def _():
            def put(c, _):
                out_ref[:, cols(c)] = ((load(c) - mean) * rstd * g_ref[:, cols(c)]).astype(BF16)
                return 0

            lax.fori_loop(0, n_chunks, put, 0)


def _norm_first_kernel(chunk, x_hbm, g_hbm, out_ref, x_buf, g_buf, sem):
    copies = [pltpu.make_async_copy(x_hbm.at[pl.ds(0, x_buf.shape[0]), :], x_buf, sem.at[0]), pltpu.make_async_copy(g_hbm, g_buf, sem.at[1])]
    for c in copies:
        c.start()
    for c in copies:
        c.wait()
    _norm_kernel(chunk, 1, x_buf, g_buf, out_ref)


def norm_first(x, gain, rows):
    width = x.shape[1]
    hbm = pl.BlockSpec(memory_space=pltpu.HBM)
    return pl.pallas_call(
        functools.partial(_norm_first_kernel, 2048),
        grid=(1,),
        in_specs=[hbm, hbm],
        out_specs=pl.BlockSpec(memory_space=pltpu.VMEM),
        out_shape=pltpu.VMEM((rows, width), BF16),
        scratch_shapes=[pltpu.VMEM((rows, width), BF16), pltpu.VMEM(gain.shape, F32), pltpu.SemaphoreType.DMA((2,))],
        compiler_params=pltpu.CompilerParams(dimension_semantics=("arbitrary",), vmem_limit_bytes=NORM_BYTES),
        cost_estimate=pl.CostEstimate(flops=8 * rows * width, bytes_accessed=4 * rows * width, transcendentals=0),
        name="norm",
    )(x, gain)


def norm_rows(x, gain, first, piece, count, rows, stride=1):
    width = x.shape[1]
    steps = piece // rows

    def out_map(i):
        return lambda s: (jnp.clip(s - i * steps, 0, steps - 1), 0)

    return pl.pallas_call(
        functools.partial(_norm_kernel, 2048, steps),
        grid=(count * steps,),
        in_specs=[pl.BlockSpec((rows, width), lambda s: (first // rows + stride * s, 0)), pl.BlockSpec((1, width), lambda s: (0, 0))],
        out_specs=[pl.BlockSpec((rows, width), out_map(i)) for i in range(count)],
        out_shape=[jax.ShapeDtypeStruct((piece, width), BF16)] * count,
        compiler_params=pltpu.CompilerParams(dimension_semantics=("arbitrary",), vmem_limit_bytes=NORM_BYTES),
        cost_estimate=pl.CostEstimate(flops=8 * count * piece * width, bytes_accessed=4 * count * piece * width, transcendentals=0),
        name="norm",
    )(x, gain)


def _order_kernel(n, *refs):
    me = lax.axis_index(AXIS)
    for i in range(2):
        blocks, out = refs[i * n:(i + 1) * n], refs[2 * n + i]
        rows = blocks[0].shape[0]
        for m, block in enumerate(blocks):
            out[pl.ds(pl.multiple_of((me ^ m) * rows, rows), rows), :] = block[...]


def order_blocks(k_blocks, v_blocks):
    n = len(k_blocks)
    rows, cols = k_blocks[0].shape
    return pl.pallas_call(
        functools.partial(_order_kernel, n),
        in_specs=[pl.BlockSpec(memory_space=pltpu.VMEM)] * (2 * n),
        out_specs=[pl.BlockSpec(memory_space=pltpu.VMEM)] * 2,
        out_shape=[jax.ShapeDtypeStruct((rows * n, cols), BF16)] * 2,
        cost_estimate=pl.CostEstimate(flops=2 * rows * n * cols, bytes_accessed=8 * rows * n * cols, transcendentals=0),
        name="order",
    )(*k_blocks, *v_blocks)


def _unit_kernel(names, parts, n_lhs, n_out, index, *flat):
    r = dict(zip(names, flat))
    lhs = [r[f"lhs{i}"] for i in range(n_lhs)]
    outs = [r[f"out{i}"] for i in range(n_out)]
    ring, ring_sem, q_buf = r["ring"], r["ring_sem"], r["q_buf"]
    slots, chunk = ring.shape[:2]
    do_q, do_o = "q" in parts, "o" in parts
    rows, proj = q_buf.shape
    n_q = r["wq"].shape[0] // chunk if do_q else 0
    n_o = r["wo"].shape[1] // chunk if do_o else 0
    total = n_q + n_o

    def at(i):
        return pl.ds(pl.multiple_of(i * chunk, chunk), chunk)

    def wq_copy(i, slot):
        return pltpu.make_async_copy(r["wq"].at[at(i), :], ring.at[slot], ring_sem.at[slot])

    def wo_copy(i, slot):
        return pltpu.make_async_copy(r["wo"].at[:, at(i - n_q)], ring.at[slot], ring_sem.at[slot])

    def h_copies(i, slot):
        cps, first = [], 0
        for j, h in enumerate(lhs):
            n = h.shape[0]
            cps.append(pltpu.make_async_copy(h.at[:, at(i)], r["h_buf"].at[slot, pl.ds(first, n), :], r["h_sem"].at[slot, j]))
            first += n
        return cps

    def y_copies(i, slot):
        cps, first = [], 0
        for j, out in enumerate(outs):
            n = out.shape[0]
            cps.append(pltpu.make_async_copy(r["y_buf"].at[slot, pl.ds(first, n), :], out.at[:, at(i)], r["y_sem"].at[slot, j]))
            first += n
        return cps

    def fetch(i, slot):
        if do_q:
            @pl.when(i < n_q)
            def _():
                wq_copy(i, slot).start()
                for c in h_copies(i, slot):
                    c.start()
        if do_o:
            @pl.when((i >= n_q) & (i < total))
            def _():
                wo_copy(i, slot).start()

    for i in range(slots):
        if i < n_q:
            wq_copy(i, i).start()
            for c in h_copies(i, i):
                c.start()
        elif i < total:
            wo_copy(i, i).start()
    extra = []
    if do_o:
        row, col = (lax.broadcasted_iota(jnp.int32, (rows, rows), d) for d in (0, 1))
        mine = jnp.where(row == col, r["qpos"][index:index + 1, :], 0.0)
        r["q_col"][...] = jnp.sum(mine, axis=1, keepdims=True)
        for i, (name, buf) in enumerate((("k", r["k_buf"]), ("v", r["v_buf"]))):
            n = r["kv_sem"].shape[1]
            for m in range(n):
                block = r[f"{name}{m}"]
                rows_m = block.shape[0]
                extra.append(pltpu.make_async_copy(block, buf.at[pl.ds(m * rows_m, rows_m), :], r["kv_sem"].at[i, m]))
    for c in extra:
        c.start()

    if do_q:
        acc = r["acc"]
        acc[...] = jnp.zeros_like(acc)

        def q_step(i, _):
            slot = lax.rem(i, slots)
            wq_copy(i, slot).wait()
            for c in h_copies(i, slot):
                c.wait()
            acc[...] += jnp.dot(r["h_buf"][slot], ring[slot], preferred_element_type=F32)
            fetch(i + slots, slot)
            return 0

        lax.fori_loop(0, n_q, q_step, 0)
        if not do_o:
            cols = proj // n_out
            for i, out in enumerate(outs):
                out[...] = acc[:, i * cols:(i + 1) * cols].astype(BF16)
            return
        q_buf[...] = acc[...].astype(BF16)

    for c in extra:
        c.wait()
    k_buf, v_buf, o_buf, y_buf = r["k_buf"], r["v_buf"], r["o_buf"], r["y_buf"]
    head = k_buf.shape[1]
    heads = proj // head

    half = rows // 2

    def score(s_ref, n, b):
        cols = pl.ds(pl.multiple_of(n * head, head), head)
        s_ref[...] = lax.dot_general(q_buf[pl.ds(b * half, half), cols], k_buf[...], (((1,), (1,)), ((), ())), preferred_element_type=F32)

    def attend(s_ref, n, b):
        mine, cols = pl.ds(b * half, half), pl.ds(pl.multiple_of(n * head, head), head)
        s = jnp.where(r["kpos"][...] <= r["q_col"][mine, :], s_ref[...], -1e30)
        e = jnp.exp2((s - jnp.max(s, axis=-1, keepdims=True)) * (head ** -0.5 * LOG2E))
        p = (e * (1.0 / jnp.sum(e, axis=-1, keepdims=True))).astype(BF16)
        o_buf[mine, cols] = jnp.dot(p, v_buf[...], preferred_element_type=F32).astype(BF16)

    def one_head(n, _):
        score(r["s_b"], n, 1)
        attend(r["s_a"], n, 0)
        score(r["s_a"], jnp.minimum(n + 1, heads - 1), 0)
        attend(r["s_b"], n, 1)
        return 0

    score(r["s_a"], 0, 0)
    lax.fori_loop(0, heads, one_head, 0)

    def o_step(i, _):
        slot, yslot = lax.rem(n_q + i, slots), lax.rem(i, 2)
        wo_copy(n_q + i, slot).wait()

        @pl.when(i >= 2)
        def _():
            for c in y_copies(i - 2, yslot):
                c.wait()

        y_buf[yslot] = jnp.dot(o_buf[...], ring[slot], preferred_element_type=F32).astype(BF16)
        for c in y_copies(i, yslot):
            c.start()
        fetch(n_q + i + slots, slot)
        return 0

    lax.fori_loop(0, n_o, o_step, 0)
    for i in (n_o - 2, n_o - 1):
        for c in y_copies(i, i % 2):
            c.wait()


def unit_call(lhs, wq, wo, keys, values, qpos, kpos, index, splits, slots=7, chunk=None):
    parts = ("q" if wq is not None else "") + ("o" if wo is not None else "")
    rows = sum(h.shape[0] for h in lhs)
    proj = wq.shape[1]
    width = wq.shape[0]
    chunk = chunk or proj
    any_ = pl.BlockSpec(memory_space=pl.ANY)
    ins = [(f"lhs{i}", h, any_) for i, h in enumerate(lhs)]
    scratch = [("ring", pltpu.VMEM((slots, chunk, proj), BF16)), ("ring_sem", pltpu.SemaphoreType.DMA((slots,))), ("q_buf", pltpu.VMEM((rows, proj), BF16))]
    flops, moved = 0, 0
    if wq is not None:
        ins.append(("wq", wq, any_))
        scratch += [("h_buf", pltpu.VMEM((slots, rows, chunk), BF16)), ("h_sem", pltpu.SemaphoreType.DMA((slots, len(lhs)))), ("acc", pltpu.VMEM((rows, proj), F32))]
        flops += 2 * rows * proj * width
        moved += 2 * (rows + proj) * width
    if wo is not None:
        n_keys, head = kpos.shape[1], keys[0].shape[1]
        ins.append(("wo", wo, any_))
        ins += [(f"k{m}", k, any_) for m, k in enumerate(keys)] + [(f"v{m}", v, any_) for m, v in enumerate(values)]
        ins += [("qpos", qpos, pl.BlockSpec(qpos.shape, lambda i: (0, 0))), ("kpos", kpos, pl.BlockSpec((1, n_keys), lambda i: (0, 0)))]
        scratch += [
            ("o_buf", pltpu.VMEM((rows, proj), BF16)), ("y_buf", pltpu.VMEM((2, rows, chunk), BF16)), ("y_sem", pltpu.SemaphoreType.DMA((2, len(splits)))),
            ("q_col", pltpu.VMEM((rows, 1), F32)), ("s_a", pltpu.VMEM((rows // 2, n_keys), F32)), ("s_b", pltpu.VMEM((rows // 2, n_keys), F32)),
            ("k_buf", pltpu.VMEM((n_keys, head), BF16)), ("v_buf", pltpu.VMEM((n_keys, head), BF16)), ("kv_sem", pltpu.SemaphoreType.DMA((2, len(keys)))),
        ]
        flops += 2 * rows * proj * (width + 2 * n_keys)
        moved += 2 * (rows + proj) * width
        outs = [((n, width), any_) for n in splits]
    else:
        outs = [((rows, n), pl.BlockSpec((rows, n), lambda i: (0, 0))) for n in splits]
    names = [i[0] for i in ins] + [f"out{i}" for i in range(len(outs))] + [s[0] for s in scratch]
    res = pl.pallas_call(
        functools.partial(_unit_kernel, names, parts, len(lhs), len(outs), index),
        grid=(1,),
        in_specs=[i[2] for i in ins],
        out_specs=[o[1] for o in outs],
        out_shape=[jax.ShapeDtypeStruct(o[0], BF16) for o in outs],
        scratch_shapes=[s[1] for s in scratch],
        compiler_params=pltpu.CompilerParams(dimension_semantics=("arbitrary",), vmem_limit_bytes=VMEM_BYTES if wo is not None else NORM_BYTES),
        cost_estimate=pl.CostEstimate(flops=flops, bytes_accessed=moved, transcendentals=0),
    )(*[i[1] for i in ins])
    return res


def _sums_kernel(jobs, n_in, *refs):
    ins, outs, bufs, in_sem, out_sem = refs[:n_in], refs[n_in:-3], refs[-3], refs[-2], refs[-1]
    halves = in_sem.shape[0]
    width = bufs.shape[1] // halves
    loads, stores, slots = {}, [], []
    at = 0
    for out, first, rows, terms in jobs:
        slots.append([])
        for _ in terms:
            slots[-1].append(at)
            at += rows
    n = 0
    for c in range(halves):
        cols = pl.ds(c * width, width)
        n = 0
        for j, (_, _, rows, terms) in enumerate(jobs):
            for i, (ref, first) in enumerate(terms):
                loads[c, j, i] = pltpu.make_async_copy(ins[ref].at[pl.ds(first, rows), cols], bufs.at[pl.ds(slots[j][i], rows), cols], in_sem.at[c, n])
                loads[c, j, i].start()
                n += 1
    for c in range(halves):
        for j, (out, first, rows, terms) in enumerate(jobs):
            for i in range(len(terms)):
                loads[c, j, i].wait()

            def some(k, _):
                cols = pl.ds(pl.multiple_of(c * width + k * 512, 512), 512)
                total = bufs[pl.ds(slots[j][0], rows), cols].astype(F32)
                for at in slots[j][1:]:
                    total = total + bufs[pl.ds(at, rows), cols].astype(F32)
                bufs[pl.ds(slots[j][0], rows), cols] = total.astype(BF16)
                return 0

            lax.fori_loop(0, width // 512, some, 0)
            cols = pl.ds(c * width, width)
            stores.append(pltpu.make_async_copy(bufs.at[pl.ds(slots[j][0], rows), cols], outs[out].at[pl.ds(first, rows), cols], out_sem.at[c, j]))
            stores[-1].start()
    for c in stores:
        c.wait()


def sums(jobs, out_rows, into=None):
    arrays = [] if into is None else [into]
    spec = []
    for out, first, rows, terms in jobs:
        at = []
        for a, f in terms:
            k = next((k for k, b in enumerate(arrays) if b is a), len(arrays))
            if k == len(arrays):
                arrays.append(a)
            at.append((k, f))
        spec.append((out, first, rows, tuple(at)))
    width = arrays[0].shape[1]
    n_terms = sum(len(j[3]) for j in jobs)
    rows_in = sum(j[2] * len(j[3]) for j in jobs)
    any_ = pl.BlockSpec(memory_space=pl.ANY)
    return pl.pallas_call(
        functools.partial(_sums_kernel, tuple(spec), len(arrays)),
        in_specs=[any_] * len(arrays),
        out_specs=[any_] * len(out_rows),
        out_shape=[jax.ShapeDtypeStruct((r, width), BF16) for r in out_rows],
        input_output_aliases={} if into is None else {0: 0},
        scratch_shapes=[pltpu.VMEM((rows_in, width), BF16), pltpu.SemaphoreType.DMA((2, n_terms)), pltpu.SemaphoreType.DMA((2, len(jobs)))],
        compiler_params=pltpu.CompilerParams(vmem_limit_bytes=VMEM_BYTES),
        cost_estimate=pl.CostEstimate(flops=rows_in * width, bytes_accessed=4 * rows_in * width, transcendentals=0),
        name="sums",
    )(*arrays)


def _where_kernel(q_ref, k_ref, q_out, k_out):
    q_out[...] = q_ref[...].astype(F32)
    k_out[...] = k_ref[...].astype(F32)


def as_float(q, k):
    return pl.pallas_call(
        _where_kernel,
        in_specs=[pl.BlockSpec(memory_space=pltpu.VMEM)] * 2,
        out_specs=[pl.BlockSpec(memory_space=pltpu.VMEM)] * 2,
        out_shape=[jax.ShapeDtypeStruct(q.shape, F32), jax.ShapeDtypeStruct(k.shape, F32)],
        cost_estimate=pl.CostEstimate(flops=q.size, bytes_accessed=16 * q.size, transcendentals=0),
        name="where",
    )(q, k)


CUTS = (16, 32, 16)
UNITS = U1A, U1B, U2A, U2B, U3A, U3B, U0A, U0B = ("u1a", "u1b", "u2a", "u2b", "u3a", "u3b", "u0a", "u0b")


def solution(mesh):
    n_dev = mesh.shape[AXIS]

    def send(value, mask):
        return lax.ppermute(value, AXIS, [(i, i ^ mask) for i in range(n_dev)])

    def by_mask(arr, me):
        cube = arr.reshape((2, 2, 2) + arr.shape[1:])
        for axis, bit in ((0, 4), (1, 2), (2, 1)):
            cube = jnp.where((me & bit) != 0, jnp.flip(cube, axis), cube)
        return cube.reshape(arr.shape)

    def local_step(x_loc, ln_gain, wq_loc, w_kv, wo_loc, positions):
        me = lax.axis_index(AXIS)
        rows, width = x_loc.shape
        seq, head = positions.shape[0], w_kv.shape[1] // 2
        piece = rows // 4
        gain = ln_gain.reshape(1, width)

        def send_all(values, mask):
            return [send(v, mask) for v in values]

        h, fx, fy, fd = [[] for _ in range(4)], [None] * 4, [None] * 4, [None] * 4
        a, b, _ = CUTS
        early = norm_first(x_loc, gain, a)
        middle, = norm_rows(x_loc, gain, a, b, 1, a)
        head_rows, tail_rows = norm_rows(x_loc, gain, 0, a, 2, a, (a + b) // a)
        h[0] = [head_rows, middle, tail_rows]
        for i, v in enumerate(norm_rows(x_loc, gain, piece, piece, 3, piece // 2)):
            h[i + 1].append(v)
        k_own, v_own = unit_call(sum(h, []), w_kv, None, None, None, None, None, 0, [head, head], slots=4, chunk=2048)
        sent = [[early] + h[0][1:]] + h[1:]
        for i in range(4):
            fx[i], fy[i] = send_all(sent[i], XN), send_all(sent[i], YN)
        for i in (0, 1):
            fd[i] = send_all(fx[i], YN)
        for i in (2, 3):
            fd[i] = send_all(fy[i], XN)
        k_m, v_m = {0: k_own}, {0: v_own}
        for m in (XN, YN):
            k_m[m], v_m[m] = send(k_own, m), send(v_own, m)
        k_m[DIAG], v_m[DIAG] = send(k_m[XN], YN), send(v_m[YN], XN)
        for m in (0, XN, YN, DIAG):
            k_m[m | CORE], v_m[m | CORE] = send(k_m[m], CORE), send(v_m[m], CORE)
        keys, values = [k_m[m] for m in range(n_dev)], [v_m[m] for m in range(n_dev)]
        k_cache, v_cache = order_blocks(keys, values)

        pos_m = by_mask(positions.reshape(n_dev, 4, piece), me)
        kpos = pos_m.reshape(1, seq)
        plan = {
            U0A: [(0, 0, h[0]), (0, 1, h[1])], U0B: [(0, 2, h[2]), (0, 3, h[3])],
            U1A: [(XN, 0, fx[0]), (YN, 0, fy[0])], U1B: [(XN, 1, fx[1]), (YN, 2, fy[2])],
            U2A: [(XN, 2, fx[2]), (YN, 3, fy[3])], U2B: [(XN, 3, fx[3]), (YN, 1, fy[1])],
            U3A: [(DIAG, 0, fd[0]), (DIAG, 2, fd[2])], U3B: [(DIAG, 1, fd[1]), (DIAG, 3, fd[3])],
        }
        qpos = jnp.concatenate([pos_m[m | c, i] for u in UNITS for c in (0, CORE) for m, i, _ in plan[u]]).reshape(len(UNITS), -1)
        qpos, kpos = as_float(qpos, kpos)

        parts = {}
        for index, name in enumerate(UNITS):
            blocks = plan[name]
            mine = sum((b for _, _, b in blocks), [])
            lhs = mine + send_all(mine, CORE)
            splits = [piece] * len(blocks) + [piece * len(blocks)]
            *own, other = unit_call(lhs, wq_loc, wo_loc, keys, values, qpos, kpos, index, splits)
            back = send(other, CORE)
            for j, (m, i, _) in enumerate(blocks):
                parts[m, i] = [(own[j], 0), (back, j * piece)]

        def total(*jobs):
            return sums([(k, 0, piece, t) for k, t in enumerate(jobs)], [piece] * len(jobs))

        def both(i, j):
            px, py = total(parts[DIAG, i], parts[DIAG, j])
            return send(px, XN), send(py, YN)

        got = {}
        px, = total(parts[XN, 0])
        got[0] = send(px, XN)
        px, py = total(parts[XN, 1], parts[YN, 2])
        got[1], got[2] = send(px, XN), send(py, YN)
        py, = total(parts[YN, 3])
        got[3] = send(py, YN)
        last = []
        for i, j, cuts in ((0, 2, (piece,)), (1, 3, (piece // 2, piece // 4, piece // 4))):
            hx, hy = both(i, j)
            first = 0
            for n in cuts:
                jobs = []
                for k, (p, owner, far) in enumerate(((i, YN, hx), (j, XN, hy))):
                    jobs.append((k, 0, n, [(a, f + first) for a, f in parts[owner, p] + [(far, 0)]]))
                py, px = sums(jobs, [n, n])
                last.append((n, (i * piece + first, send(py, YN)), (j * piece + first, send(px, XN))))
                first += n
        y, = sums([(0, i * piece, piece, parts[0, i] + [(got[i], 0)]) for i in range(4)], [rows])
        for n, *arrived in last:
            y, = sums([(0, f, n, [(y, f), (a, 0)]) for f, a in arrived], [rows], into=y)
        return y, k_cache, v_cache

    return jax.shard_map(
        local_step,
        mesh=mesh,
        in_specs=(P(AXIS, None), P(None), P(None, AXIS), P(None, None), P(AXIS, None), P(None)),
        out_specs=(P(AXIS, None), P(None, None), P(None, None)),
        check_vma=False,
    )
```

profile of v0, /device:TPU:0, one launch (start us, length us, event | category | flops | bytes accessed | tf_op | source)
XLA Modules:
  0.0 914.4 jit_solution(2117865734906418431)
XLA Ops:
  0.6 11.6 %norm.6 = (bf16[64,18432]{1,0:T(8,128)(2,1)}, bf16[64,18432]{1,0:T(8,128)(2,1)}, bf16[64,18432]{1,0:T(8,128)(2,1)}) custom-call(bf16[256,18432]{1,0:T(8,128)(2,1)} %x_hbm.1, f32[1,18432]{1,0:T(1,128)} %bitcast.66), custom_call_target="tpu_custom_call" | custom-call | flops 28311552 | bytes 14155776 | tf_op jit(solution)/shard_map/norm/pallas_call | solution.py:86
  12.2 3.7 norm.4
  15.9 3.5 norm.5.flat_1_
  19.3 12.0 %shard_map.85 = (bf16[256,256]{1,0:T(8,128)(2,1)}, bf16[256,256]{1,0:T(8,128)(2,1)}) custom-call(bf16[16,18432]{1,0:T(8,128)(2,1)} %get-tuple-element.52.flat_0_, bf16[32,18432]{1,0:T(8,128)(2,1)} %norm.5.flat_1_, bf16[16,18432]{1,0:T(8,128)(2,1)} %get-tuple-element.53.flat_2_, bf16[64,18432]{1,0:T(8,128)(2,1)} %get-tuple-element.54.flat_3_, ...), custom_call_target="tpu_custom_call" | custom-call | flops 4831838208 | bytes 28311552 | tf_op jit(solution)/shard_map/pallas_call | solution.py:292
  31.3 3.3 collective-permute-start.5
  36.7 2.1 collective-permute-done.5.flat_12_.flat_16_.flat_8_.refs_2_
  38.9 2.3 collective-permute-done.14.flat_22_.flat_26_.flat_18_.refs_12_
  41.1 1.6 collective-permute-start.9
  46.1 3.0 collective-permute-done.16.flat_24_.flat_28_.flat_20_.refs_14_
  49.1 3.8 collective-permute-done.15.flat_23_.flat_27_.flat_19_.refs_13_
  55.7 1.9 norm.7
  60.2 13.0 %collective-permute-done.19.flat_0_ = bf16[16,18432]{1,0:T(8,128)(2,1)S(1)} collective-permute-done((bf16[16,18432]{1,0:T(8,128)(2,1)S(1)}, bf16[16,18432]{1,0:T(8,128)(2,1)S(1)}, u32[]{:S(2)}, u32[]{:S(2)}) %collective-permute-start.19) | collective-permute-done | bytes 589856 | tf_op jit(solution)/shard_map/ppermute | solution.py:398
  74.4 11.7 %collective-permute-done.22.flat_3_ = bf16[16,18432]{1,0:T(8,128)(2,1)S(1)} collective-permute-done((bf16[16,18432]{1,0:T(8,128)(2,1)S(1)}, bf16[16,18432]{1,0:T(8,128)(2,1)S(1)}, u32[]{:S(2)}, u32[]{:S(2)}) %collective-permute-start.22) | collective-permute-done | bytes 589856 | tf_op jit(solution)/shard_map/ppermute | solution.py:398
  93.8 9.1 collective-permute-done.51.flat_2_
  103.6 9.9 %collective-permute-done.20.flat_1_ = bf16[32,18432]{1,0:T(8,128)(2,1)} collective-permute-done((bf16[32,18432]{1,0:T(8,128)(2,1)}, bf16[32,18432]{1,0:T(8,128)(2,1)}, u32[]{:S(2)}, u32[]{:S(2)}) %collective-permute-start.20) | collective-permute-done | bytes 1179680 | tf_op jit(solution)/shard_map/ppermute | solution.py:398
  114.9 50.3 %shard_map.89 = (bf16[64,18432]{1,0:T(8,128)(2,1)}, bf16[64,18432]{1,0:T(8,128)(2,1)}, bf16[128,18432]{1,0:T(8,128)(2,1)}) custom-call(bf16[64,18432]{1,0:T(8,128)(2,1)} %get-tuple-element.55.flat_4_.flat_0_, bf16[64,18432]{1,0:T(8,128)(2,1)} %get-tuple-element.56.flat_5_.flat_1_, bf16[64,18432]{1,0:T(8,128)(2,1)} %collective-permute-done.39.flat_2_, ...), custom_call_target="tpu_custom_call" | custom-call | flops 32212254720 | bytes 132120576 | tf_op jit(solution)/shard_map/pallas_call | solution.py:292
  167.7 50.5 %shard_map.86 = (bf16[64,18432]{1,0:T(8,128)(2,1)}, bf16[64,18432]{1,0:T(8,128)(2,1)}, bf16[128,18432]{1,0:T(8,128)(2,1)}) custom-call(bf16[16,18432]{1,0:T(8,128)(2,1)} %get-tuple-element.52.flat_0_, bf16[32,18432]{1,0:T(8,128)(2,1)} %norm.5.flat_1_, bf16[16,18432]{1,0:T(8,128)(2,1)} %get-tuple-element.53.flat_2_, ...), custom_call_target="tpu_custom_call" | custom-call | flops 32212254720 | bytes 132120576 | tf_op jit(solution)/shard_map/pallas_call | solution.py:292
  222.4 51.1 %shard_map.87 = (bf16[64,18432]{1,0:T(8,128)(2,1)}, bf16[64,18432]{1,0:T(8,128)(2,1)}, bf16[128,18432]{1,0:T(8,128)(2,1)}) custom-call(bf16[16,18432]{1,0:T(8,128)(2,1)} %copy-done.18, bf16[32,18432]{1,0:T(8,128)(2,1)} %collective-permute-done.20.flat_1_, bf16[16,18432]{1,0:T(8,128)(2,1)} %copy-done.19, bf16[16,18432]{1,0:T(8,128)(2,1)} %copy-done.21, ...), custom_call_target="tpu_custom_call" | custom-call | flops 32212254720 | bytes 132120576 | tf_op jit(solution)/shard_map/pallas_call | solution.py:292
  275.2 48.0 %collective-permute-done.43.flat_0_ = bf16[64,18432]{1,0:T(8,128)(2,1)} collective-permute-done((bf16[64,18432]{1,0:T(8,128)(2,1)}, bf16[64,18432]{1,0:T(8,128)(2,1)}, u32[]{:S(2)}, u32[]{:S(2)}) %collective-permute-start.43) | collective-permute-done | bytes 2359328 | tf_op jit(solution)/shard_map/ppermute | solution.py:398
  323.3 1.6 collective-permute-start.67
  325.1 50.3 %shard_map.92 = (bf16[64,18432]{1,0:T(8,128)(2,1)}, bf16[64,18432]{1,0:T(8,128)(2,1)}, bf16[128,18432]{1,0:T(8,128)(2,1)}) custom-call(bf16[64,18432]{1,0:T(8,128)(2,1)} %collective-permute-done.62.flat_0_, bf16[64,18432]{1,0:T(8,128)(2,1)} %collective-permute-done.63.flat_1_, bf16[64,18432]{1,0:T(8,128)(2,1)} %collective-permute-done.64.flat_2_, ...), custom_call_target="tpu_custom_call" | custom-call | flops 32212254720 | bytes 132120576 | tf_op jit(solution)/shard_map/pallas_call | solution.py:292
  375.8 1.8 collective-permute-done.67.flat_0_
  379.9 50.2 %shard_map.90 = (bf16[64,18432]{1,0:T(8,128)(2,1)}, bf16[64,18432]{1,0:T(8,128)(2,1)}, bf16[128,18432]{1,0:T(8,128)(2,1)}) custom-call(bf16[64,18432]{1,0:T(8,128)(2,1)} %collective-permute-done.43.flat_0_, bf16[64,18432]{1,0:T(8,128)(2,1)} %collective-permute-done.44.flat_1_, bf16[64,18432]{1,0:T(8,128)(2,1)} %collective-permute-done.45.flat_2_, ...), custom_call_target="tpu_custom_call" | custom-call | flops 32212254720 | bytes 132120576 | tf_op jit(solution)/shard_map/pallas_call | solution.py:292
  432.2 50.5 %shard_map.93 = (bf16[64,18432]{1,0:T(8,128)(2,1)}, bf16[64,18432]{1,0:T(8,128)(2,1)}, bf16[128,18432]{1,0:T(8,128)(2,1)}) custom-call(bf16[64,18432]{1,0:T(8,128)(2,1)} %collective-permute-done.67.flat_0_, bf16[64,18432]{1,0:T(8,128)(2,1)} %collective-permute-done.68.flat_1_, bf16[64,18432]{1,0:T(8,128)(2,1)} %collective-permute-done.69.flat_2_, ...), custom_call_target="tpu_custom_call" | custom-call | flops 32212254720 | bytes 132120576 | tf_op jit(solution)/shard_map/pallas_call | solution.py:292
  483.8 50.5 %shard_map.91 = (bf16[64,18432]{1,0:T(8,128)(2,1)}, bf16[64,18432]{1,0:T(8,128)(2,1)}, bf16[128,18432]{1,0:T(8,128)(2,1)}) custom-call(bf16[16,18432]{1,0:T(8,128)(2,1)} %collective-permute-done.49.flat_0_, bf16[32,18432]{1,0:T(8,128)(2,1)} %collective-permute-done.50.flat_1_, bf16[16,18432]{1,0:T(8,128)(2,1)} %copy-done.17, ...), custom_call_target="tpu_custom_call" | custom-call | flops 32212254720 | bytes 132120576 | tf_op jit(solution)/shard_map/pallas_call | solution.py:292
  535.3 50.3 %shard_map.88 = (bf16[64,18432]{1,0:T(8,128)(2,1)}, bf16[64,18432]{1,0:T(8,128)(2,1)}, bf16[128,18432]{1,0:T(8,128)(2,1)}) custom-call(bf16[64,18432]{1,0:T(8,128)(2,1)} %collective-permute-done.33.flat_0_, bf16[64,18432]{1,0:T(8,128)(2,1)} %collective-permute-done.34.flat_1_, bf16[64,18432]{1,0:T(8,128)(2,1)} %collective-permute-done.35.flat_2_, ...), custom_call_target="tpu_custom_call" | custom-call | flops 32212254720 | bytes 132120576 | tf_op jit(solution)/shard_map/pallas_call | solution.py:292
  586.1 3.8 sums.14
  590.5 6.1 sums.18
  599.0 6.1 sums.21
  606.7 3.8 sums.16
  610.5 33.8 %collective-permute-done.32.refs_2_ = bf16[64,18432]{1,0:T(8,128)(2,1)} collective-permute-done((bf16[64,18432]{1,0:T(8,128)(2,1)}, bf16[64,18432]{1,0:T(8,128)(2,1)}, u32[]{:S(2)}, u32[]{:S(2)}) %collective-permute-start.32) | collective-permute-done | bytes 2359328 | tf_op jit(solution)/shard_map/ppermute | solution.py:398
  645.3 6.1 sums.15
  651.4 43.6 %collective-permute-done.58.refs_2_ = bf16[64,18432]{1,0:T(8,128)(2,1)} collective-permute-done((bf16[64,18432]{1,0:T(8,128)(2,1)}, bf16[64,18432]{1,0:T(8,128)(2,1)}, u32[]{:S(2)}, u32[]{:S(2)}) %collective-permute-start.58) | collective-permute-done | bytes 2359328 | tf_op jit(solution)/shard_map/ppermute | solution.py:398
  696.6 7.6 sums.19
  704.3 41.3 %collective-permute-done.72.refs_2_ = bf16[64,18432]{1,0:T(8,128)(2,1)} collective-permute-done((bf16[64,18432]{1,0:T(8,128)(2,1)}, bf16[64,18432]{1,0:T(8,128)(2,1)}, u32[]{:S(2)}, u32[]{:S(2)}) %collective-permute-start.72) | collective-permute-done | bytes 2359328 | tf_op jit(solution)/shard_map/ppermute | solution.py:398
  747.2 4.6 sums.22
  751.8 1.8 collective-permute-done.48.refs_9_
  754.5 41.5 %collective-permute-done.38.refs_4_ = bf16[64,18432]{1,0:T(8,128)(2,1)} collective-permute-done((bf16[64,18432]{1,0:T(8,128)(2,1)}, bf16[64,18432]{1,0:T(8,128)(2,1)}, u32[]{:S(2)}, u32[]{:S(2)}) %collective-permute-start.38) | collective-permute-done | bytes 2359328 | tf_op jit(solution)/shard_map/ppermute | solution.py:398
  796.6 3.0 sums.26
  799.6 3.0 sums.24
  802.6 1.6 collective-permute-done.42.refs_7_
  805.1 74.9 %collective-permute-done.74.refs_1_ = bf16[32,18432]{1,0:T(8,128)(2,1)} collective-permute-done((bf16[32,18432]{1,0:T(8,128)(2,1)}, bf16[32,18432]{1,0:T(8,128)(2,1)}, u32[]{:S(2)}, u32[]{:S(2)}) %collective-permute-start.74) | collective-permute-done | bytes 1179680 | tf_op jit(solution)/shard_map/ppermute | solution.py:398
  883.0 3.0 order.1
  886.0 13.5 %sums.17.refs_0_ = bf16[256,18432]{1,0:T(8,128)(2,1)} custom-call(bf16[64,18432]{1,0:T(8,128)(2,1)} %get-tuple-element.61.refs_0_, bf16[128,18432]{1,0:T(8,128)(2,1)} %collective-permute-done.18.refs_1_, bf16[64,18432]{1,0:T(8,128)(2,1)} %collective-permute-done.32.refs_2_, bf16[64,18432]{1,0:T(8,128)(2,1)} %get-tuple-element.65.refs_3_, ...), custom_call_target="tpu_custom_call" | custom-call | flops 14155776 | bytes 56623104 | tf_op jit(solution)/shard_map/sums/pallas_call | solution.py:361
  899.5 6.1 sums.20.refs_0_
  905.6 3.5 sums.23.refs_0_
  909.1 2.6 sums.25.refs_0_
  911.7 2.6 sums.27
  (196 shorter events, 51.8 us)
Async XLA Ops:
  44.8 69.3 %collective-permute-start.39 = (bf16[64,18432]{1,0:T(8,128)(2,1)S(1)}, bf16[64,18432]{1,0:T(8,128)(2,1)}, u32[]{:S(2)}, u32[]{:S(2)}) collective-permute-start(bf16[64,18432]{1,0:T(8,128)(2,1)S(1)} %copy-done.14), channel_id=1, source_target_pairs={{0,1},{1,0},{2,3},{3,2},{4,5},{5,4},{6,7},{7,6}} | collective-permute-start | bytes 7077896 | tf_op jit(solution)/shard_map/ppermute | solution.py:398
  44.9 69.6 %collective-permute-start.40 = (bf16[64,18432]{1,0:T(8,128)(2,1)}, bf16[64,18432]{1,0:T(8,128)(2,1)}, u32[]{:S(2)}, u32[]{:S(2)}) collective-permute-start(bf16[64,18432]{1,0:T(8,128)(2,1)} %get-tuple-element.56.flat_5_.flat_1_), channel_id=1, source_target_pairs={{0,1},{1,0},{2,3},{3,2},{4,5},{5,4},{6,7},{7,6}} | collective-permute-start | bytes 7077896 | tf_op jit(solution)/shard_map/ppermute | solution.py:398
  102.9 63.8 %collective-permute-start.23 = (bf16[32,18432]{1,0:T(8,128)(2,1)}, bf16[32,18432]{1,0:T(8,128)(2,1)}, u32[]{:S(2)}, u32[]{:S(2)}) collective-permute-start(bf16[32,18432]{1,0:T(8,128)(2,1)} %norm.5.flat_1_), channel_id=1, source_target_pairs={{0,4},{1,5},{2,6},{3,7},{4,0},{5,1},{6,2},{7,3}} | collective-permute-start | bytes 3538952 | tf_op jit(solution)/shard_map/ppermute | solution.py:398
  113.6 54.1 %collective-permute-start.3 = (bf16[64,18432]{1,0:T(8,128)(2,1)}, bf16[64,18432]{1,0:T(8,128)(2,1)}, u32[]{:S(2)}, u32[]{:S(2)}) collective-permute-start(bf16[64,18432]{1,0:T(8,128)(2,1)} %get-tuple-element.54.flat_3_), channel_id=1, source_target_pairs={{0,1},{1,0},{2,3},{3,2},{4,5},{5,4},{6,7},{7,6}} | collective-permute-start | bytes 7077896 | tf_op jit(solution)/shard_map/ppermute | solution.py:398
  113.6 53.6 %collective-permute-start.1 = (bf16[32,18432]{1,0:T(8,128)(2,1)}, bf16[32,18432]{1,0:T(8,128)(2,1)}, u32[]{:S(2)}, u32[]{:S(2)}) collective-permute-start(bf16[32,18432]{1,0:T(8,128)(2,1)} %norm.5.flat_1_), channel_id=1, source_target_pairs={{0,1},{1,0},{2,3},{3,2},{4,5},{5,4},{6,7},{7,6}} | collective-permute-start | bytes 3538952 | tf_op jit(solution)/shard_map/ppermute | solution.py:398
  114.4 52.8 %collective-permute-start.25 = (bf16[16,18432]{1,0:T(8,128)(2,1)}, bf16[16,18432]{1,0:T(8,128)(2,1)}, u32[]{:S(2)}, u32[]{:S(2)}) collective-permute-start(bf16[16,18432]{1,0:T(8,128)(2,1)} %copy-done.18), channel_id=1, source_target_pairs={{0,1},{1,0},{2,3},{3,2},{4,5},{5,4},{6,7},{7,6}} | collective-permute-start | bytes 1769480 | tf_op jit(solution)/shard_map/ppermute | solution.py:398
  165.2 54.3 %collective-permute-start.62 = (bf16[64,18432]{1,0:T(8,128)(2,1)}, bf16[64,18432]{1,0:T(8,128)(2,1)}, u32[]{:S(2)}, u32[]{:S(2)}) collective-permute-start(bf16[64,18432]{1,0:T(8,128)(2,1)} %get-tuple-element.56.flat_5_.flat_1_), channel_id=1, source_target_pairs={{0,2},{1,3},{2,0},{3,1},{4,6},{5,7},{6,4},{7,5}} | collective-permute-start | bytes 7077896 | tf_op jit(solution)/shard_map/ppermute | solution.py:398
  166.8 53.6 %collective-permute-start.63 = (bf16[64,18432]{1,0:T(8,128)(2,1)}, bf16[64,18432]{1,0:T(8,128)(2,1)}, u32[]{:S(2)}, u32[]{:S(2)}) collective-permute-start(bf16[64,18432]{1,0:T(8,128)(2,1)} %get-tuple-element.54.flat_3_), channel_id=1, source_target_pairs={{0,4},{1,5},{2,6},{3,7},{4,0},{5,1},{6,2},{7,3}} | collective-permute-start | bytes 7077896 | tf_op jit(solution)/shard_map/ppermute | solution.py:398
  167.2 54.7 %collective-permute-start.26 = (bf16[32,18432]{1,0:T(8,128)(2,1)}, bf16[32,18432]{1,0:T(8,128)(2,1)}, u32[]{:S(2)}, u32[]{:S(2)}) collective-permute-start(bf16[32,18432]{1,0:T(8,128)(2,1)} %collective-permute-done.20.flat_1_), channel_id=1, source_target_pairs={{0,1},{1,0},{2,3},{3,2},{4,5},{5,4},{6,7},{7,6}} | collective-permute-start | bytes 3538952 | tf_op jit(solution)/shard_map/ppermute | solution.py:398
  167.7 54.2 %collective-permute-start.29 = (bf16[32,18432]{1,0:T(8,128)(2,1)}, bf16[32,18432]{1,0:T(8,128)(2,1)}, u32[]{:S(2)}, u32[]{:S(2)}) collective-permute-start(bf16[32,18432]{1,0:T(8,128)(2,1)} %collective-permute-done.23.flat_4_), channel_id=1, source_target_pairs={{0,1},{1,0},{2,3},{3,2},{4,5},{5,4},{6,7},{7,6}} | collective-permute-start | bytes 3538952 | tf_op jit(solution)/shard_map/ppermute | solution.py:398
  218.2 55.3 %collective-permute-start.33 = (bf16[64,18432]{1,0:T(8,128)(2,1)}, bf16[64,18432]{1,0:T(8,128)(2,1)}, u32[]{:S(2)}, u32[]{:S(2)}) collective-permute-start(bf16[64,18432]{1,0:T(8,128)(2,1)} %get-tuple-element.54.flat_3_), channel_id=1, source_target_pairs={{0,2},{1,3},{2,0},{3,1},{4,6},{5,7},{6,4},{7,5}} | collective-permute-start | bytes 7077896 | tf_op jit(solution)/shard_map/ppermute | solution.py:398
  219.5 54.8 %collective-permute-start.44 = (bf16[64,18432]{1,0:T(8,128)(2,1)}, bf16[64,18432]{1,0:T(8,128)(2,1)}, u32[]{:S(2)}, u32[]{:S(2)}) collective-permute-start(bf16[64,18432]{1,0:T(8,128)(2,1)} %get-tuple-element.56.flat_5_.flat_1_), channel_id=1, source_target_pairs={{0,4},{1,5},{2,6},{3,7},{4,0},{5,1},{6,2},{7,3}} | collective-permute-start | bytes 7077896 | tf_op jit(solution)/shard_map/ppermute | solution.py:398
  220.4 102.9 %collective-permute-start.43 = (bf16[64,18432]{1,0:T(8,128)(2,1)}, bf16[64,18432]{1,0:T(8,128)(2,1)}, u32[]{:S(2)}, u32[]{:S(2)}) collective-permute-start(bf16[64,18432]{1,0:T(8,128)(2,1)} %get-tuple-element.55.flat_4_.flat_0_), channel_id=1, source_target_pairs={{0,2},{1,3},{2,0},{3,1},{4,6},{5,7},{6,4},{7,5}} | collective-permute-start | bytes 7077896 | tf_op jit(solution)/shard_map/ppermute | solution.py:398
  221.9 101.4 %collective-permute-start.64 = (bf16[64,18432]{1,0:T(8,128)(2,1)}, bf16[64,18432]{1,0:T(8,128)(2,1)}, u32[]{:S(2)}, u32[]{:S(2)}) collective-permute-start(bf16[64,18432]{1,0:T(8,128)(2,1)} %collective-permute-done.62.flat_0_), channel_id=1, source_target_pairs={{0,1},{1,0},{2,3},{3,2},{4,5},{5,4},{6,7},{7,6}} | collective-permute-start | bytes 7077896 | tf_op jit(solution)/shard_map/ppermute | solution.py:398
  221.9 103.0 %collective-permute-start.65 = (bf16[64,18432]{1,0:T(8,128)(2,1)}, bf16[64,18432]{1,0:T(8,128)(2,1)}, u32[]{:S(2)}, u32[]{:S(2)}) collective-permute-start(bf16[64,18432]{1,0:T(8,128)(2,1)} %collective-permute-done.63.flat_1_), channel_id=1, source_target_pairs={{0,1},{1,0},{2,3},{3,2},{4,5},{5,4},{6,7},{7,6}} | collective-permute-start | bytes 7077896 | tf_op jit(solution)/shard_map/ppermute | solution.py:398
  273.5 101.8 %collective-permute-start.34 = (bf16[64,18432]{1,0:T(8,128)(2,1)}, bf16[64,18432]{1,0:T(8,128)(2,1)}, u32[]{:S(2)}, u32[]{:S(2)}) collective-permute-start(bf16[64,18432]{1,0:T(8,128)(2,1)} %get-tuple-element.55.flat_4_.flat_0_), channel_id=1, source_target_pairs={{0,4},{1,5},{2,6},{3,7},{4,0},{5,1},{6,2},{7,3}} | collective-permute-start | bytes 7077896 | tf_op jit(solution)/shard_map/ppermute | solution.py:398
  274.3 104.5 %collective-permute-start.68 = (bf16[64,18432]{1,0:T(8,128)(2,1)}, bf16[64,18432]{1,0:T(8,128)(2,1)}, u32[]{:S(2)}, u32[]{:S(2)}) collective-permute-start(bf16[64,18432]{1,0:T(8,128)(2,1)} %collective-permute-done.44.flat_1_), channel_id=1, source_target_pairs={{0,2},{1,3},{2,0},{3,1},{4,6},{5,7},{6,4},{7,5}} | collective-permute-start | bytes 7077896 | tf_op jit(solution)/shard_map/ppermute | solution.py:398
  323.3 56.1 %collective-permute-start.46 = (bf16[64,18432]{1,0:T(8,128)(2,1)}, bf16[64,18432]{1,0:T(8,128)(2,1)}, u32[]{:S(2)}, u32[]{:S(2)}) collective-permute-start(bf16[64,18432]{1,0:T(8,128)(2,1)} %collective-permute-done.44.flat_1_), channel_id=1, source_target_pairs={{0,1},{1,0},{2,3},{3,2},{4,5},{5,4},{6,7},{7,6}} | collective-permute-start | bytes 7077896 | tf_op jit(solution)/shard_map/ppermute | solution.py:398
  323.3 54.3 %collective-permute-start.67 = (bf16[64,18432]{1,0:T(8,128)(2,1)}, bf16[64,18432]{1,0:T(8,128)(2,1)}, u32[]{:S(2)}, u32[]{:S(2)}) collective-permute-start(bf16[64,18432]{1,0:T(8,128)(2,1)} %collective-permute-done.33.flat_0_), channel_id=1, source_target_pairs={{0,4},{1,5},{2,6},{3,7},{4,0},{5,1},{6,2},{7,3}} | collective-permute-start | bytes 7077896 | tf_op jit(solution)/shard_map/ppermute | solution.py:398
  324.9 54.5 %collective-permute-start.45 = (bf16[64,18432]{1,0:T(8,128)(2,1)}, bf16[64,18432]{1,0:T(8,128)(2,1)}, u32[]{:S(2)}, u32[]{:S(2)}) collective-permute-start(bf16[64,18432]{1,0:T(8,128)(2,1)} %collective-permute-done.43.flat_0_), channel_id=1, source_target_pairs={{0,1},{1,0},{2,3},{3,2},{4,5},{5,4},{6,7},{7,6}} | collective-permute-start | bytes 7077896 | tf_op jit(solution)/shard_map/ppermute | solution.py:398
  375.4 54.8 %collective-permute-start.49 = (bf16[16,18432]{1,0:T(8,128)(2,1)}, bf16[16,18432]{1,0:T(8,128)(2,1)}, u32[]{:S(2)}, u32[]{:S(2)}) collective-permute-start(bf16[16,18432]{1,0:T(8,128)(2,1)} %copy-done.18), channel_id=1, source_target_pairs={{0,4},{1,5},{2,6},{3,7},{4,0},{5,1},{6,2},{7,3}} | collective-permute-start | bytes 1769480 | tf_op jit(solution)/shard_map/ppermute | solution.py:398
  377.6 52.6 %collective-permute-start.50 = (bf16[32,18432]{1,0:T(8,128)(2,1)}, bf16[32,18432]{1,0:T(8,128)(2,1)}, u32[]{:S(2)}, u32[]{:S(2)}) collective-permute-start(bf16[32,18432]{1,0:T(8,128)(2,1)} %collective-permute-done.20.flat_1_), channel_id=1, source_target_pairs={{0,4},{1,5},{2,6},{3,7},{4,0},{5,1},{6,2},{7,3}} | collective-permute-start | bytes 3538952 | tf_op jit(solution)/shard_map/ppermute | solution.py:398
  378.8 52.8 %collective-permute-start.52 = (bf16[64,18432]{1,0:T(8,128)(2,1)}, bf16[64,18432]{1,0:T(8,128)(2,1)}, u32[]{:S(2)}, u32[]{:S(2)}) collective-permute-start(bf16[64,18432]{1,0:T(8,128)(2,1)} %collective-permute-done.34.flat_1_), channel_id=1, source_target_pairs={{0,2},{1,3},{2,0},{3,1},{4,6},{5,7},{6,4},{7,5}} | collective-permute-start | bytes 7077896 | tf_op jit(solution)/shard_map/ppermute | solution.py:398
  379.3 52.3 %collective-permute-start.69 = (bf16[64,18432]{1,0:T(8,128)(2,1)}, bf16[64,18432]{1,0:T(8,128)(2,1)}, u32[]{:S(2)}, u32[]{:S(2)}) collective-permute-start(bf16[64,18432]{1,0:T(8,128)(2,1)} %collective-permute-done.67.flat_0_), channel_id=1, source_target_pairs={{0,1},{1,0},{2,3},{3,2},{4,5},{5,4},{6,7},{7,6}} | collective-permute-start | bytes 7077896 | tf_op jit(solution)/shard_map/ppermute | solution.py:398
  379.4 52.8 %collective-permute-start.70 = (bf16[64,18432]{1,0:T(8,128)(2,1)}, bf16[64,18432]{1,0:T(8,128)(2,1)}, u32[]{:S(2)}, u32[]{:S(2)}) collective-permute-start(bf16[64,18432]{1,0:T(8,128)(2,1)} %collective-permute-done.68.flat_1_), channel_id=1, source_target_pairs={{0,1},{1,0},{2,3},{3,2},{4,5},{5,4},{6,7},{7,6}} | collective-permute-start | bytes 7077896 | tf_op jit(solution)/shard_map/ppermute | solution.py:398
  430.1 52.6 %collective-permute-start.55 = (bf16[16,18432]{1,0:T(8,128)(2,1)}, bf16[16,18432]{1,0:T(8,128)(2,1)}, u32[]{:S(2)}, u32[]{:S(2)}) collective-permute-start(bf16[16,18432]{1,0:T(8,128)(2,1)} %copy-done.17), channel_id=1, source_target_pairs={{0,1},{1,0},{2,3},{3,2},{4,5},{5,4},{6,7},{7,6}} | collective-permute-start | bytes 1769480 | tf_op jit(solution)/shard_map/ppermute | solution.py:398
  430.2 53.0 %collective-permute-start.53 = (bf16[16,18432]{1,0:T(8,128)(2,1)}, bf16[16,18432]{1,0:T(8,128)(2,1)}, u32[]{:S(2)}, u32[]{:S(2)}) collective-permute-start(bf16[16,18432]{1,0:T(8,128)(2,1)} %collective-permute-done.49.flat_0_), channel_id=1, source_target_pairs={{0,1},{1,0},{2,3},{3,2},{4,5},{5,4},{6,7},{7,6}} | collective-permute-start | bytes 1769480 | tf_op jit(solution)/shard_map/ppermute | solution.py:398
  431.7 103.2 %collective-permute-start.31 = (bf16[128,18432]{1,0:T(8,128)(2,1)}, bf16[128,18432]{1,0:T(8,128)(2,1)}, u32[]{:S(2)}, u32[]{:S(2)}) collective-permute-start(bf16[128,18432]{1,0:T(8,128)(2,1)} %get-tuple-element.64), channel_id=1, source_target_pairs={{0,1},{1,0},{2,3},{3,2},{4,5},{5,4},{6,7},{7,6}} | collective-permute-start | bytes 14155784 | tf_op jit(solution)/shard_map/ppermute | solution.py:398
  431.7 51.6 %collective-permute-start.54 = (bf16[32,18432]{1,0:T(8,128)(2,1)}, bf16[32,18432]{1,0:T(8,128)(2,1)}, u32[]{:S(2)}, u32[]{:S(2)}) collective-permute-start(bf16[32,18432]{1,0:T(8,128)(2,1)} %collective-permute-done.50.flat_1_), channel_id=1, source_target_pairs={{0,1},{1,0},{2,3},{3,2},{4,5},{5,4},{6,7},{7,6}} | collective-permute-start | bytes 3538952 | tf_op jit(solution)/shard_map/ppermute | solution.py:398
  432.2 51.5 %collective-permute-start.56 = (bf16[64,18432]{1,0:T(8,128)(2,1)}, bf16[64,18432]{1,0:T(8,128)(2,1)}, u32[]{:S(2)}, u32[]{:S(2)}) collective-permute-start(bf16[64,18432]{1,0:T(8,128)(2,1)} %collective-permute-done.52.flat_3_), channel_id=1, source_target_pairs={{0,1},{1,0},{2,3},{3,2},{4,5},{5,4},{6,7},{7,6}} | collective-permute-start | bytes 7077896 | tf_op jit(solution)/shard_map/ppermute | solution.py:398
  482.7 102.9 %collective-permute-start.41 = (bf16[128,18432]{1,0:T(8,128)(2,1)}, bf16[128,18432]{1,0:T(8,128)(2,1)}, u32[]{:S(2)}, u32[]{:S(2)}) collective-permute-start(bf16[128,18432]{1,0:T(8,128)(2,1)} %get-tuple-element.71), channel_id=1, source_target_pairs={{0,1},{1,0},{2,3},{3,2},{4,5},{5,4},{6,7},{7,6}} | collective-permute-start | bytes 14155784 | tf_op jit(solution)/shard_map/ppermute | solution.py:398
  483.2 102.5 %collective-permute-start.18 = (bf16[128,18432]{1,0:T(8,128)(2,1)}, bf16[128,18432]{1,0:T(8,128)(2,1)}, u32[]{:S(2)}, u32[]{:S(2)}) collective-permute-start(bf16[128,18432]{1,0:T(8,128)(2,1)} %get-tuple-element.62), channel_id=1, source_target_pairs={{0,1},{1,0},{2,3},{3,2},{4,5},{5,4},{6,7},{7,6}} | collective-permute-start | bytes 14155784 | tf_op jit(solution)/shard_map/ppermute | solution.py:398
  534.3 62.2 %collective-permute-start.66 = (bf16[128,18432]{1,0:T(8,128)(2,1)}, bf16[128,18432]{1,0:T(8,128)(2,1)}, u32[]{:S(2)}, u32[]{:S(2)}) collective-permute-start(bf16[128,18432]{1,0:T(8,128)(2,1)} %get-tuple-element.86), channel_id=1, source_target_pairs={{0,1},{1,0},{2,3},{3,2},{4,5},{5,4},{6,7},{7,6}} | collective-permute-start | bytes 14155784 | tf_op jit(solution)/shard_map/ppermute | solution.py:398
  534.8 63.3 %collective-permute-start.71 = (bf16[128,18432]{1,0:T(8,128)(2,1)}, bf16[128,18432]{1,0:T(8,128)(2,1)}, u32[]{:S(2)}, u32[]{:S(2)}) collective-permute-start(bf16[128,18432]{1,0:T(8,128)(2,1)} %get-tuple-element.88), channel_id=1, source_target_pairs={{0,1},{1,0},{2,3},{3,2},{4,5},{5,4},{6,7},{7,6}} | collective-permute-start | bytes 14155784 | tf_op jit(solution)/shard_map/ppermute | solution.py:398
  534.8 55.1 %collective-permute-start.57 = (bf16[128,18432]{1,0:T(8,128)(2,1)}, bf16[128,18432]{1,0:T(8,128)(2,1)}, u32[]{:S(2)}, u32[]{:S(2)}) collective-permute-start(bf16[128,18432]{1,0:T(8,128)(2,1)} %get-tuple-element.78), channel_id=1, source_target_pairs={{0,1},{1,0},{2,3},{3,2},{4,5},{5,4},{6,7},{7,6}} | collective-permute-start | bytes 14155784 | tf_op jit(solution)/shard_map/ppermute | solution.py:398
  589.9 54.5 %collective-permute-start.32 = (bf16[64,18432]{1,0:T(8,128)(2,1)}, bf16[64,18432]{1,0:T(8,128)(2,1)}, u32[]{:S(2)}, u32[]{:S(2)}) collective-permute-start(bf16[64,18432]{1,0:T(8,128)(2,1)} %sums.14), channel_id=1, source_target_pairs={{0,2},{1,3},{2,0},{3,1},{4,6},{5,7},{6,4},{7,5}} | collective-permute-start | bytes 7077896 | tf_op jit(solution)/shard_map/ppermute | solution.py:398
  596.5 98.4 %collective-permute-start.58 = (bf16[64,18432]{1,0:T(8,128)(2,1)}, bf16[64,18432]{1,0:T(8,128)(2,1)}, u32[]{:S(2)}, u32[]{:S(2)}) collective-permute-start(bf16[64,18432]{1,0:T(8,128)(2,1)} %get-tuple-element.80), channel_id=1, source_target_pairs={{0,2},{1,3},{2,0},{3,1},{4,6},{5,7},{6,4},{7,5}} | collective-permute-start | bytes 7077896 | tf_op jit(solution)/shard_map/ppermute | solution.py:398
  598.1 97.4 %collective-permute-start.59 = (bf16[64,18432]{1,0:T(8,128)(2,1)}, bf16[64,18432]{1,0:T(8,128)(2,1)}, u32[]{:S(2)}, u32[]{:S(2)}) collective-permute-start(bf16[64,18432]{1,0:T(8,128)(2,1)} %get-tuple-element.82), channel_id=1, source_target_pairs={{0,4},{1,5},{2,6},{3,7},{4,0},{5,1},{6,2},{7,3}} | collective-permute-start | bytes 7077896 | tf_op jit(solution)/shard_map/ppermute | solution.py:398
  605.1 140.4 %collective-permute-start.72 = (bf16[64,18432]{1,0:T(8,128)(2,1)}, bf16[64,18432]{1,0:T(8,128)(2,1)}, u32[]{:S(2)}, u32[]{:S(2)}) collective-permute-start(bf16[64,18432]{1,0:T(8,128)(2,1)} %get-tuple-element.90), channel_id=1, source_target_pairs={{0,2},{1,3},{2,0},{3,1},{4,6},{5,7},{6,4},{7,5}} | collective-permute-start | bytes 7077896 | tf_op jit(solution)/shard_map/ppermute | solution.py:398
  605.9 140.6 %collective-permute-start.73 = (bf16[64,18432]{1,0:T(8,128)(2,1)}, bf16[64,18432]{1,0:T(8,128)(2,1)}, u32[]{:S(2)}, u32[]{:S(2)}) collective-permute-start(bf16[64,18432]{1,0:T(8,128)(2,1)} %get-tuple-element.92), channel_id=1, source_target_pairs={{0,4},{1,5},{2,6},{3,7},{4,0},{5,1},{6,2},{7,3}} | collective-permute-start | bytes 7077896 | tf_op jit(solution)/shard_map/ppermute | solution.py:398
  644.4 109.2 %collective-permute-start.48 = (bf16[64,18432]{1,0:T(8,128)(2,1)}, bf16[64,18432]{1,0:T(8,128)(2,1)}, u32[]{:S(2)}, u32[]{:S(2)}) collective-permute-start(bf16[64,18432]{1,0:T(8,128)(2,1)} %sums.16), channel_id=1, source_target_pairs={{0,4},{1,5},{2,6},{3,7},{4,0},{5,1},{6,2},{7,3}} | collective-permute-start | bytes 7077896 | tf_op jit(solution)/shard_map/ppermute | solution.py:398
  695.0 101.1 %collective-permute-start.38 = (bf16[64,18432]{1,0:T(8,128)(2,1)}, bf16[64,18432]{1,0:T(8,128)(2,1)}, u32[]{:S(2)}, u32[]{:S(2)}) collective-permute-start(bf16[64,18432]{1,0:T(8,128)(2,1)} %get-tuple-element.69), channel_id=1, source_target_pairs={{0,2},{1,3},{2,0},{3,1},{4,6},{5,7},{6,4},{7,5}} | collective-permute-start | bytes 7077896 | tf_op jit(solution)/shard_map/ppermute | solution.py:398
  695.5 108.7 %collective-permute-start.42 = (bf16[64,18432]{1,0:T(8,128)(2,1)}, bf16[64,18432]{1,0:T(8,128)(2,1)}, u32[]{:S(2)}, u32[]{:S(2)}) collective-permute-start(bf16[64,18432]{1,0:T(8,128)(2,1)} %get-tuple-element.72), channel_id=1, source_target_pairs={{0,4},{1,5},{2,6},{3,7},{4,0},{5,1},{6,2},{7,3}} | collective-permute-start | bytes 7077896 | tf_op jit(solution)/shard_map/ppermute | solution.py:398
  745.5 135.0 %collective-permute-start.60 = (bf16[64,18432]{1,0:T(8,128)(2,1)}, bf16[64,18432]{1,0:T(8,128)(2,1)}, u32[]{:S(2)}, u32[]{:S(2)}) collective-permute-start(bf16[64,18432]{1,0:T(8,128)(2,1)} %get-tuple-element.83), channel_id=1, source_target_pairs={{0,4},{1,5},{2,6},{3,7},{4,0},{5,1},{6,2},{7,3}} | collective-permute-start | bytes 7077896 | tf_op jit(solution)/shard_map/ppermute | solution.py:398
  746.4 135.3 %collective-permute-start.61 = (bf16[64,18432]{1,0:T(8,128)(2,1)}, bf16[64,18432]{1,0:T(8,128)(2,1)}, u32[]{:S(2)}, u32[]{:S(2)}) collective-permute-start(bf16[64,18432]{1,0:T(8,128)(2,1)} %get-tuple-element.84), channel_id=1, source_target_pairs={{0,2},{1,3},{2,0},{3,1},{4,6},{5,7},{6,4},{7,5}} | collective-permute-start | bytes 7077896 | tf_op jit(solution)/shard_map/ppermute | solution.py:398
  753.6 126.4 %collective-permute-start.74 = (bf16[32,18432]{1,0:T(8,128)(2,1)}, bf16[32,18432]{1,0:T(8,128)(2,1)}, u32[]{:S(2)}, u32[]{:S(2)}) collective-permute-start(bf16[32,18432]{1,0:T(8,128)(2,1)} %get-tuple-element.93), channel_id=1, source_target_pairs={{0,4},{1,5},{2,6},{3,7},{4,0},{5,1},{6,2},{7,3}} | collective-permute-start | bytes 3538952 | tf_op jit(solution)/shard_map/ppermute | solution.py:398
  796.1 109.5 %collective-permute-start.75 = (bf16[32,18432]{1,0:T(8,128)(2,1)}, bf16[32,18432]{1,0:T(8,128)(2,1)}, u32[]{:S(2)}, u32[]{:S(2)}) collective-permute-start(bf16[32,18432]{1,0:T(8,128)(2,1)} %get-tuple-element.94), channel_id=1, source_target_pairs={{0,2},{1,3},{2,0},{3,1},{4,6},{5,7},{6,4},{7,5}} | collective-permute-start | bytes 3538952 | tf_op jit(solution)/shard_map/ppermute | solution.py:398
  804.2 104.9 %collective-permute-start.76 = (bf16[16,18432]{1,0:T(8,128)(2,1)}, bf16[16,18432]{1,0:T(8,128)(2,1)}, u32[]{:S(2)}, u32[]{:S(2)}) collective-permute-start(bf16[16,18432]{1,0:T(8,128)(2,1)} %get-tuple-element.95), channel_id=1, source_target_pairs={{0,4},{1,5},{2,6},{3,7},{4,0},{5,1},{6,2},{7,3}} | collective-permute-start | bytes 1769480 | tf_op jit(solution)/shard_map/ppermute | solution.py:398
  (55 other events, 888.8 us)
where the time goes:
time: 916 us; the launch traced here: 914 us
  Pallas kernels  513 us (56%)
  waiting for transfers between devices  348 us (38%)
  starting transfers between devices  47.1 us (5%)
    pallas_call x9, Pallas kernels, unit_call(): pl.pallas_call(functools.partial(_unit_kernel, names, parts, len(lhs), le...  416 us
    ppermute x80, waiting for transfers between devices, send(): return lax.ppermute(value, AXIS, [(i, i ^ mask) for i in range(n_dev)])  348 us
    pallas_call x14, Pallas kernels, sums(): pl.pallas_call(functools.partial(_sums_kernel, tuple(spec), len(arrays)),...  72.1 us
    ppermute x80, starting transfers between devices, send(): return lax.ppermute(value, AXIS, [(i, i ^ mask) for i in range(n_dev)])  47.1 us
    pallas_call x3, Pallas kernels, norm_rows(): pl.pallas_call(functools.partial(_norm_kernel, 2048, steps), grid=(count...  18.7 us
  transfers between devices with their start and end apart: 80, of which 22 were waited for; matrix products, arithmetic and copies ran while one was open for 0% of the time, Pallas kernels for 52%

commit v1 on v0

--- a/solution.py
+++ b/solution.py
@@ -18,7 +18,7 @@
 BF16, F32 = jnp.bfloat16, jnp.float32
 
 
-def _norm_kernel(chunk, steps, x_ref, g_ref, *out_refs):
+def _norm_kernel(chunk, steps, x_ref, g_ref, *out_refs, landing=((),)):
     rows, width = x_ref.shape
     n_chunks = width // chunk
 
@@ -39,7 +39,12 @@
         return acc + fold(d * d)
 
     zero = jnp.zeros((rows, 128), F32)
-    mean = jnp.sum(lax.fori_loop(0, n_chunks, lambda c, acc: acc + fold(load(c)), zero), axis=1, keepdims=True) / width
+    total, part = zero, n_chunks // len(landing)
+    for i, copies in enumerate(landing):
+        for c in copies:
+            c.wait()
+        total = lax.fori_loop(i * part, (i + 1) * part, lambda c, acc: acc + fold(load(c)), total)
+    mean = jnp.sum(total, axis=1, keepdims=True) / width
     rstd = lax.rsqrt(jnp.sum(lax.fori_loop(0, n_chunks, square, zero), axis=1, keepdims=True) / width + NORM_EPS)
     for i, out_ref in enumerate(out_refs):
         @pl.when(pl.program_id(0) // steps == i)
@@ -52,24 +57,25 @@
 
 
 def _norm_first_kernel(chunk, x_hbm, g_hbm, out_ref, x_buf, g_buf, sem):
-    copies = [pltpu.make_async_copy(x_hbm.at[pl.ds(0, x_buf.shape[0]), :], x_buf, sem.at[0]), pltpu.make_async_copy(g_hbm, g_buf, sem.at[1])]
+    rows, width = x_buf.shape
+    halves = [pl.ds(i * width // 2, width // 2) for i in range(2)]
+    copies = [pltpu.make_async_copy(x_hbm.at[pl.ds(0, rows), c], x_buf.at[:, c], sem.at[i]) for i, c in enumerate(halves)]
+    copies.append(pltpu.make_async_copy(g_hbm, g_buf, sem.at[2]))
     for c in copies:
         c.start()
-    for c in copies:
-        c.wait()
-    _norm_kernel(chunk, 1, x_buf, g_buf, out_ref)
+    _norm_kernel(chunk, 1, x_buf, g_buf, out_ref, landing=(copies[:1], copies[1:]))
 
 
 def norm_first(x, gain, rows):
     width = x.shape[1]
     hbm = pl.BlockSpec(memory_space=pltpu.HBM)
     return pl.pallas_call(
-        functools.partial(_norm_first_kernel, 2048),
+        functools.partial(_norm_first_kernel, 4608),
         grid=(1,),
         in_specs=[hbm, hbm],
         out_specs=pl.BlockSpec(memory_space=pltpu.VMEM),
         out_shape=pltpu.VMEM((rows, width), BF16),
-        scratch_shapes=[pltpu.VMEM((rows, width), BF16), pltpu.VMEM(gain.shape, F32), pltpu.SemaphoreType.DMA((2,))],
+        scratch_shapes=[pltpu.VMEM((rows, width), BF16), pltpu.VMEM(gain.shape, F32), pltpu.SemaphoreType.DMA((3,))],
         compiler_params=pltpu.CompilerParams(dimension_semantics=("arbitrary",), vmem_limit_bytes=NORM_BYTES),
         cost_estimate=pl.CostEstimate(flops=8 * rows * width, bytes_accessed=4 * rows * width, transcendentals=0),
         name="norm",
@@ -97,16 +103,18 @@
 
 def _order_kernel(n, *refs):
     me = lax.axis_index(AXIS)
-    for i in range(2):
-        blocks, out = refs[i * n:(i + 1) * n], refs[2 * n + i]
-        rows = blocks[0].shape[0]
-        for m, block in enumerate(blocks):
-            out[pl.ds(pl.multiple_of((me ^ m) * rows, rows), rows), :] = block[...]
-
-
-def order_blocks(k_blocks, v_blocks):
-    n = len(k_blocks)
-    rows, cols = k_blocks[0].shape
+    k_out, v_out = refs[2 * n:]
+    for m, (top, rest) in enumerate(zip(refs[:n], refs[n:2 * n])):
+        high, rows = top.shape[0], (top.shape[0] + rest.shape[0]) // 2
+        first = pl.multiple_of((me ^ m) * rows, rows)
+        k_out[pl.ds(first, high), :] = top[...]
+        k_out[pl.ds(pl.multiple_of(first + high, 16), rows - high), :] = rest[rows:, :]
+        v_out[pl.ds(first, rows), :] = rest[:rows, :]
+
+
+def order_blocks(tops, rests):
+    n, cols = len(tops), tops[0].shape[1]
+    rows = (tops[0].shape[0] + rests[0].shape[0]) // 2
     return pl.pallas_call(
         functools.partial(_order_kernel, n),
         in_specs=[pl.BlockSpec(memory_space=pltpu.VMEM)] * (2 * n),
@@ -114,7 +122,7 @@
         out_shape=[jax.ShapeDtypeStruct((rows * n, cols), BF16)] * 2,
         cost_estimate=pl.CostEstimate(flops=2 * rows * n * cols, bytes_accessed=8 * rows * n * cols, transcendentals=0),
         name="order",
-    )(*k_blocks, *v_blocks)
+    )(*tops, *rests)
 
 
 def _unit_kernel(names, parts, n_lhs, n_out, index, *flat):
@@ -178,12 +186,12 @@
         row, col = (lax.broadcasted_iota(jnp.int32, (rows, rows), d) for d in (0, 1))
         mine = jnp.where(row == col, r["qpos"][index:index + 1, :], 0.0)
         r["q_col"][...] = jnp.sum(mine, axis=1, keepdims=True)
-        for i, (name, buf) in enumerate((("k", r["k_buf"]), ("v", r["v_buf"]))):
-            n = r["kv_sem"].shape[1]
-            for m in range(n):
-                block = r[f"{name}{m}"]
-                rows_m = block.shape[0]
-                extra.append(pltpu.make_async_copy(block, buf.at[pl.ds(m * rows_m, rows_m), :], r["kv_sem"].at[i, m]))
+        for m in range(r["kv_sem"].shape[0]):
+            top, rest = r[f"k{m}"], r[f"v{m}"]
+            high, n = top.shape[0], (top.shape[0] + rest.shape[0]) // 2
+            moves = ((top, 0, high, "k_buf", 0), (rest, n, n - high, "k_buf", high), (rest, 0, n, "v_buf", 0))
+            for j, (src, first, count, buf, to) in enumerate(moves):
+                extra.append(pltpu.make_async_copy(src.at[pl.ds(first, count), :], r[buf].at[pl.ds(m * n + to, count), :], r["kv_sem"].at[m, j]))
     for c in extra:
         c.start()
 
@@ -202,9 +210,10 @@
 
         lax.fori_loop(0, n_q, q_step, 0)
         if not do_o:
-            cols = proj // n_out
-            for i, out in enumerate(outs):
-                out[...] = acc[:, i * cols:(i + 1) * cols].astype(BF16)
+            high, cols = outs[0].shape
+            outs[0][...] = acc[:high, :cols].astype(BF16)
+            outs[1][:rows, :] = acc[:, cols:].astype(BF16)
+            outs[1][rows:, :] = acc[high:, :cols].astype(BF16)
             return
         q_buf[...] = acc[...].astype(BF16)
 
@@ -281,13 +290,13 @@
         scratch += [
             ("o_buf", pltpu.VMEM((rows, proj), BF16)), ("y_buf", pltpu.VMEM((2, rows, chunk), BF16)), ("y_sem", pltpu.SemaphoreType.DMA((2, len(splits)))),
             ("q_col", pltpu.VMEM((rows, 1), F32)), ("s_a", pltpu.VMEM((rows // 2, n_keys), F32)), ("s_b", pltpu.VMEM((rows // 2, n_keys), F32)),
-            ("k_buf", pltpu.VMEM((n_keys, head), BF16)), ("v_buf", pltpu.VMEM((n_keys, head), BF16)), ("kv_sem", pltpu.SemaphoreType.DMA((2, len(keys)))),
+            ("k_buf", pltpu.VMEM((n_keys, head), BF16)), ("v_buf", pltpu.VMEM((n_keys, head), BF16)), ("kv_sem", pltpu.SemaphoreType.DMA((len(keys), 3))),
         ]
         flops += 2 * rows * proj * (width + 2 * n_keys)
         moved += 2 * (rows + proj) * width
         outs = [((n, width), any_) for n in splits]
     else:
-        outs = [((rows, n), pl.BlockSpec((rows, n), lambda i: (0, 0))) for n in splits]
+        outs = [((n, proj // 2), pl.BlockSpec((n, proj // 2), lambda i: (0, 0))) for n in splits]
     names = [i[0] for i in ins] + [f"out{i}" for i in range(len(outs))] + [s[0] for s in scratch]
     res = pl.pallas_call(
         functools.partial(_unit_kernel, names, parts, len(lhs), len(outs), index),
@@ -357,6 +366,7 @@
     width = arrays[0].shape[1]
     n_terms = sum(len(j[3]) for j in jobs)
     rows_in = sum(j[2] * len(j[3]) for j in jobs)
+    cuts = 1 if rows_in <= 32 else 2
     any_ = pl.BlockSpec(memory_space=pl.ANY)
     return pl.pallas_call(
         functools.partial(_sums_kernel, tuple(spec), len(arrays)),
@@ -364,7 +374,7 @@
         out_specs=[any_] * len(out_rows),
         out_shape=[jax.ShapeDtypeStruct((r, width), BF16) for r in out_rows],
         input_output_aliases={} if into is None else {0: 0},
-        scratch_shapes=[pltpu.VMEM((rows_in, width), BF16), pltpu.SemaphoreType.DMA((2, n_terms)), pltpu.SemaphoreType.DMA((2, len(jobs)))],
+        scratch_shapes=[pltpu.VMEM((rows_in, width), BF16), pltpu.SemaphoreType.DMA((cuts, n_terms)), pltpu.SemaphoreType.DMA((cuts, len(jobs)))],
         compiler_params=pltpu.CompilerParams(vmem_limit_bytes=VMEM_BYTES),
         cost_estimate=pl.CostEstimate(flops=rows_in * width, bytes_accessed=4 * rows_in * width, transcendentals=0),
         name="sums",
@@ -406,7 +416,7 @@
     def local_step(x_loc, ln_gain, wq_loc, w_kv, wo_loc, positions):
         me = lax.axis_index(AXIS)
         rows, width = x_loc.shape
-        seq, head = positions.shape[0], w_kv.shape[1] // 2
+        seq = positions.shape[0]
         piece = rows // 4
         gain = ln_gain.reshape(1, width)
 
@@ -421,7 +431,7 @@
         h[0] = [head_rows, middle, tail_rows]
         for i, v in enumerate(norm_rows(x_loc, gain, piece, piece, 3, piece // 2)):
             h[i + 1].append(v)
-        k_own, v_own = unit_call(sum(h, []), w_kv, None, None, None, None, None, 0, [head, head], slots=4, chunk=2048)
+        k_own, v_own = unit_call(sum(h, []), w_kv, None, None, None, None, None, 0, [rows - piece, rows + piece], slots=4, chunk=2048)
         sent = [[early] + h[0][1:]] + h[1:]
         for i in range(4):
             fx[i], fy[i] = send_all(sent[i], XN), send_all(sent[i], YN)
@@ -475,7 +485,7 @@
         py, = total(parts[YN, 3])
         got[3] = send(py, YN)
         last = []
-        for i, j, cuts in ((0, 2, (piece,)), (1, 3, (piece // 2, piece // 4, piece // 4))):
+        for i, j, cuts in ((0, 2, (piece,)), (1, 3, (piece // 2, piece // 4, piece // 8, piece // 8))):
             hx, hy = both(i, j)
             first = 0
             for n in cuts:

time: 916 us -> 932 us (1.017)
    ppermute x80 -> x82, waiting for transfers between devices: 348 us -> 355 us  [send(): return lax.ppermute(value, AXIS, [(i, i ^ mask) for i in range(n_dev)])]
    ppermute x80 -> x82, starting transfers between devices: 47.1 us -> 53 us  [send(): return lax.ppermute(value, AXIS, [(i, i ^ mask) for i in range(n_dev)])]
    pallas_call x14 -> x16, Pallas kernels: 72.1 us -> 76.2 us  [sums(): pl.pallas_call(functools.partial(_sums_kernel, tuple(spec), len(arrays)),...]
  transfers between devices with their start and end apart: 80 -> 82, of which waited for: 22 -> 16; matrix products, arithmetic and copies ran while one was open for 0% -> 0% of each run, Pallas kernels for 52% -> 52%
where the time goes in v1:
time: 932 us; the launch traced here: 931 us
  Pallas kernels  517 us (55%)
  waiting for transfers between devices  355 us (38%)
  starting transfers between devices  53 us (6%)
    pallas_call x9, Pallas kernels, unit_call(): pl.pallas_call(functools.partial(_unit_kernel, names, parts, len(lhs), le...  415 us
    ppermute x82, waiting for transfers between devices, send(): return lax.ppermute(value, AXIS, [(i, i ^ mask) for i in range(n_dev)])  355 us
    pallas_call x16, Pallas kernels, sums(): pl.pallas_call(functools.partial(_sums_kernel, tuple(spec), len(arrays)),...  76.2 us
    ppermute x82, starting transfers between devices, send(): return lax.ppermute(value, AXIS, [(i, i ^ mask) for i in range(n_dev)])  53 us
    pallas_call x3, Pallas kernels, norm_rows(): pl.pallas_call(functools.partial(_norm_kernel, 2048, steps), grid=(count...  18.8 us
  transfers between devices with their start and end apart: 82, of which 16 were waited for; matrix products, arithmetic and copies ran while one was open for 0% of the time, Pallas kernels for 52%

profile of v1, /device:TPU:0, one launch (start us, length us, event | category | flops | bytes accessed | tf_op | source)
XLA Modules:
  0.0 931.2 jit_solution(1471083013006483624)
XLA Ops:
  0.6 11.6 %norm.6 = (bf16[64,18432]{1,0:T(8,128)(2,1)}, bf16[64,18432]{1,0:T(8,128)(2,1)}, bf16[64,18432]{1,0:T(8,128)(2,1)}) custom-call(bf16[256,18432]{1,0:T(8,128)(2,1)} %x_hbm.1, f32[1,18432]{1,0:T(1,128)} %bitcast.66), custom_call_target="tpu_custom_call" | custom-call | flops 28311552 | bytes 14155776 | tf_op jit(solution)/shard_map/norm/pallas_call | solution.py:92
  12.3 3.7 norm.4
  15.9 3.5 norm.5.flat_1_
  19.4 11.0 %shard_map.85 = (bf16[192,256]{1,0:T(8,128)(2,1)}, bf16[320,256]{1,0:T(8,128)(2,1)}) custom-call(bf16[16,18432]{1,0:T(8,128)(2,1)} %get-tuple-element.54.flat_0_, bf16[32,18432]{1,0:T(8,128)(2,1)} %norm.5.flat_1_, bf16[16,18432]{1,0:T(8,128)(2,1)} %get-tuple-element.55.flat_2_, bf16[64,18432]{1,0:T(8,128)(2,1)} %get-tuple-element.56.flat_3_, ...), custom_call_target="tpu_custom_call" | custom-call | flops 4831838208 | bytes 28311552 | tf_op jit(solution)/shard_map/pallas_call | solution.py:301
  30.5 3.4 collective-permute-start.14
  33.8 1.5 collective-permute-start.5
  35.9 3.8 collective-permute-done.5.flat_12_.flat_16_.flat_8_.refs_2_
  39.7 1.5 collective-permute-start.16
  41.2 1.3 collective-permute-start.9
  43.7 2.5 collective-permute-done.9.flat_16_.flat_20_.flat_12_.refs_6_
  46.7 1.7 norm.7
  48.5 1.2 collective-permute-start.21
  52.1 12.7 %collective-permute-done.21.flat_2_ = bf16[16,18432]{1,0:T(8,128)(2,1)} collective-permute-done((bf16[16,18432]{1,0:T(8,128)(2,1)S(1)}, bf16[16,18432]{1,0:T(8,128)(2,1)}, u32[]{:S(2)}, u32[]{:S(2)}) %collective-permute-start.21) | collective-permute-done | bytes 589856 | tf_op jit(solution)/shard_map/ppermute | solution.py:408
  65.8 11.0 %collective-permute-done.19.flat_0_ = bf16[16,18432]{1,0:T(8,128)(2,1)S(1)} collective-permute-done((bf16[16,18432]{1,0:T(8,128)(2,1)S(1)}, bf16[16,18432]{1,0:T(8,128)(2,1)S(1)}, u32[]{:S(2)}, u32[]{:S(2)}) %collective-permute-start.19) | collective-permute-done | bytes 589856 | tf_op jit(solution)/shard_map/ppermute | solution.py:408
  81.4 13.7 %collective-permute-done.51.flat_2_ = bf16[16,18432]{1,0:T(8,128)(2,1)S(1)} collective-permute-done((bf16[16,18432]{1,0:T(8,128)(2,1)}, bf16[16,18432]{1,0:T(8,128)(2,1)S(1)}, u32[]{:S(2)}, u32[]{:S(2)}) %collective-permute-start.51) | collective-permute-done | bytes 589856 | tf_op jit(solution)/shard_map/ppermute | solution.py:408
  96.2 9.4 %collective-permute-done.20.flat_1_ = bf16[32,18432]{1,0:T(8,128)(2,1)} collective-permute-done((bf16[32,18432]{1,0:T(8,128)(2,1)}, bf16[32,18432]{1,0:T(8,128)(2,1)}, u32[]{:S(2)}, u32[]{:S(2)}) %collective-permute-start.20) | collective-permute-done | bytes 1179680 | tf_op jit(solution)/shard_map/ppermute | solution.py:408
  109.1 1.3 where.1
  112.4 50.4 %shard_map.89 = (bf16[64,18432]{1,0:T(8,128)(2,1)}, bf16[64,18432]{1,0:T(8,128)(2,1)}, bf16[128,18432]{1,0:T(8,128)(2,1)}) custom-call(bf16[64,18432]{1,0:T(8,128)(2,1)} %get-tuple-element.57.flat_4_.flat_0_, bf16[64,18432]{1,0:T(8,128)(2,1)} %get-tuple-element.58.flat_5_.flat_1_, bf16[64,18432]{1,0:T(8,128)(2,1)} %collective-permute-done.39.flat_2_, ...), custom_call_target="tpu_custom_call" | custom-call | flops 32212254720 | bytes 132120576 | tf_op jit(solution)/shard_map/pallas_call | solution.py:301
  165.6 50.6 %shard_map.86 = (bf16[64,18432]{1,0:T(8,128)(2,1)}, bf16[64,18432]{1,0:T(8,128)(2,1)}, bf16[128,18432]{1,0:T(8,128)(2,1)}) custom-call(bf16[16,18432]{1,0:T(8,128)(2,1)} %get-tuple-element.54.flat_0_, bf16[32,18432]{1,0:T(8,128)(2,1)} %norm.5.flat_1_, bf16[16,18432]{1,0:T(8,128)(2,1)} %get-tuple-element.55.flat_2_, ...), custom_call_target="tpu_custom_call" | custom-call | flops 32212254720 | bytes 132120576 | tf_op jit(solution)/shard_map/pallas_call | solution.py:301
  219.6 51.2 %shard_map.87 = (bf16[64,18432]{1,0:T(8,128)(2,1)}, bf16[64,18432]{1,0:T(8,128)(2,1)}, bf16[128,18432]{1,0:T(8,128)(2,1)}) custom-call(bf16[16,18432]{1,0:T(8,128)(2,1)} %copy-done.18, bf16[32,18432]{1,0:T(8,128)(2,1)} %collective-permute-done.20.flat_1_, bf16[16,18432]{1,0:T(8,128)(2,1)} %collective-permute-done.21.flat_2_, bf16[16,18432]{1,0:T(8,128)(2,1)} %copy-done.20, ...), custom_call_target="tpu_custom_call" | custom-call | flops 32212254720 | bytes 132120576 | tf_op jit(solution)/shard_map/pallas_call | solution.py:301
  272.0 48.7 %collective-permute-done.34.flat_1_ = bf16[64,18432]{1,0:T(8,128)(2,1)} collective-permute-done((bf16[64,18432]{1,0:T(8,128)(2,1)}, bf16[64,18432]{1,0:T(8,128)(2,1)}, u32[]{:S(2)}, u32[]{:S(2)}) %collective-permute-start.34) | collective-permute-done | bytes 2359328 | tf_op jit(solution)/shard_map/ppermute | solution.py:408
  323.1 50.4 %shard_map.92 = (bf16[64,18432]{1,0:T(8,128)(2,1)}, bf16[64,18432]{1,0:T(8,128)(2,1)}, bf16[128,18432]{1,0:T(8,128)(2,1)}) custom-call(bf16[64,18432]{1,0:T(8,128)(2,1)} %collective-permute-done.62.flat_0_, bf16[64,18432]{1,0:T(8,128)(2,1)} %collective-permute-done.63.flat_1_, bf16[64,18432]{1,0:T(8,128)(2,1)} %collective-permute-done.64.flat_2_, ...), custom_call_target="tpu_custom_call" | custom-call | flops 32212254720 | bytes 132120576 | tf_op jit(solution)/shard_map/pallas_call | solution.py:301
  376.4 50.4 %shard_map.90 = (bf16[64,18432]{1,0:T(8,128)(2,1)}, bf16[64,18432]{1,0:T(8,128)(2,1)}, bf16[128,18432]{1,0:T(8,128)(2,1)}) custom-call(bf16[64,18432]{1,0:T(8,128)(2,1)} %collective-permute-done.43.flat_0_, bf16[64,18432]{1,0:T(8,128)(2,1)} %collective-permute-done.44.flat_1_, bf16[64,18432]{1,0:T(8,128)(2,1)} %collective-permute-done.45.flat_2_, ...), custom_call_target="tpu_custom_call" | custom-call | flops 32212254720 | bytes 132120576 | tf_op jit(solution)/shard_map/pallas_call | solution.py:301
  428.8 50.9 %shard_map.91 = (bf16[64,18432]{1,0:T(8,128)(2,1)}, bf16[64,18432]{1,0:T(8,128)(2,1)}, bf16[128,18432]{1,0:T(8,128)(2,1)}) custom-call(bf16[16,18432]{1,0:T(8,128)(2,1)} %copy-done.17, bf16[32,18432]{1,0:T(8,128)(2,1)} %collective-permute-done.50.flat_1_, bf16[16,18432]{1,0:T(8,128)(2,1)} %copy-done.16, bf16[64,18432]{1,0:T(8,128)(2,1)} %collective-permute-done.52.flat_3_, ...), custom_call_target="tpu_custom_call" | custom-call | flops 32212254720 | bytes 132120576 | tf_op jit(solution)/shard_map/pallas_call | solution.py:301
  480.2 50.3 %shard_map.93 = (bf16[64,18432]{1,0:T(8,128)(2,1)}, bf16[64,18432]{1,0:T(8,128)(2,1)}, bf16[128,18432]{1,0:T(8,128)(2,1)}) custom-call(bf16[64,18432]{1,0:T(8,128)(2,1)} %collective-permute-done.67.flat_0_, bf16[64,18432]{1,0:T(8,128)(2,1)} %collective-permute-done.68.flat_1_, bf16[64,18432]{1,0:T(8,128)(2,1)} %collective-permute-done.69.flat_2_, ...), custom_call_target="tpu_custom_call" | custom-call | flops 32212254720 | bytes 132120576 | tf_op jit(solution)/shard_map/pallas_call | solution.py:301
  531.6 50.4 %shard_map.88 = (bf16[64,18432]{1,0:T(8,128)(2,1)}, bf16[64,18432]{1,0:T(8,128)(2,1)}, bf16[128,18432]{1,0:T(8,128)(2,1)}) custom-call(bf16[64,18432]{1,0:T(8,128)(2,1)} %collective-permute-done.33.flat_0_, bf16[64,18432]{1,0:T(8,128)(2,1)} %collective-permute-done.34.flat_1_, bf16[64,18432]{1,0:T(8,128)(2,1)} %collective-permute-done.35.flat_2_, ...), custom_call_target="tpu_custom_call" | custom-call | flops 32212254720 | bytes 132120576 | tf_op jit(solution)/shard_map/pallas_call | solution.py:301
  582.5 3.8 sums.16
  586.3 6.1 sums.20
  595.6 6.1 sums.23
  603.6 3.8 sums.18
  607.4 6.0 sums.17
  613.4 33.4 %collective-permute-done.32.refs_2_ = bf16[64,18432]{1,0:T(8,128)(2,1)} collective-permute-done((bf16[64,18432]{1,0:T(8,128)(2,1)}, bf16[64,18432]{1,0:T(8,128)(2,1)}, u32[]{:S(2)}, u32[]{:S(2)}) %collective-permute-start.32) | collective-permute-done | bytes 2359328 | tf_op jit(solution)/shard_map/ppermute | solution.py:408
  648.0 49.4 %collective-permute-done.58.refs_2_ = bf16[64,18432]{1,0:T(8,128)(2,1)} collective-permute-done((bf16[64,18432]{1,0:T(8,128)(2,1)}, bf16[64,18432]{1,0:T(8,128)(2,1)}, u32[]{:S(2)}, u32[]{:S(2)}) %collective-permute-start.58) | collective-permute-done | bytes 2359328 | tf_op jit(solution)/shard_map/ppermute | solution.py:408
  699.4 7.6 sums.21
  707.1 40.9 %collective-permute-done.72.refs_2_ = bf16[64,18432]{1,0:T(8,128)(2,1)} collective-permute-done((bf16[64,18432]{1,0:T(8,128)(2,1)}, bf16[64,18432]{1,0:T(8,128)(2,1)}, u32[]{:S(2)}, u32[]{:S(2)}) %collective-permute-start.72) | collective-permute-done | bytes 2359328 | tf_op jit(solution)/shard_map/ppermute | solution.py:408
  750.0 4.6 sums.24
  755.6 42.9 %collective-permute-done.38.refs_4_ = bf16[64,18432]{1,0:T(8,128)(2,1)} collective-permute-done((bf16[64,18432]{1,0:T(8,128)(2,1)}, bf16[64,18432]{1,0:T(8,128)(2,1)}, u32[]{:S(2)}, u32[]{:S(2)}) %collective-permute-start.38) | collective-permute-done | bytes 2359328 | tf_op jit(solution)/shard_map/ppermute | solution.py:408
  799.5 3.0 sums.26
  803.6 84.0 %collective-permute-done.76.refs_1_ = bf16[16,18432]{1,0:T(8,128)(2,1)} collective-permute-done((bf16[16,18432]{1,0:T(8,128)(2,1)}, bf16[16,18432]{1,0:T(8,128)(2,1)}, u32[]{:S(2)}, u32[]{:S(2)}) %collective-permute-start.76) | collective-permute-done | bytes 589856 | tf_op jit(solution)/shard_map/ppermute | solution.py:408
  888.5 2.5 sums.30
  891.0 2.5 sums.28
  897.6 3.1 order.1
  900.7 13.5 %sums.19.refs_0_ = bf16[256,18432]{1,0:T(8,128)(2,1)} custom-call(bf16[64,18432]{1,0:T(8,128)(2,1)} %get-tuple-element.63.refs_0_, bf16[128,18432]{1,0:T(8,128)(2,1)} %collective-permute-done.18.refs_1_, bf16[64,18432]{1,0:T(8,128)(2,1)} %collective-permute-done.32.refs_2_, bf16[64,18432]{1,0:T(8,128)(2,1)} %get-tuple-element.67.refs_3_, ...), custom_call_target="tpu_custom_call" | custom-call | flops 14155776 | bytes 56623104 | tf_op jit(solution)/shard_map/sums/pallas_call | solution.py:371
  914.2 6.1 sums.22.refs_0_
  920.2 3.5 sums.25.refs_0_
  923.7 2.6 sums.27.refs_0_
  926.3 2.3 sums.29.refs_0_
  928.7 2.3 sums.31
  (200 shorter events, 51.9 us)
Async XLA Ops:
  51.6 60.3 %collective-permute-start.39 = (bf16[64,18432]{1,0:T(8,128)(2,1)S(1)}, bf16[64,18432]{1,0:T(8,128)(2,1)}, u32[]{:S(2)}, u32[]{:S(2)}) collective-permute-start(bf16[64,18432]{1,0:T(8,128)(2,1)S(1)} %copy-done.7), channel_id=1, source_target_pairs={{0,1},{1,0},{2,3},{3,2},{4,5},{5,4},{6,7},{7,6}} | collective-permute-start | bytes 7077896 | tf_op jit(solution)/shard_map/ppermute | solution.py:408
  51.6 60.5 %collective-permute-start.40 = (bf16[64,18432]{1,0:T(8,128)(2,1)}, bf16[64,18432]{1,0:T(8,128)(2,1)}, u32[]{:S(2)}, u32[]{:S(2)}) collective-permute-start(bf16[64,18432]{1,0:T(8,128)(2,1)} %get-tuple-element.58.flat_5_.flat_1_), channel_id=1, source_target_pairs={{0,1},{1,0},{2,3},{3,2},{4,5},{5,4},{6,7},{7,6}} | collective-permute-start | bytes 7077896 | tf_op jit(solution)/shard_map/ppermute | solution.py:408
  110.4 52.5 %collective-permute-start.23 = (bf16[32,18432]{1,0:T(8,128)(2,1)}, bf16[32,18432]{1,0:T(8,128)(2,1)}, u32[]{:S(2)}, u32[]{:S(2)}) collective-permute-start(bf16[32,18432]{1,0:T(8,128)(2,1)} %norm.5.flat_1_), channel_id=1, source_target_pairs={{0,4},{1,5},{2,6},{3,7},{4,0},{5,1},{6,2},{7,3}} | collective-permute-start | bytes 3538952 | tf_op jit(solution)/shard_map/ppermute | solution.py:408
  111.4 54.2 %collective-permute-start.3 = (bf16[64,18432]{1,0:T(8,128)(2,1)}, bf16[64,18432]{1,0:T(8,128)(2,1)}, u32[]{:S(2)}, u32[]{:S(2)}) collective-permute-start(bf16[64,18432]{1,0:T(8,128)(2,1)} %get-tuple-element.56.flat_3_), channel_id=1, source_target_pairs={{0,1},{1,0},{2,3},{3,2},{4,5},{5,4},{6,7},{7,6}} | collective-permute-start | bytes 7077896 | tf_op jit(solution)/shard_map/ppermute | solution.py:408
  111.6 53.4 %collective-permute-start.1 = (bf16[32,18432]{1,0:T(8,128)(2,1)}, bf16[32,18432]{1,0:T(8,128)(2,1)}, u32[]{:S(2)}, u32[]{:S(2)}) collective-permute-start(bf16[32,18432]{1,0:T(8,128)(2,1)} %norm.5.flat_1_), channel_id=1, source_target_pairs={{0,1},{1,0},{2,3},{3,2},{4,5},{5,4},{6,7},{7,6}} | collective-permute-start | bytes 3538952 | tf_op jit(solution)/shard_map/ppermute | solution.py:408
  111.9 52.0 %collective-permute-start.25 = (bf16[16,18432]{1,0:T(8,128)(2,1)}, bf16[16,18432]{1,0:T(8,128)(2,1)}, u32[]{:S(2)}, u32[]{:S(2)}) collective-permute-start(bf16[16,18432]{1,0:T(8,128)(2,1)} %copy-done.18), channel_id=1, source_target_pairs={{0,1},{1,0},{2,3},{3,2},{4,5},{5,4},{6,7},{7,6}} | collective-permute-start | bytes 1769480 | tf_op jit(solution)/shard_map/ppermute | solution.py:408
  112.1 52.9 %collective-permute-start.28 = (bf16[16,18432]{1,0:T(8,128)(2,1)}, bf16[16,18432]{1,0:T(8,128)(2,1)}, u32[]{:S(2)}, u32[]{:S(2)}) collective-permute-start(bf16[16,18432]{1,0:T(8,128)(2,1)} %copy-done.20), channel_id=1, source_target_pairs={{0,1},{1,0},{2,3},{3,2},{4,5},{5,4},{6,7},{7,6}} | collective-permute-start | bytes 1769480 | tf_op jit(solution)/shard_map/ppermute | solution.py:408
  162.8 54.2 %collective-permute-start.62 = (bf16[64,18432]{1,0:T(8,128)(2,1)}, bf16[64,18432]{1,0:T(8,128)(2,1)}, u32[]{:S(2)}, u32[]{:S(2)}) collective-permute-start(bf16[64,18432]{1,0:T(8,128)(2,1)} %get-tuple-element.58.flat_5_.flat_1_), channel_id=1, source_target_pairs={{0,2},{1,3},{2,0},{3,1},{4,6},{5,7},{6,4},{7,5}} | collective-permute-start | bytes 7077896 | tf_op jit(solution)/shard_map/ppermute | solution.py:408
  163.9 54.3 %collective-permute-start.63 = (bf16[64,18432]{1,0:T(8,128)(2,1)}, bf16[64,18432]{1,0:T(8,128)(2,1)}, u32[]{:S(2)}, u32[]{:S(2)}) collective-permute-start(bf16[64,18432]{1,0:T(8,128)(2,1)} %get-tuple-element.56.flat_3_), channel_id=1, source_target_pairs={{0,4},{1,5},{2,6},{3,7},{4,0},{5,1},{6,2},{7,3}} | collective-permute-start | bytes 7077896 | tf_op jit(solution)/shard_map/ppermute | solution.py:408
  165.0 54.1 %collective-permute-start.26 = (bf16[32,18432]{1,0:T(8,128)(2,1)}, bf16[32,18432]{1,0:T(8,128)(2,1)}, u32[]{:S(2)}, u32[]{:S(2)}) collective-permute-start(bf16[32,18432]{1,0:T(8,128)(2,1)} %collective-permute-done.20.flat_1_), channel_id=1, source_target_pairs={{0,1},{1,0},{2,3},{3,2},{4,5},{5,4},{6,7},{7,6}} | collective-permute-start | bytes 3538952 | tf_op jit(solution)/shard_map/ppermute | solution.py:408
  165.5 53.6 %collective-permute-start.29 = (bf16[32,18432]{1,0:T(8,128)(2,1)}, bf16[32,18432]{1,0:T(8,128)(2,1)}, u32[]{:S(2)}, u32[]{:S(2)}) collective-permute-start(bf16[32,18432]{1,0:T(8,128)(2,1)} %collective-permute-done.23.flat_4_), channel_id=1, source_target_pairs={{0,1},{1,0},{2,3},{3,2},{4,5},{5,4},{6,7},{7,6}} | collective-permute-start | bytes 3538952 | tf_op jit(solution)/shard_map/ppermute | solution.py:408
  216.2 54.7 %collective-permute-start.44 = (bf16[64,18432]{1,0:T(8,128)(2,1)}, bf16[64,18432]{1,0:T(8,128)(2,1)}, u32[]{:S(2)}, u32[]{:S(2)}) collective-permute-start(bf16[64,18432]{1,0:T(8,128)(2,1)} %get-tuple-element.58.flat_5_.flat_1_), channel_id=1, source_target_pairs={{0,4},{1,5},{2,6},{3,7},{4,0},{5,1},{6,2},{7,3}} | collective-permute-start | bytes 7077896 | tf_op jit(solution)/shard_map/ppermute | solution.py:408
  217.1 103.6 %collective-permute-start.34 = (bf16[64,18432]{1,0:T(8,128)(2,1)}, bf16[64,18432]{1,0:T(8,128)(2,1)}, u32[]{:S(2)}, u32[]{:S(2)}) collective-permute-start(bf16[64,18432]{1,0:T(8,128)(2,1)} %get-tuple-element.57.flat_4_.flat_0_), channel_id=1, source_target_pairs={{0,4},{1,5},{2,6},{3,7},{4,0},{5,1},{6,2},{7,3}} | collective-permute-start | bytes 7077896 | tf_op jit(solution)/shard_map/ppermute | solution.py:408
  218.2 103.4 %collective-permute-start.43 = (bf16[64,18432]{1,0:T(8,128)(2,1)}, bf16[64,18432]{1,0:T(8,128)(2,1)}, u32[]{:S(2)}, u32[]{:S(2)}) collective-permute-start(bf16[64,18432]{1,0:T(8,128)(2,1)} %get-tuple-element.57.flat_4_.flat_0_), channel_id=1, source_target_pairs={{0,2},{1,3},{2,0},{3,1},{4,6},{5,7},{6,4},{7,5}} | collective-permute-start | bytes 7077896 | tf_op jit(solution)/shard_map/ppermute | solution.py:408
  219.1 103.5 %collective-permute-start.64 = (bf16[64,18432]{1,0:T(8,128)(2,1)}, bf16[64,18432]{1,0:T(8,128)(2,1)}, u32[]{:S(2)}, u32[]{:S(2)}) collective-permute-start(bf16[64,18432]{1,0:T(8,128)(2,1)} %collective-permute-done.62.flat_0_), channel_id=1, source_target_pairs={{0,1},{1,0},{2,3},{3,2},{4,5},{5,4},{6,7},{7,6}} | collective-permute-start | bytes 7077896 | tf_op jit(solution)/shard_map/ppermute | solution.py:408
  219.1 103.5 %collective-permute-start.65 = (bf16[64,18432]{1,0:T(8,128)(2,1)}, bf16[64,18432]{1,0:T(8,128)(2,1)}, u32[]{:S(2)}, u32[]{:S(2)}) collective-permute-start(bf16[64,18432]{1,0:T(8,128)(2,1)} %collective-permute-done.63.flat_1_), channel_id=1, source_target_pairs={{0,1},{1,0},{2,3},{3,2},{4,5},{5,4},{6,7},{7,6}} | collective-permute-start | bytes 7077896 | tf_op jit(solution)/shard_map/ppermute | solution.py:408
  270.8 102.7 %collective-permute-start.33 = (bf16[64,18432]{1,0:T(8,128)(2,1)}, bf16[64,18432]{1,0:T(8,128)(2,1)}, u32[]{:S(2)}, u32[]{:S(2)}) collective-permute-start(bf16[64,18432]{1,0:T(8,128)(2,1)} %get-tuple-element.56.flat_3_), channel_id=1, source_target_pairs={{0,2},{1,3},{2,0},{3,1},{4,6},{5,7},{6,4},{7,5}} | collective-permute-start | bytes 7077896 | tf_op jit(solution)/shard_map/ppermute | solution.py:408
  320.7 52.8 %collective-permute-start.50 = (bf16[32,18432]{1,0:T(8,128)(2,1)}, bf16[32,18432]{1,0:T(8,128)(2,1)}, u32[]{:S(2)}, u32[]{:S(2)}) collective-permute-start(bf16[32,18432]{1,0:T(8,128)(2,1)} %collective-permute-done.20.flat_1_), channel_id=1, source_target_pairs={{0,4},{1,5},{2,6},{3,7},{4,0},{5,1},{6,2},{7,3}} | collective-permute-start | bytes 3538952 | tf_op jit(solution)/shard_map/ppermute | solution.py:408
  321.6 53.3 %collective-permute-start.52 = (bf16[64,18432]{1,0:T(8,128)(2,1)}, bf16[64,18432]{1,0:T(8,128)(2,1)}, u32[]{:S(2)}, u32[]{:S(2)}) collective-permute-start(bf16[64,18432]{1,0:T(8,128)(2,1)} %collective-permute-done.34.flat_1_), channel_id=1, source_target_pairs={{0,2},{1,3},{2,0},{3,1},{4,6},{5,7},{6,4},{7,5}} | collective-permute-start | bytes 7077896 | tf_op jit(solution)/shard_map/ppermute | solution.py:408
  322.6 53.3 %collective-permute-start.46 = (bf16[64,18432]{1,0:T(8,128)(2,1)}, bf16[64,18432]{1,0:T(8,128)(2,1)}, u32[]{:S(2)}, u32[]{:S(2)}) collective-permute-start(bf16[64,18432]{1,0:T(8,128)(2,1)} %collective-permute-done.44.flat_1_), channel_id=1, source_target_pairs={{0,1},{1,0},{2,3},{3,2},{4,5},{5,4},{6,7},{7,6}} | collective-permute-start | bytes 7077896 | tf_op jit(solution)/shard_map/ppermute | solution.py:408
  322.6 53.3 %collective-permute-start.45 = (bf16[64,18432]{1,0:T(8,128)(2,1)}, bf16[64,18432]{1,0:T(8,128)(2,1)}, u32[]{:S(2)}, u32[]{:S(2)}) collective-permute-start(bf16[64,18432]{1,0:T(8,128)(2,1)} %collective-permute-done.43.flat_0_), channel_id=1, source_target_pairs={{0,1},{1,0},{2,3},{3,2},{4,5},{5,4},{6,7},{7,6}} | collective-permute-start | bytes 7077896 | tf_op jit(solution)/shard_map/ppermute | solution.py:408
  373.5 53.3 %collective-permute-start.53 = (bf16[16,18432]{1,0:T(8,128)(2,1)}, bf16[16,18432]{1,0:T(8,128)(2,1)}, u32[]{:S(2)}, u32[]{:S(2)}) collective-permute-start(bf16[16,18432]{1,0:T(8,128)(2,1)} %copy-done.17), channel_id=1, source_target_pairs={{0,1},{1,0},{2,3},{3,2},{4,5},{5,4},{6,7},{7,6}} | collective-permute-start | bytes 1769480 | tf_op jit(solution)/shard_map/ppermute | solution.py:408
  373.5 54.7 %collective-permute-start.68 = (bf16[64,18432]{1,0:T(8,128)(2,1)}, bf16[64,18432]{1,0:T(8,128)(2,1)}, u32[]{:S(2)}, u32[]{:S(2)}) collective-permute-start(bf16[64,18432]{1,0:T(8,128)(2,1)} %collective-permute-done.44.flat_1_), channel_id=1, source_target_pairs={{0,2},{1,3},{2,0},{3,1},{4,6},{5,7},{6,4},{7,5}} | collective-permute-start | bytes 7077896 | tf_op jit(solution)/shard_map/ppermute | solution.py:408
  374.9 53.3 %collective-permute-start.67 = (bf16[64,18432]{1,0:T(8,128)(2,1)}, bf16[64,18432]{1,0:T(8,128)(2,1)}, u32[]{:S(2)}, u32[]{:S(2)}) collective-permute-start(bf16[64,18432]{1,0:T(8,128)(2,1)} %collective-permute-done.33.flat_0_), channel_id=1, source_target_pairs={{0,4},{1,5},{2,6},{3,7},{4,0},{5,1},{6,2},{7,3}} | collective-permute-start | bytes 7077896 | tf_op jit(solution)/shard_map/ppermute | solution.py:408
  375.9 52.9 %collective-permute-start.56 = (bf16[64,18432]{1,0:T(8,128)(2,1)}, bf16[64,18432]{1,0:T(8,128)(2,1)}, u32[]{:S(2)}, u32[]{:S(2)}) collective-permute-start(bf16[64,18432]{1,0:T(8,128)(2,1)} %collective-permute-done.52.flat_3_), channel_id=1, source_target_pairs={{0,1},{1,0},{2,3},{3,2},{4,5},{5,4},{6,7},{7,6}} | collective-permute-start | bytes 7077896 | tf_op jit(solution)/shard_map/ppermute | solution.py:408
  426.8 104.3 %collective-permute-start.31 = (bf16[128,18432]{1,0:T(8,128)(2,1)}, bf16[128,18432]{1,0:T(8,128)(2,1)}, u32[]{:S(2)}, u32[]{:S(2)}) collective-permute-start(bf16[128,18432]{1,0:T(8,128)(2,1)} %get-tuple-element.66), channel_id=1, source_target_pairs={{0,1},{1,0},{2,3},{3,2},{4,5},{5,4},{6,7},{7,6}} | collective-permute-start | bytes 14155784 | tf_op jit(solution)/shard_map/ppermute | solution.py:408
  426.9 155.1 %collective-permute-start.41 = (bf16[128,18432]{1,0:T(8,128)(2,1)}, bf16[128,18432]{1,0:T(8,128)(2,1)}, u32[]{:S(2)}, u32[]{:S(2)}) collective-permute-start(bf16[128,18432]{1,0:T(8,128)(2,1)} %get-tuple-element.73), channel_id=1, source_target_pairs={{0,1},{1,0},{2,3},{3,2},{4,5},{5,4},{6,7},{7,6}} | collective-permute-start | bytes 14155784 | tf_op jit(solution)/shard_map/ppermute | solution.py:408
  428.2 102.3 %collective-permute-start.35 = (bf16[64,18432]{1,0:T(8,128)(2,1)}, bf16[64,18432]{1,0:T(8,128)(2,1)}, u32[]{:S(2)}, u32[]{:S(2)}) collective-permute-start(bf16[64,18432]{1,0:T(8,128)(2,1)} %collective-permute-done.33.flat_0_), channel_id=1, source_target_pairs={{0,1},{1,0},{2,3},{3,2},{4,5},{5,4},{6,7},{7,6}} | collective-permute-start | bytes 7077896 | tf_op jit(solution)/shard_map/ppermute | solution.py:408
  428.3 51.4 %collective-permute-start.69 = (bf16[64,18432]{1,0:T(8,128)(2,1)}, bf16[64,18432]{1,0:T(8,128)(2,1)}, u32[]{:S(2)}, u32[]{:S(2)}) collective-permute-start(bf16[64,18432]{1,0:T(8,128)(2,1)} %collective-permute-done.67.flat_0_), channel_id=1, source_target_pairs={{0,1},{1,0},{2,3},{3,2},{4,5},{5,4},{6,7},{7,6}} | collective-permute-start | bytes 7077896 | tf_op jit(solution)/shard_map/ppermute | solution.py:408
  428.8 51.4 %collective-permute-start.70 = (bf16[64,18432]{1,0:T(8,128)(2,1)}, bf16[64,18432]{1,0:T(8,128)(2,1)}, u32[]{:S(2)}, u32[]{:S(2)}) collective-permute-start(bf16[64,18432]{1,0:T(8,128)(2,1)} %collective-permute-done.68.flat_1_), channel_id=1, source_target_pairs={{0,1},{1,0},{2,3},{3,2},{4,5},{5,4},{6,7},{7,6}} | collective-permute-start | bytes 7077896 | tf_op jit(solution)/shard_map/ppermute | solution.py:408
  479.7 51.4 %collective-permute-start.36 = (bf16[64,18432]{1,0:T(8,128)(2,1)}, bf16[64,18432]{1,0:T(8,128)(2,1)}, u32[]{:S(2)}, u32[]{:S(2)}) collective-permute-start(bf16[64,18432]{1,0:T(8,128)(2,1)} %collective-permute-done.34.flat_1_), channel_id=1, source_target_pairs={{0,1},{1,0},{2,3},{3,2},{4,5},{5,4},{6,7},{7,6}} | collective-permute-start | bytes 7077896 | tf_op jit(solution)/shard_map/ppermute | solution.py:408
  480.2 101.9 %collective-permute-start.57 = (bf16[128,18432]{1,0:T(8,128)(2,1)}, bf16[128,18432]{1,0:T(8,128)(2,1)}, u32[]{:S(2)}, u32[]{:S(2)}) collective-permute-start(bf16[128,18432]{1,0:T(8,128)(2,1)} %get-tuple-element.80), channel_id=1, source_target_pairs={{0,1},{1,0},{2,3},{3,2},{4,5},{5,4},{6,7},{7,6}} | collective-permute-start | bytes 14155784 | tf_op jit(solution)/shard_map/ppermute | solution.py:408
  530.6 61.8 %collective-permute-start.18 = (bf16[128,18432]{1,0:T(8,128)(2,1)}, bf16[128,18432]{1,0:T(8,128)(2,1)}, u32[]{:S(2)}, u32[]{:S(2)}) collective-permute-start(bf16[128,18432]{1,0:T(8,128)(2,1)} %get-tuple-element.64), channel_id=1, source_target_pairs={{0,1},{1,0},{2,3},{3,2},{4,5},{5,4},{6,7},{7,6}} | collective-permute-start | bytes 14155784 | tf_op jit(solution)/shard_map/ppermute | solution.py:408
  531.1 62.3 %collective-permute-start.66 = (bf16[128,18432]{1,0:T(8,128)(2,1)}, bf16[128,18432]{1,0:T(8,128)(2,1)}, u32[]{:S(2)}, u32[]{:S(2)}) collective-permute-start(bf16[128,18432]{1,0:T(8,128)(2,1)} %get-tuple-element.88), channel_id=1, source_target_pairs={{0,1},{1,0},{2,3},{3,2},{4,5},{5,4},{6,7},{7,6}} | collective-permute-start | bytes 14155784 | tf_op jit(solution)/shard_map/ppermute | solution.py:408
  531.1 63.3 %collective-permute-start.71 = (bf16[128,18432]{1,0:T(8,128)(2,1)}, bf16[128,18432]{1,0:T(8,128)(2,1)}, u32[]{:S(2)}, u32[]{:S(2)}) collective-permute-start(bf16[128,18432]{1,0:T(8,128)(2,1)} %get-tuple-element.90), channel_id=1, source_target_pairs={{0,1},{1,0},{2,3},{3,2},{4,5},{5,4},{6,7},{7,6}} | collective-permute-start | bytes 14155784 | tf_op jit(solution)/shard_map/ppermute | solution.py:408
  592.4 54.5 %collective-permute-start.32 = (bf16[64,18432]{1,0:T(8,128)(2,1)}, bf16[64,18432]{1,0:T(8,128)(2,1)}, u32[]{:S(2)}, u32[]{:S(2)}) collective-permute-start(bf16[64,18432]{1,0:T(8,128)(2,1)} %sums.16), channel_id=1, source_target_pairs={{0,2},{1,3},{2,0},{3,1},{4,6},{5,7},{6,4},{7,5}} | collective-permute-start | bytes 7077896 | tf_op jit(solution)/shard_map/ppermute | solution.py:408
  593.4 104.0 %collective-permute-start.58 = (bf16[64,18432]{1,0:T(8,128)(2,1)}, bf16[64,18432]{1,0:T(8,128)(2,1)}, u32[]{:S(2)}, u32[]{:S(2)}) collective-permute-start(bf16[64,18432]{1,0:T(8,128)(2,1)} %get-tuple-element.82), channel_id=1, source_target_pairs={{0,2},{1,3},{2,0},{3,1},{4,6},{5,7},{6,4},{7,5}} | collective-permute-start | bytes 7077896 | tf_op jit(solution)/shard_map/ppermute | solution.py:408
  594.4 104.0 %collective-permute-start.59 = (bf16[64,18432]{1,0:T(8,128)(2,1)}, bf16[64,18432]{1,0:T(8,128)(2,1)}, u32[]{:S(2)}, u32[]{:S(2)}) collective-permute-start(bf16[64,18432]{1,0:T(8,128)(2,1)} %get-tuple-element.84), channel_id=1, source_target_pairs={{0,4},{1,5},{2,6},{3,7},{4,0},{5,1},{6,2},{7,3}} | collective-permute-start | bytes 7077896 | tf_op jit(solution)/shard_map/ppermute | solution.py:408
  601.6 146.3 %collective-permute-start.72 = (bf16[64,18432]{1,0:T(8,128)(2,1)}, bf16[64,18432]{1,0:T(8,128)(2,1)}, u32[]{:S(2)}, u32[]{:S(2)}) collective-permute-start(bf16[64,18432]{1,0:T(8,128)(2,1)} %get-tuple-element.92), channel_id=1, source_target_pairs={{0,2},{1,3},{2,0},{3,1},{4,6},{5,7},{6,4},{7,5}} | collective-permute-start | bytes 7077896 | tf_op jit(solution)/shard_map/ppermute | solution.py:408
  602.6 146.5 %collective-permute-start.73 = (bf16[64,18432]{1,0:T(8,128)(2,1)}, bf16[64,18432]{1,0:T(8,128)(2,1)}, u32[]{:S(2)}, u32[]{:S(2)}) collective-permute-start(bf16[64,18432]{1,0:T(8,128)(2,1)} %get-tuple-element.94), channel_id=1, source_target_pairs={{0,4},{1,5},{2,6},{3,7},{4,0},{5,1},{6,2},{7,3}} | collective-permute-start | bytes 7077896 | tf_op jit(solution)/shard_map/ppermute | solution.py:408
  646.8 107.7 %collective-permute-start.48 = (bf16[64,18432]{1,0:T(8,128)(2,1)}, bf16[64,18432]{1,0:T(8,128)(2,1)}, u32[]{:S(2)}, u32[]{:S(2)}) collective-permute-start(bf16[64,18432]{1,0:T(8,128)(2,1)} %sums.18), channel_id=1, source_target_pairs={{0,4},{1,5},{2,6},{3,7},{4,0},{5,1},{6,2},{7,3}} | collective-permute-start | bytes 7077896 | tf_op jit(solution)/shard_map/ppermute | solution.py:408
  697.4 101.1 %collective-permute-start.38 = (bf16[64,18432]{1,0:T(8,128)(2,1)}, bf16[64,18432]{1,0:T(8,128)(2,1)}, u32[]{:S(2)}, u32[]{:S(2)}) collective-permute-start(bf16[64,18432]{1,0:T(8,128)(2,1)} %get-tuple-element.71), channel_id=1, source_target_pairs={{0,2},{1,3},{2,0},{3,1},{4,6},{5,7},{6,4},{7,5}} | collective-permute-start | bytes 7077896 | tf_op jit(solution)/shard_map/ppermute | solution.py:408
  698.4 104.1 %collective-permute-start.42 = (bf16[64,18432]{1,0:T(8,128)(2,1)}, bf16[64,18432]{1,0:T(8,128)(2,1)}, u32[]{:S(2)}, u32[]{:S(2)}) collective-permute-start(bf16[64,18432]{1,0:T(8,128)(2,1)} %get-tuple-element.74), channel_id=1, source_target_pairs={{0,4},{1,5},{2,6},{3,7},{4,0},{5,1},{6,2},{7,3}} | collective-permute-start | bytes 7077896 | tf_op jit(solution)/shard_map/ppermute | solution.py:408
  748.0 147.8 %collective-permute-start.60 = (bf16[64,18432]{1,0:T(8,128)(2,1)}, bf16[64,18432]{1,0:T(8,128)(2,1)}, u32[]{:S(2)}, u32[]{:S(2)}) collective-permute-start(bf16[64,18432]{1,0:T(8,128)(2,1)} %get-tuple-element.85), channel_id=1, source_target_pairs={{0,4},{1,5},{2,6},{3,7},{4,0},{5,1},{6,2},{7,3}} | collective-permute-start | bytes 7077896 | tf_op jit(solution)/shard_map/ppermute | solution.py:408
  749.1 147.6 %collective-permute-start.61 = (bf16[64,18432]{1,0:T(8,128)(2,1)}, bf16[64,18432]{1,0:T(8,128)(2,1)}, u32[]{:S(2)}, u32[]{:S(2)}) collective-permute-start(bf16[64,18432]{1,0:T(8,128)(2,1)} %get-tuple-element.86), channel_id=1, source_target_pairs={{0,2},{1,3},{2,0},{3,1},{4,6},{5,7},{6,4},{7,5}} | collective-permute-start | bytes 7077896 | tf_op jit(solution)/shard_map/ppermute | solution.py:408
  754.6 139.0 %collective-permute-start.74 = (bf16[32,18432]{1,0:T(8,128)(2,1)}, bf16[32,18432]{1,0:T(8,128)(2,1)}, u32[]{:S(2)}, u32[]{:S(2)}) collective-permute-start(bf16[32,18432]{1,0:T(8,128)(2,1)} %get-tuple-element.95), channel_id=1, source_target_pairs={{0,4},{1,5},{2,6},{3,7},{4,0},{5,1},{6,2},{7,3}} | collective-permute-start | bytes 3538952 | tf_op jit(solution)/shard_map/ppermute | solution.py:408
  798.5 96.1 %collective-permute-start.75 = (bf16[32,18432]{1,0:T(8,128)(2,1)}, bf16[32,18432]{1,0:T(8,128)(2,1)}, u32[]{:S(2)}, u32[]{:S(2)}) collective-permute-start(bf16[32,18432]{1,0:T(8,128)(2,1)} %get-tuple-element.96), channel_id=1, source_target_pairs={{0,2},{1,3},{2,0},{3,1},{4,6},{5,7},{6,4},{7,5}} | collective-permute-start | bytes 3538952 | tf_op jit(solution)/shard_map/ppermute | solution.py:408
  802.5 85.0 %collective-permute-start.76 = (bf16[16,18432]{1,0:T(8,128)(2,1)}, bf16[16,18432]{1,0:T(8,128)(2,1)}, u32[]{:S(2)}, u32[]{:S(2)}) collective-permute-start(bf16[16,18432]{1,0:T(8,128)(2,1)} %get-tuple-element.97), channel_id=1, source_target_pairs={{0,4},{1,5},{2,6},{3,7},{4,0},{5,1},{6,2},{7,3}} | collective-permute-start | bytes 1769480 | tf_op jit(solution)/shard_map/ppermute | solution.py:408
  (56 other events, 891.9 us)

commit v2 on v1

--- a/solution.py
+++ b/solution.py
@@ -18,7 +18,7 @@
 BF16, F32 = jnp.bfloat16, jnp.float32
 
 
-def _norm_kernel(chunk, steps, x_ref, g_ref, *out_refs, landing=((),)):
+def _norm_kernel(chunk, steps, x_ref, g_ref, *out_refs):
     rows, width = x_ref.shape
     n_chunks = width // chunk
 
@@ -39,12 +39,7 @@
         return acc + fold(d * d)
 
     zero = jnp.zeros((rows, 128), F32)
-    total, part = zero, n_chunks // len(landing)
-    for i, copies in enumerate(landing):
-        for c in copies:
-            c.wait()
-        total = lax.fori_loop(i * part, (i + 1) * part, lambda c, acc: acc + fold(load(c)), total)
-    mean = jnp.sum(total, axis=1, keepdims=True) / width
+    mean = jnp.sum(lax.fori_loop(0, n_chunks, lambda c, acc: acc + fold(load(c)), zero), axis=1, keepdims=True) / width
     rstd = lax.rsqrt(jnp.sum(lax.fori_loop(0, n_chunks, square, zero), axis=1, keepdims=True) / width + NORM_EPS)
     for i, out_ref in enumerate(out_refs):
         @pl.when(pl.program_id(0) // steps == i)
@@ -56,30 +51,23 @@
             lax.fori_loop(0, n_chunks, put, 0)
 
 
-def _norm_first_kernel(chunk, x_hbm, g_hbm, out_ref, x_buf, g_buf, sem):
-    rows, width = x_buf.shape
-    halves = [pl.ds(i * width // 2, width // 2) for i in range(2)]
-    copies = [pltpu.make_async_copy(x_hbm.at[pl.ds(0, rows), c], x_buf.at[:, c], sem.at[i]) for i, c in enumerate(halves)]
-    copies.append(pltpu.make_async_copy(g_hbm, g_buf, sem.at[2]))
-    for c in copies:
-        c.start()
-    _norm_kernel(chunk, 1, x_buf, g_buf, out_ref, landing=(copies[:1], copies[1:]))
-
-
-def norm_first(x, gain, rows):
-    width = x.shape[1]
-    hbm = pl.BlockSpec(memory_space=pltpu.HBM)
+def _fetch_kernel(x_hbm, out_ref, sem):
+    copy = pltpu.make_async_copy(x_hbm.at[pl.ds(0, out_ref.shape[0]), :], out_ref, sem)
+    copy.start()
+    copy.wait()
+
+
+def fetch_first(x, rows):
     return pl.pallas_call(
-        functools.partial(_norm_first_kernel, 4608),
-        grid=(1,),
-        in_specs=[hbm, hbm],
+        _fetch_kernel,
+        in_specs=[pl.BlockSpec(memory_space=pltpu.HBM)],
         out_specs=pl.BlockSpec(memory_space=pltpu.VMEM),
-        out_shape=pltpu.VMEM((rows, width), BF16),
-        scratch_shapes=[pltpu.VMEM((rows, width), BF16), pltpu.VMEM(gain.shape, F32), pltpu.SemaphoreType.DMA((3,))],
-        compiler_params=pltpu.CompilerParams(dimension_semantics=("arbitrary",), vmem_limit_bytes=NORM_BYTES),
-        cost_estimate=pl.CostEstimate(flops=8 * rows * width, bytes_accessed=4 * rows * width, transcendentals=0),
-        name="norm",
-    )(x, gain)
+        out_shape=pltpu.VMEM((rows, x.shape[1]), BF16),
+        scratch_shapes=[pltpu.SemaphoreType.DMA],
+        compiler_params=pltpu.CompilerParams(vmem_limit_bytes=NORM_BYTES),
+        cost_estimate=pl.CostEstimate(flops=rows * x.shape[1], bytes_accessed=4 * rows * x.shape[1], transcendentals=0),
+        name="fetch",
+    )(x)
 
 
 def norm_rows(x, gain, first, piece, count, rows, stride=1):
@@ -425,7 +413,7 @@
 
         h, fx, fy, fd = [[] for _ in range(4)], [None] * 4, [None] * 4, [None] * 4
         a, b, _ = CUTS
-        early = norm_first(x_loc, gain, a)
+        early = fetch_first(x_loc, a)
         middle, = norm_rows(x_loc, gain, a, b, 1, a)
         head_rows, tail_rows = norm_rows(x_loc, gain, 0, a, 2, a, (a + b) // a)
         h[0] = [head_rows, middle, tail_rows]
@@ -439,6 +427,8 @@
             fd[i] = send_all(fx[i], YN)
         for i in (2, 3):
             fd[i] = send_all(fy[i], XN)
+        for far in (fx, fy, fd):
+            far[0] = [*norm_rows(far[0][0], gain, 0, a, 1, a), *far[0][1:]]
         k_m, v_m = {0: k_own}, {0: v_own}
         for m in (XN, YN):
             k_m[m], v_m[m] = send(k_own, m), send(v_own, m)

time: 932 us -> 940 us (level)
    pallas_call x3 -> x6, Pallas kernels: 18.8 us -> 26.8 us  [norm_rows(): pl.pallas_call(functools.partial(_norm_kernel, 2048, steps), grid=(count...]
where the time goes in v2:
time: 940 us; the launch traced here: 939 us
  Pallas kernels  524 us (56%)
  waiting for transfers between devices  355 us (38%)
  starting transfers between devices  54 us (6%)
    pallas_call x9, Pallas kernels, unit_call(): pl.pallas_call(functools.partial(_unit_kernel, names, parts, len(lhs), le...  415 us
    ppermute x82, waiting for transfers between devices, send(): return lax.ppermute(value, AXIS, [(i, i ^ mask) for i in range(n_dev)])  355 us
    pallas_call x16, Pallas kernels, sums(): pl.pallas_call(functools.partial(_sums_kernel, tuple(spec), len(arrays)),...  76.2 us
    ppermute x82, starting transfers between devices, send(): return lax.ppermute(value, AXIS, [(i, i ^ mask) for i in range(n_dev)])  54 us
    pallas_call x6, Pallas kernels, norm_rows(): pl.pallas_call(functools.partial(_norm_kernel, 2048, steps), grid=(count...  26.8 us
  transfers between devices with their start and end apart: 82, of which 16 were waited for; matrix products, arithmetic and copies ran while one was open for 0% of the time, Pallas kernels for 52%

profile of v2, /device:TPU:0, one launch (start us, length us, event | category | flops | bytes accessed | tf_op | source)
XLA Modules:
  0.0 938.8 jit_solution(7078503874156297440)
XLA Ops:
  0.6 11.6 %norm.8 = (bf16[64,18432]{1,0:T(8,128)(2,1)}, bf16[64,18432]{1,0:T(8,128)(2,1)}, bf16[64,18432]{1,0:T(8,128)(2,1)}) custom-call(bf16[256,18432]{1,0:T(8,128)(2,1)} %x_hbm.1, f32[1,18432]{1,0:T(1,128)} %bitcast.66), custom_call_target="tpu_custom_call" | custom-call | flops 28311552 | bytes 14155776 | tf_op jit(solution)/shard_map/norm/pallas_call | solution.py:80
  12.3 3.7 norm.6
  15.9 3.5 norm.7.flat_1_
  19.4 11.0 %shard_map.85 = (bf16[192,256]{1,0:T(8,128)(2,1)}, bf16[320,256]{1,0:T(8,128)(2,1)}) custom-call(bf16[16,18432]{1,0:T(8,128)(2,1)} %get-tuple-element.54.flat_0_, bf16[32,18432]{1,0:T(8,128)(2,1)} %norm.7.flat_1_, bf16[16,18432]{1,0:T(8,128)(2,1)} %get-tuple-element.55.flat_2_, bf16[64,18432]{1,0:T(8,128)(2,1)} %get-tuple-element.56.flat_3_, ...), custom_call_target="tpu_custom_call" | custom-call | flops 4831838208 | bytes 28311552 | tf_op jit(solution)/shard_map/pallas_call | solution.py:289
  30.5 3.4 collective-permute-start.14
  33.8 1.5 collective-permute-start.5
  35.9 2.7 collective-permute-done.5.flat_12_.flat_16_.flat_8_.refs_2_
  39.1 1.9 collective-permute-start.16
  41.0 1.5 collective-permute-start.9
  43.1 2.7 collective-permute-done.9.flat_16_.flat_20_.flat_12_.refs_6_
  52.1 12.4 %collective-permute-done.21.flat_2_ = bf16[16,18432]{1,0:T(8,128)(2,1)} collective-permute-done((bf16[16,18432]{1,0:T(8,128)(2,1)S(1)}, bf16[16,18432]{1,0:T(8,128)(2,1)}, u32[]{:S(2)}, u32[]{:S(2)}) %collective-permute-start.21) | collective-permute-done | bytes 589856 | tf_op jit(solution)/shard_map/ppermute | solution.py:396
  65.8 10.4 %collective-permute-done.19.x_ref = bf16[16,18432]{1,0:T(8,128)(2,1)} collective-permute-done((bf16[16,18432]{1,0:T(8,128)(2,1)S(1)}, bf16[16,18432]{1,0:T(8,128)(2,1)}, u32[]{:S(2)}, u32[]{:S(2)}) %collective-permute-start.19) | collective-permute-done | bytes 589856 | tf_op jit(solution)/shard_map/ppermute | solution.py:396
  82.0 12.5 %collective-permute-done.51.flat_2_ = bf16[16,18432]{1,0:T(8,128)(2,1)} collective-permute-done((bf16[16,18432]{1,0:T(8,128)(2,1)}, bf16[16,18432]{1,0:T(8,128)(2,1)}, u32[]{:S(2)}, u32[]{:S(2)}) %collective-permute-start.51) | collective-permute-done | bytes 589856 | tf_op jit(solution)/shard_map/ppermute | solution.py:396
  94.5 10.5 %collective-permute-done.49.x_ref = bf16[16,18432]{1,0:T(8,128)(2,1)} collective-permute-done((bf16[16,18432]{1,0:T(8,128)(2,1)}, bf16[16,18432]{1,0:T(8,128)(2,1)}, u32[]{:S(2)}, u32[]{:S(2)}) %collective-permute-start.49) | collective-permute-done | bytes 589856 | tf_op jit(solution)/shard_map/ppermute | solution.py:396
  109.8 2.7 norm.9.flat_0_
  112.4 2.7 norm.10.flat_3_
  115.1 2.7 norm.11.flat_0_
  120.1 50.3 %shard_map.89 = (bf16[64,18432]{1,0:T(8,128)(2,1)}, bf16[64,18432]{1,0:T(8,128)(2,1)}, bf16[128,18432]{1,0:T(8,128)(2,1)}) custom-call(bf16[64,18432]{1,0:T(8,128)(2,1)} %get-tuple-element.57.flat_4_.flat_0_, bf16[64,18432]{1,0:T(8,128)(2,1)} %get-tuple-element.58.flat_5_.flat_1_, bf16[64,18432]{1,0:T(8,128)(2,1)} %collective-permute-done.39.flat_2_, ...), custom_call_target="tpu_custom_call" | custom-call | flops 32212254720 | bytes 132120576 | tf_op jit(solution)/shard_map/pallas_call | solution.py:289
  172.7 50.6 %shard_map.86 = (bf16[64,18432]{1,0:T(8,128)(2,1)}, bf16[64,18432]{1,0:T(8,128)(2,1)}, bf16[128,18432]{1,0:T(8,128)(2,1)}) custom-call(bf16[16,18432]{1,0:T(8,128)(2,1)} %get-tuple-element.54.flat_0_, bf16[32,18432]{1,0:T(8,128)(2,1)} %norm.7.flat_1_, bf16[16,18432]{1,0:T(8,128)(2,1)} %get-tuple-element.55.flat_2_, ...), custom_call_target="tpu_custom_call" | custom-call | flops 32212254720 | bytes 132120576 | tf_op jit(solution)/shard_map/pallas_call | solution.py:289
  226.9 51.2 %shard_map.87 = (bf16[64,18432]{1,0:T(8,128)(2,1)}, bf16[64,18432]{1,0:T(8,128)(2,1)}, bf16[128,18432]{1,0:T(8,128)(2,1)}) custom-call(bf16[16,18432]{1,0:T(8,128)(2,1)} %norm.9.flat_0_, bf16[32,18432]{1,0:T(8,128)(2,1)} %copy-done.16, bf16[16,18432]{1,0:T(8,128)(2,1)} %collective-permute-done.21.flat_2_, bf16[16,18432]{1,0:T(8,128)(2,1)} %norm.10.flat_3_, ...), custom_call_target="tpu_custom_call" | custom-call | flops 32212254720 | bytes 132120576 | tf_op jit(solution)/shard_map/pallas_call | solution.py:289
  279.1 48.7 %collective-permute-done.34.flat_1_ = bf16[64,18432]{1,0:T(8,128)(2,1)} collective-permute-done((bf16[64,18432]{1,0:T(8,128)(2,1)}, bf16[64,18432]{1,0:T(8,128)(2,1)}, u32[]{:S(2)}, u32[]{:S(2)}) %collective-permute-start.34) | collective-permute-done | bytes 2359328 | tf_op jit(solution)/shard_map/ppermute | solution.py:396
  330.8 50.4 %shard_map.92 = (bf16[64,18432]{1,0:T(8,128)(2,1)}, bf16[64,18432]{1,0:T(8,128)(2,1)}, bf16[128,18432]{1,0:T(8,128)(2,1)}) custom-call(bf16[64,18432]{1,0:T(8,128)(2,1)} %collective-permute-done.62.flat_0_, bf16[64,18432]{1,0:T(8,128)(2,1)} %collective-permute-done.63.flat_1_, bf16[64,18432]{1,0:T(8,128)(2,1)} %collective-permute-done.64.flat_2_, ...), custom_call_target="tpu_custom_call" | custom-call | flops 32212254720 | bytes 132120576 | tf_op jit(solution)/shard_map/pallas_call | solution.py:289
  384.0 50.4 %shard_map.90 = (bf16[64,18432]{1,0:T(8,128)(2,1)}, bf16[64,18432]{1,0:T(8,128)(2,1)}, bf16[128,18432]{1,0:T(8,128)(2,1)}) custom-call(bf16[64,18432]{1,0:T(8,128)(2,1)} %collective-permute-done.43.flat_0_, bf16[64,18432]{1,0:T(8,128)(2,1)} %collective-permute-done.44.flat_1_, bf16[64,18432]{1,0:T(8,128)(2,1)} %collective-permute-done.45.flat_2_, ...), custom_call_target="tpu_custom_call" | custom-call | flops 32212254720 | bytes 132120576 | tf_op jit(solution)/shard_map/pallas_call | solution.py:289
  436.5 50.8 %shard_map.91 = (bf16[64,18432]{1,0:T(8,128)(2,1)}, bf16[64,18432]{1,0:T(8,128)(2,1)}, bf16[128,18432]{1,0:T(8,128)(2,1)}) custom-call(bf16[16,18432]{1,0:T(8,128)(2,1)} %norm.11.flat_0_, bf16[32,18432]{1,0:T(8,128)(2,1)} %collective-permute-done.50.flat_1_, bf16[16,18432]{1,0:T(8,128)(2,1)} %collective-permute-done.51.flat_2_, ...), custom_call_target="tpu_custom_call" | custom-call | flops 32212254720 | bytes 132120576 | tf_op jit(solution)/shard_map/pallas_call | solution.py:289
  487.9 50.3 %shard_map.93 = (bf16[64,18432]{1,0:T(8,128)(2,1)}, bf16[64,18432]{1,0:T(8,128)(2,1)}, bf16[128,18432]{1,0:T(8,128)(2,1)}) custom-call(bf16[64,18432]{1,0:T(8,128)(2,1)} %collective-permute-done.67.flat_0_, bf16[64,18432]{1,0:T(8,128)(2,1)} %collective-permute-done.68.flat_1_, bf16[64,18432]{1,0:T(8,128)(2,1)} %collective-permute-done.69.flat_2_, ...), custom_call_target="tpu_custom_call" | custom-call | flops 32212254720 | bytes 132120576 | tf_op jit(solution)/shard_map/pallas_call | solution.py:289
  539.3 50.4 %shard_map.88 = (bf16[64,18432]{1,0:T(8,128)(2,1)}, bf16[64,18432]{1,0:T(8,128)(2,1)}, bf16[128,18432]{1,0:T(8,128)(2,1)}) custom-call(bf16[64,18432]{1,0:T(8,128)(2,1)} %collective-permute-done.33.flat_0_, bf16[64,18432]{1,0:T(8,128)(2,1)} %collective-permute-done.34.flat_1_, bf16[64,18432]{1,0:T(8,128)(2,1)} %collective-permute-done.35.flat_2_, ...), custom_call_target="tpu_custom_call" | custom-call | flops 32212254720 | bytes 132120576 | tf_op jit(solution)/shard_map/pallas_call | solution.py:289
  590.2 3.8 sums.16
  594.0 6.1 sums.20
  602.7 6.1 sums.23
  611.2 3.8 sums.18
  615.0 6.1 sums.17
  621.1 33.4 %collective-permute-done.32.refs_2_ = bf16[64,18432]{1,0:T(8,128)(2,1)} collective-permute-done((bf16[64,18432]{1,0:T(8,128)(2,1)}, bf16[64,18432]{1,0:T(8,128)(2,1)}, u32[]{:S(2)}, u32[]{:S(2)}) %collective-permute-start.32) | collective-permute-done | bytes 2359328 | tf_op jit(solution)/shard_map/ppermute | solution.py:396
  655.1 50.0 %collective-permute-done.58.refs_2_ = bf16[64,18432]{1,0:T(8,128)(2,1)} collective-permute-done((bf16[64,18432]{1,0:T(8,128)(2,1)}, bf16[64,18432]{1,0:T(8,128)(2,1)}, u32[]{:S(2)}, u32[]{:S(2)}) %collective-permute-start.58) | collective-permute-done | bytes 2359328 | tf_op jit(solution)/shard_map/ppermute | solution.py:396
  706.7 7.6 sums.21
  714.4 41.2 %collective-permute-done.72.refs_2_ = bf16[64,18432]{1,0:T(8,128)(2,1)} collective-permute-done((bf16[64,18432]{1,0:T(8,128)(2,1)}, bf16[64,18432]{1,0:T(8,128)(2,1)}, u32[]{:S(2)}, u32[]{:S(2)}) %collective-permute-start.72) | collective-permute-done | bytes 2359328 | tf_op jit(solution)/shard_map/ppermute | solution.py:396
  757.3 4.6 sums.24
  763.3 42.9 %collective-permute-done.38.refs_4_ = bf16[64,18432]{1,0:T(8,128)(2,1)} collective-permute-done((bf16[64,18432]{1,0:T(8,128)(2,1)}, bf16[64,18432]{1,0:T(8,128)(2,1)}, u32[]{:S(2)}, u32[]{:S(2)}) %collective-permute-start.38) | collective-permute-done | bytes 2359328 | tf_op jit(solution)/shard_map/ppermute | solution.py:396
  807.2 3.0 sums.26
  810.9 84.3 %collective-permute-done.76.refs_1_ = bf16[16,18432]{1,0:T(8,128)(2,1)} collective-permute-done((bf16[16,18432]{1,0:T(8,128)(2,1)}, bf16[16,18432]{1,0:T(8,128)(2,1)}, u32[]{:S(2)}, u32[]{:S(2)}) %collective-permute-start.76) | collective-permute-done | bytes 589856 | tf_op jit(solution)/shard_map/ppermute | solution.py:396
  896.2 2.5 sums.30
  898.7 2.5 sums.28
  905.3 3.1 order.1
  908.3 13.5 %sums.19.refs_0_ = bf16[256,18432]{1,0:T(8,128)(2,1)} custom-call(bf16[64,18432]{1,0:T(8,128)(2,1)} %get-tuple-element.63.refs_0_, bf16[128,18432]{1,0:T(8,128)(2,1)} %collective-permute-done.18.refs_1_, bf16[64,18432]{1,0:T(8,128)(2,1)} %collective-permute-done.32.refs_2_, bf16[64,18432]{1,0:T(8,128)(2,1)} %get-tuple-element.67.refs_3_, ...), custom_call_target="tpu_custom_call" | custom-call | flops 14155776 | bytes 56623104 | tf_op jit(solution)/shard_map/sums/pallas_call | solution.py:359
  921.8 6.1 sums.22.refs_0_
  927.9 3.5 sums.25.refs_0_
  931.4 2.6 sums.27.refs_0_
  934.0 2.3 sums.29.refs_0_
  936.3 2.3 sums.31
  (201 shorter events, 55.8 us)
Async XLA Ops:
  51.5 68.1 %collective-permute-start.39 = (bf16[64,18432]{1,0:T(8,128)(2,1)S(1)}, bf16[64,18432]{1,0:T(8,128)(2,1)}, u32[]{:S(2)}, u32[]{:S(2)}) collective-permute-start(bf16[64,18432]{1,0:T(8,128)(2,1)S(1)} %copy-done.7), channel_id=1, source_target_pairs={{0,1},{1,0},{2,3},{3,2},{4,5},{5,4},{6,7},{7,6}} | collective-permute-start | bytes 7077896 | tf_op jit(solution)/shard_map/ppermute | solution.py:396
  51.6 68.3 %collective-permute-start.40 = (bf16[64,18432]{1,0:T(8,128)(2,1)}, bf16[64,18432]{1,0:T(8,128)(2,1)}, u32[]{:S(2)}, u32[]{:S(2)}) collective-permute-start(bf16[64,18432]{1,0:T(8,128)(2,1)} %get-tuple-element.58.flat_5_.flat_1_), channel_id=1, source_target_pairs={{0,1},{1,0},{2,3},{3,2},{4,5},{5,4},{6,7},{7,6}} | collective-permute-start | bytes 7077896 | tf_op jit(solution)/shard_map/ppermute | solution.py:396
  117.8 52.7 %collective-permute-start.23 = (bf16[32,18432]{1,0:T(8,128)(2,1)}, bf16[32,18432]{1,0:T(8,128)(2,1)}, u32[]{:S(2)}, u32[]{:S(2)}) collective-permute-start(bf16[32,18432]{1,0:T(8,128)(2,1)} %norm.7.flat_1_), channel_id=1, source_target_pairs={{0,4},{1,5},{2,6},{3,7},{4,0},{5,1},{6,2},{7,3}} | collective-permute-start | bytes 3538952 | tf_op jit(solution)/shard_map/ppermute | solution.py:396
  119.1 53.6 %collective-permute-start.3 = (bf16[64,18432]{1,0:T(8,128)(2,1)}, bf16[64,18432]{1,0:T(8,128)(2,1)}, u32[]{:S(2)}, u32[]{:S(2)}) collective-permute-start(bf16[64,18432]{1,0:T(8,128)(2,1)} %get-tuple-element.56.flat_3_), channel_id=1, source_target_pairs={{0,1},{1,0},{2,3},{3,2},{4,5},{5,4},{6,7},{7,6}} | collective-permute-start | bytes 7077896 | tf_op jit(solution)/shard_map/ppermute | solution.py:396
  119.3 52.8 %collective-permute-start.1 = (bf16[32,18432]{1,0:T(8,128)(2,1)}, bf16[32,18432]{1,0:T(8,128)(2,1)}, u32[]{:S(2)}, u32[]{:S(2)}) collective-permute-start(bf16[32,18432]{1,0:T(8,128)(2,1)} %norm.7.flat_1_), channel_id=1, source_target_pairs={{0,1},{1,0},{2,3},{3,2},{4,5},{5,4},{6,7},{7,6}} | collective-permute-start | bytes 3538952 | tf_op jit(solution)/shard_map/ppermute | solution.py:396
  119.6 51.9 %collective-permute-start.25 = (bf16[16,18432]{1,0:T(8,128)(2,1)}, bf16[16,18432]{1,0:T(8,128)(2,1)}, u32[]{:S(2)}, u32[]{:S(2)}) collective-permute-start(bf16[16,18432]{1,0:T(8,128)(2,1)} %norm.9.flat_0_), channel_id=1, source_target_pairs={{0,1},{1,0},{2,3},{3,2},{4,5},{5,4},{6,7},{7,6}} | collective-permute-start | bytes 1769480 | tf_op jit(solution)/shard_map/ppermute | solution.py:396
  119.8 52.3 %collective-permute-start.28 = (bf16[16,18432]{1,0:T(8,128)(2,1)}, bf16[16,18432]{1,0:T(8,128)(2,1)}, u32[]{:S(2)}, u32[]{:S(2)}) collective-permute-start(bf16[16,18432]{1,0:T(8,128)(2,1)} %norm.10.flat_3_), channel_id=1, source_target_pairs={{0,1},{1,0},{2,3},{3,2},{4,5},{5,4},{6,7},{7,6}} | collective-permute-start | bytes 1769480 | tf_op jit(solution)/shard_map/ppermute | solution.py:396
  170.5 54.3 %collective-permute-start.62 = (bf16[64,18432]{1,0:T(8,128)(2,1)}, bf16[64,18432]{1,0:T(8,128)(2,1)}, u32[]{:S(2)}, u32[]{:S(2)}) collective-permute-start(bf16[64,18432]{1,0:T(8,128)(2,1)} %get-tuple-element.58.flat_5_.flat_1_), channel_id=1, source_target_pairs={{0,2},{1,3},{2,0},{3,1},{4,6},{5,7},{6,4},{7,5}} | collective-permute-start | bytes 7077896 | tf_op jit(solution)/shard_map/ppermute | solution.py:396
  171.6 53.8 %collective-permute-start.63 = (bf16[64,18432]{1,0:T(8,128)(2,1)}, bf16[64,18432]{1,0:T(8,128)(2,1)}, u32[]{:S(2)}, u32[]{:S(2)}) collective-permute-start(bf16[64,18432]{1,0:T(8,128)(2,1)} %get-tuple-element.56.flat_3_), channel_id=1, source_target_pairs={{0,4},{1,5},{2,6},{3,7},{4,0},{5,1},{6,2},{7,3}} | collective-permute-start | bytes 7077896 | tf_op jit(solution)/shard_map/ppermute | solution.py:396
  172.2 54.3 %collective-permute-start.26 = (bf16[32,18432]{1,0:T(8,128)(2,1)}, bf16[32,18432]{1,0:T(8,128)(2,1)}, u32[]{:S(2)}, u32[]{:S(2)}) collective-permute-start(bf16[32,18432]{1,0:T(8,128)(2,1)} %copy-done.16), channel_id=1, source_target_pairs={{0,1},{1,0},{2,3},{3,2},{4,5},{5,4},{6,7},{7,6}} | collective-permute-start | bytes 3538952 | tf_op jit(solution)/shard_map/ppermute | solution.py:396
  172.7 53.8 %collective-permute-start.29 = (bf16[32,18432]{1,0:T(8,128)(2,1)}, bf16[32,18432]{1,0:T(8,128)(2,1)}, u32[]{:S(2)}, u32[]{:S(2)}) collective-permute-start(bf16[32,18432]{1,0:T(8,128)(2,1)} %collective-permute-done.23.flat_4_), channel_id=1, source_target_pairs={{0,1},{1,0},{2,3},{3,2},{4,5},{5,4},{6,7},{7,6}} | collective-permute-start | bytes 3538952 | tf_op jit(solution)/shard_map/ppermute | solution.py:396
  223.3 54.8 %collective-permute-start.44 = (bf16[64,18432]{1,0:T(8,128)(2,1)}, bf16[64,18432]{1,0:T(8,128)(2,1)}, u32[]{:S(2)}, u32[]{:S(2)}) collective-permute-start(bf16[64,18432]{1,0:T(8,128)(2,1)} %get-tuple-element.58.flat_5_.flat_1_), channel_id=1, source_target_pairs={{0,4},{1,5},{2,6},{3,7},{4,0},{5,1},{6,2},{7,3}} | collective-permute-start | bytes 7077896 | tf_op jit(solution)/shard_map/ppermute | solution.py:396
  224.7 103.1 %collective-permute-start.34 = (bf16[64,18432]{1,0:T(8,128)(2,1)}, bf16[64,18432]{1,0:T(8,128)(2,1)}, u32[]{:S(2)}, u32[]{:S(2)}) collective-permute-start(bf16[64,18432]{1,0:T(8,128)(2,1)} %get-tuple-element.57.flat_4_.flat_0_), channel_id=1, source_target_pairs={{0,4},{1,5},{2,6},{3,7},{4,0},{5,1},{6,2},{7,3}} | collective-permute-start | bytes 7077896 | tf_op jit(solution)/shard_map/ppermute | solution.py:396
  225.3 103.9 %collective-permute-start.43 = (bf16[64,18432]{1,0:T(8,128)(2,1)}, bf16[64,18432]{1,0:T(8,128)(2,1)}, u32[]{:S(2)}, u32[]{:S(2)}) collective-permute-start(bf16[64,18432]{1,0:T(8,128)(2,1)} %get-tuple-element.57.flat_4_.flat_0_), channel_id=1, source_target_pairs={{0,2},{1,3},{2,0},{3,1},{4,6},{5,7},{6,4},{7,5}} | collective-permute-start | bytes 7077896 | tf_op jit(solution)/shard_map/ppermute | solution.py:396
  226.4 103.8 %collective-permute-start.64 = (bf16[64,18432]{1,0:T(8,128)(2,1)}, bf16[64,18432]{1,0:T(8,128)(2,1)}, u32[]{:S(2)}, u32[]{:S(2)}) collective-permute-start(bf16[64,18432]{1,0:T(8,128)(2,1)} %collective-permute-done.62.flat_0_), channel_id=1, source_target_pairs={{0,1},{1,0},{2,3},{3,2},{4,5},{5,4},{6,7},{7,6}} | collective-permute-start | bytes 7077896 | tf_op jit(solution)/shard_map/ppermute | solution.py:396
  226.4 103.8 %collective-permute-start.65 = (bf16[64,18432]{1,0:T(8,128)(2,1)}, bf16[64,18432]{1,0:T(8,128)(2,1)}, u32[]{:S(2)}, u32[]{:S(2)}) collective-permute-start(bf16[64,18432]{1,0:T(8,128)(2,1)} %collective-permute-done.63.flat_1_), channel_id=1, source_target_pairs={{0,1},{1,0},{2,3},{3,2},{4,5},{5,4},{6,7},{7,6}} | collective-permute-start | bytes 7077896 | tf_op jit(solution)/shard_map/ppermute | solution.py:396
  278.1 103.0 %collective-permute-start.33 = (bf16[64,18432]{1,0:T(8,128)(2,1)}, bf16[64,18432]{1,0:T(8,128)(2,1)}, u32[]{:S(2)}, u32[]{:S(2)}) collective-permute-start(bf16[64,18432]{1,0:T(8,128)(2,1)} %get-tuple-element.56.flat_3_), channel_id=1, source_target_pairs={{0,2},{1,3},{2,0},{3,1},{4,6},{5,7},{6,4},{7,5}} | collective-permute-start | bytes 7077896 | tf_op jit(solution)/shard_map/ppermute | solution.py:396
  327.8 53.4 %collective-permute-start.50 = (bf16[32,18432]{1,0:T(8,128)(2,1)}, bf16[32,18432]{1,0:T(8,128)(2,1)}, u32[]{:S(2)}, u32[]{:S(2)}) collective-permute-start(bf16[32,18432]{1,0:T(8,128)(2,1)} %copy-done.16), channel_id=1, source_target_pairs={{0,4},{1,5},{2,6},{3,7},{4,0},{5,1},{6,2},{7,3}} | collective-permute-start | bytes 3538952 | tf_op jit(solution)/shard_map/ppermute | solution.py:396
  329.3 53.0 %collective-permute-start.52 = (bf16[64,18432]{1,0:T(8,128)(2,1)}, bf16[64,18432]{1,0:T(8,128)(2,1)}, u32[]{:S(2)}, u32[]{:S(2)}) collective-permute-start(bf16[64,18432]{1,0:T(8,128)(2,1)} %collective-permute-done.34.flat_1_), channel_id=1, source_target_pairs={{0,2},{1,3},{2,0},{3,1},{4,6},{5,7},{6,4},{7,5}} | collective-permute-start | bytes 7077896 | tf_op jit(solution)/shard_map/ppermute | solution.py:396
  330.2 53.3 %collective-permute-start.46 = (bf16[64,18432]{1,0:T(8,128)(2,1)}, bf16[64,18432]{1,0:T(8,128)(2,1)}, u32[]{:S(2)}, u32[]{:S(2)}) collective-permute-start(bf16[64,18432]{1,0:T(8,128)(2,1)} %collective-permute-done.44.flat_1_), channel_id=1, source_target_pairs={{0,1},{1,0},{2,3},{3,2},{4,5},{5,4},{6,7},{7,6}} | collective-permute-start | bytes 7077896 | tf_op jit(solution)/shard_map/ppermute | solution.py:396
  330.2 53.3 %collective-permute-start.45 = (bf16[64,18432]{1,0:T(8,128)(2,1)}, bf16[64,18432]{1,0:T(8,128)(2,1)}, u32[]{:S(2)}, u32[]{:S(2)}) collective-permute-start(bf16[64,18432]{1,0:T(8,128)(2,1)} %collective-permute-done.43.flat_0_), channel_id=1, source_target_pairs={{0,1},{1,0},{2,3},{3,2},{4,5},{5,4},{6,7},{7,6}} | collective-permute-start | bytes 7077896 | tf_op jit(solution)/shard_map/ppermute | solution.py:396
  381.2 53.3 %collective-permute-start.53 = (bf16[16,18432]{1,0:T(8,128)(2,1)}, bf16[16,18432]{1,0:T(8,128)(2,1)}, u32[]{:S(2)}, u32[]{:S(2)}) collective-permute-start(bf16[16,18432]{1,0:T(8,128)(2,1)} %norm.11.flat_0_), channel_id=1, source_target_pairs={{0,1},{1,0},{2,3},{3,2},{4,5},{5,4},{6,7},{7,6}} | collective-permute-start | bytes 1769480 | tf_op jit(solution)/shard_map/ppermute | solution.py:396
  381.2 54.7 %collective-permute-start.68 = (bf16[64,18432]{1,0:T(8,128)(2,1)}, bf16[64,18432]{1,0:T(8,128)(2,1)}, u32[]{:S(2)}, u32[]{:S(2)}) collective-permute-start(bf16[64,18432]{1,0:T(8,128)(2,1)} %collective-permute-done.44.flat_1_), channel_id=1, source_target_pairs={{0,2},{1,3},{2,0},{3,1},{4,6},{5,7},{6,4},{7,5}} | collective-permute-start | bytes 7077896 | tf_op jit(solution)/shard_map/ppermute | solution.py:396
  382.3 53.7 %collective-permute-start.67 = (bf16[64,18432]{1,0:T(8,128)(2,1)}, bf16[64,18432]{1,0:T(8,128)(2,1)}, u32[]{:S(2)}, u32[]{:S(2)}) collective-permute-start(bf16[64,18432]{1,0:T(8,128)(2,1)} %collective-permute-done.33.flat_0_), channel_id=1, source_target_pairs={{0,4},{1,5},{2,6},{3,7},{4,0},{5,1},{6,2},{7,3}} | collective-permute-start | bytes 7077896 | tf_op jit(solution)/shard_map/ppermute | solution.py:396
  383.5 52.9 %collective-permute-start.56 = (bf16[64,18432]{1,0:T(8,128)(2,1)}, bf16[64,18432]{1,0:T(8,128)(2,1)}, u32[]{:S(2)}, u32[]{:S(2)}) collective-permute-start(bf16[64,18432]{1,0:T(8,128)(2,1)} %collective-permute-done.52.flat_3_), channel_id=1, source_target_pairs={{0,1},{1,0},{2,3},{3,2},{4,5},{5,4},{6,7},{7,6}} | collective-permute-start | bytes 7077896 | tf_op jit(solution)/shard_map/ppermute | solution.py:396
  434.4 104.4 %collective-permute-start.31 = (bf16[128,18432]{1,0:T(8,128)(2,1)}, bf16[128,18432]{1,0:T(8,128)(2,1)}, u32[]{:S(2)}, u32[]{:S(2)}) collective-permute-start(bf16[128,18432]{1,0:T(8,128)(2,1)} %get-tuple-element.66), channel_id=1, source_target_pairs={{0,1},{1,0},{2,3},{3,2},{4,5},{5,4},{6,7},{7,6}} | collective-permute-start | bytes 14155784 | tf_op jit(solution)/shard_map/ppermute | solution.py:396
  434.5 155.2 %collective-permute-start.41 = (bf16[128,18432]{1,0:T(8,128)(2,1)}, bf16[128,18432]{1,0:T(8,128)(2,1)}, u32[]{:S(2)}, u32[]{:S(2)}) collective-permute-start(bf16[128,18432]{1,0:T(8,128)(2,1)} %get-tuple-element.73), channel_id=1, source_target_pairs={{0,1},{1,0},{2,3},{3,2},{4,5},{5,4},{6,7},{7,6}} | collective-permute-start | bytes 14155784 | tf_op jit(solution)/shard_map/ppermute | solution.py:396
  435.9 102.3 %collective-permute-start.35 = (bf16[64,18432]{1,0:T(8,128)(2,1)}, bf16[64,18432]{1,0:T(8,128)(2,1)}, u32[]{:S(2)}, u32[]{:S(2)}) collective-permute-start(bf16[64,18432]{1,0:T(8,128)(2,1)} %collective-permute-done.33.flat_0_), channel_id=1, source_target_pairs={{0,1},{1,0},{2,3},{3,2},{4,5},{5,4},{6,7},{7,6}} | collective-permute-start | bytes 7077896 | tf_op jit(solution)/shard_map/ppermute | solution.py:396
  435.9 51.4 %collective-permute-start.69 = (bf16[64,18432]{1,0:T(8,128)(2,1)}, bf16[64,18432]{1,0:T(8,128)(2,1)}, u32[]{:S(2)}, u32[]{:S(2)}) collective-permute-start(bf16[64,18432]{1,0:T(8,128)(2,1)} %collective-permute-done.67.flat_0_), channel_id=1, source_target_pairs={{0,1},{1,0},{2,3},{3,2},{4,5},{5,4},{6,7},{7,6}} | collective-permute-start | bytes 7077896 | tf_op jit(solution)/shard_map/ppermute | solution.py:396
  436.5 51.4 %collective-permute-start.70 = (bf16[64,18432]{1,0:T(8,128)(2,1)}, bf16[64,18432]{1,0:T(8,128)(2,1)}, u32[]{:S(2)}, u32[]{:S(2)}) collective-permute-start(bf16[64,18432]{1,0:T(8,128)(2,1)} %collective-permute-done.68.flat_1_), channel_id=1, source_target_pairs={{0,1},{1,0},{2,3},{3,2},{4,5},{5,4},{6,7},{7,6}} | collective-permute-start | bytes 7077896 | tf_op jit(solution)/shard_map/ppermute | solution.py:396
  487.3 51.4 %collective-permute-start.36 = (bf16[64,18432]{1,0:T(8,128)(2,1)}, bf16[64,18432]{1,0:T(8,128)(2,1)}, u32[]{:S(2)}, u32[]{:S(2)}) collective-permute-start(bf16[64,18432]{1,0:T(8,128)(2,1)} %collective-permute-done.34.flat_1_), channel_id=1, source_target_pairs={{0,1},{1,0},{2,3},{3,2},{4,5},{5,4},{6,7},{7,6}} | collective-permute-start | bytes 7077896 | tf_op jit(solution)/shard_map/ppermute | solution.py:396
  487.9 101.9 %collective-permute-start.57 = (bf16[128,18432]{1,0:T(8,128)(2,1)}, bf16[128,18432]{1,0:T(8,128)(2,1)}, u32[]{:S(2)}, u32[]{:S(2)}) collective-permute-start(bf16[128,18432]{1,0:T(8,128)(2,1)} %get-tuple-element.80), channel_id=1, source_target_pairs={{0,1},{1,0},{2,3},{3,2},{4,5},{5,4},{6,7},{7,6}} | collective-permute-start | bytes 14155784 | tf_op jit(solution)/shard_map/ppermute | solution.py:396
  538.3 61.8 %collective-permute-start.18 = (bf16[128,18432]{1,0:T(8,128)(2,1)}, bf16[128,18432]{1,0:T(8,128)(2,1)}, u32[]{:S(2)}, u32[]{:S(2)}) collective-permute-start(bf16[128,18432]{1,0:T(8,128)(2,1)} %get-tuple-element.64), channel_id=1, source_target_pairs={{0,1},{1,0},{2,3},{3,2},{4,5},{5,4},{6,7},{7,6}} | collective-permute-start | bytes 14155784 | tf_op jit(solution)/shard_map/ppermute | solution.py:396
  538.7 62.3 %collective-permute-start.66 = (bf16[128,18432]{1,0:T(8,128)(2,1)}, bf16[128,18432]{1,0:T(8,128)(2,1)}, u32[]{:S(2)}, u32[]{:S(2)}) collective-permute-start(bf16[128,18432]{1,0:T(8,128)(2,1)} %get-tuple-element.88), channel_id=1, source_target_pairs={{0,1},{1,0},{2,3},{3,2},{4,5},{5,4},{6,7},{7,6}} | collective-permute-start | bytes 14155784 | tf_op jit(solution)/shard_map/ppermute | solution.py:396
  538.8 63.3 %collective-permute-start.71 = (bf16[128,18432]{1,0:T(8,128)(2,1)}, bf16[128,18432]{1,0:T(8,128)(2,1)}, u32[]{:S(2)}, u32[]{:S(2)}) collective-permute-start(bf16[128,18432]{1,0:T(8,128)(2,1)} %get-tuple-element.90), channel_id=1, source_target_pairs={{0,1},{1,0},{2,3},{3,2},{4,5},{5,4},{6,7},{7,6}} | collective-permute-start | bytes 14155784 | tf_op jit(solution)/shard_map/ppermute | solution.py:396
  600.0 54.5 %collective-permute-start.32 = (bf16[64,18432]{1,0:T(8,128)(2,1)}, bf16[64,18432]{1,0:T(8,128)(2,1)}, u32[]{:S(2)}, u32[]{:S(2)}) collective-permute-start(bf16[64,18432]{1,0:T(8,128)(2,1)} %sums.16), channel_id=1, source_target_pairs={{0,2},{1,3},{2,0},{3,1},{4,6},{5,7},{6,4},{7,5}} | collective-permute-start | bytes 7077896 | tf_op jit(solution)/shard_map/ppermute | solution.py:396
  601.0 104.0 %collective-permute-start.58 = (bf16[64,18432]{1,0:T(8,128)(2,1)}, bf16[64,18432]{1,0:T(8,128)(2,1)}, u32[]{:S(2)}, u32[]{:S(2)}) collective-permute-start(bf16[64,18432]{1,0:T(8,128)(2,1)} %get-tuple-element.82), channel_id=1, source_target_pairs={{0,2},{1,3},{2,0},{3,1},{4,6},{5,7},{6,4},{7,5}} | collective-permute-start | bytes 7077896 | tf_op jit(solution)/shard_map/ppermute | solution.py:396
  602.1 103.9 %collective-permute-start.59 = (bf16[64,18432]{1,0:T(8,128)(2,1)}, bf16[64,18432]{1,0:T(8,128)(2,1)}, u32[]{:S(2)}, u32[]{:S(2)}) collective-permute-start(bf16[64,18432]{1,0:T(8,128)(2,1)} %get-tuple-element.84), channel_id=1, source_target_pairs={{0,4},{1,5},{2,6},{3,7},{4,0},{5,1},{6,2},{7,3}} | collective-permute-start | bytes 7077896 | tf_op jit(solution)/shard_map/ppermute | solution.py:396
  608.8 146.8 %collective-permute-start.72 = (bf16[64,18432]{1,0:T(8,128)(2,1)}, bf16[64,18432]{1,0:T(8,128)(2,1)}, u32[]{:S(2)}, u32[]{:S(2)}) collective-permute-start(bf16[64,18432]{1,0:T(8,128)(2,1)} %get-tuple-element.92), channel_id=1, source_target_pairs={{0,2},{1,3},{2,0},{3,1},{4,6},{5,7},{6,4},{7,5}} | collective-permute-start | bytes 7077896 | tf_op jit(solution)/shard_map/ppermute | solution.py:396
  609.9 146.3 %collective-permute-start.73 = (bf16[64,18432]{1,0:T(8,128)(2,1)}, bf16[64,18432]{1,0:T(8,128)(2,1)}, u32[]{:S(2)}, u32[]{:S(2)}) collective-permute-start(bf16[64,18432]{1,0:T(8,128)(2,1)} %get-tuple-element.94), channel_id=1, source_target_pairs={{0,4},{1,5},{2,6},{3,7},{4,0},{5,1},{6,2},{7,3}} | collective-permute-start | bytes 7077896 | tf_op jit(solution)/shard_map/ppermute | solution.py:396
  654.5 107.5 %collective-permute-start.48 = (bf16[64,18432]{1,0:T(8,128)(2,1)}, bf16[64,18432]{1,0:T(8,128)(2,1)}, u32[]{:S(2)}, u32[]{:S(2)}) collective-permute-start(bf16[64,18432]{1,0:T(8,128)(2,1)} %sums.18), channel_id=1, source_target_pairs={{0,4},{1,5},{2,6},{3,7},{4,0},{5,1},{6,2},{7,3}} | collective-permute-start | bytes 7077896 | tf_op jit(solution)/shard_map/ppermute | solution.py:396
  705.1 101.1 %collective-permute-start.38 = (bf16[64,18432]{1,0:T(8,128)(2,1)}, bf16[64,18432]{1,0:T(8,128)(2,1)}, u32[]{:S(2)}, u32[]{:S(2)}) collective-permute-start(bf16[64,18432]{1,0:T(8,128)(2,1)} %get-tuple-element.71), channel_id=1, source_target_pairs={{0,2},{1,3},{2,0},{3,1},{4,6},{5,7},{6,4},{7,5}} | collective-permute-start | bytes 7077896 | tf_op jit(solution)/shard_map/ppermute | solution.py:396
  706.0 104.1 %collective-permute-start.42 = (bf16[64,18432]{1,0:T(8,128)(2,1)}, bf16[64,18432]{1,0:T(8,128)(2,1)}, u32[]{:S(2)}, u32[]{:S(2)}) collective-permute-start(bf16[64,18432]{1,0:T(8,128)(2,1)} %get-tuple-element.74), channel_id=1, source_target_pairs={{0,4},{1,5},{2,6},{3,7},{4,0},{5,1},{6,2},{7,3}} | collective-permute-start | bytes 7077896 | tf_op jit(solution)/shard_map/ppermute | solution.py:396
  755.6 147.2 %collective-permute-start.60 = (bf16[64,18432]{1,0:T(8,128)(2,1)}, bf16[64,18432]{1,0:T(8,128)(2,1)}, u32[]{:S(2)}, u32[]{:S(2)}) collective-permute-start(bf16[64,18432]{1,0:T(8,128)(2,1)} %get-tuple-element.85), channel_id=1, source_target_pairs={{0,4},{1,5},{2,6},{3,7},{4,0},{5,1},{6,2},{7,3}} | collective-permute-start | bytes 7077896 | tf_op jit(solution)/shard_map/ppermute | solution.py:396
  756.2 148.1 %collective-permute-start.61 = (bf16[64,18432]{1,0:T(8,128)(2,1)}, bf16[64,18432]{1,0:T(8,128)(2,1)}, u32[]{:S(2)}, u32[]{:S(2)}) collective-permute-start(bf16[64,18432]{1,0:T(8,128)(2,1)} %get-tuple-element.86), channel_id=1, source_target_pairs={{0,2},{1,3},{2,0},{3,1},{4,6},{5,7},{6,4},{7,5}} | collective-permute-start | bytes 7077896 | tf_op jit(solution)/shard_map/ppermute | solution.py:396
  762.0 139.2 %collective-permute-start.74 = (bf16[32,18432]{1,0:T(8,128)(2,1)}, bf16[32,18432]{1,0:T(8,128)(2,1)}, u32[]{:S(2)}, u32[]{:S(2)}) collective-permute-start(bf16[32,18432]{1,0:T(8,128)(2,1)} %get-tuple-element.95), channel_id=1, source_target_pairs={{0,4},{1,5},{2,6},{3,7},{4,0},{5,1},{6,2},{7,3}} | collective-permute-start | bytes 3538952 | tf_op jit(solution)/shard_map/ppermute | solution.py:396
  806.2 95.7 %collective-permute-start.75 = (bf16[32,18432]{1,0:T(8,128)(2,1)}, bf16[32,18432]{1,0:T(8,128)(2,1)}, u32[]{:S(2)}, u32[]{:S(2)}) collective-permute-start(bf16[32,18432]{1,0:T(8,128)(2,1)} %get-tuple-element.96), channel_id=1, source_target_pairs={{0,2},{1,3},{2,0},{3,1},{4,6},{5,7},{6,4},{7,5}} | collective-permute-start | bytes 3538952 | tf_op jit(solution)/shard_map/ppermute | solution.py:396
  810.2 85.0 %collective-permute-start.76 = (bf16[16,18432]{1,0:T(8,128)(2,1)}, bf16[16,18432]{1,0:T(8,128)(2,1)}, u32[]{:S(2)}, u32[]{:S(2)}) collective-permute-start(bf16[16,18432]{1,0:T(8,128)(2,1)} %get-tuple-element.97), channel_id=1, source_target_pairs={{0,4},{1,5},{2,6},{3,7},{4,0},{5,1},{6,2},{7,3}} | collective-permute-start | bytes 1769480 | tf_op jit(solution)/shard_map/ppermute | solution.py:396
  (55 other events, 932.0 us)

commit v3 on v2

--- a/solution.py
+++ b/solution.py
@@ -89,31 +89,26 @@
     )(x, gain)
 
 
-def _order_kernel(n, *refs):
+def _order_kernel(moves, per, *refs):
     me = lax.axis_index(AXIS)
-    k_out, v_out = refs[2 * n:]
-    for m, (top, rest) in enumerate(zip(refs[:n], refs[n:2 * n])):
-        high, rows = top.shape[0], (top.shape[0] + rest.shape[0]) // 2
-        first = pl.multiple_of((me ^ m) * rows, rows)
-        k_out[pl.ds(first, high), :] = top[...]
-        k_out[pl.ds(pl.multiple_of(first + high, 16), rows - high), :] = rest[rows:, :]
-        v_out[pl.ds(first, rows), :] = rest[:rows, :]
-
-
-def order_blocks(tops, rests):
-    n, cols = len(tops), tops[0].shape[1]
-    rows = (tops[0].shape[0] + rests[0].shape[0]) // 2
+    for src, first, n, which, m, row in moves:
+        to = pl.multiple_of((me ^ m) * per + row, 16)
+        refs[which - 2][pl.ds(to, n), :] = refs[src][first:first + n, :]
+
+
+def order_blocks(sources, moves, per, total):
+    cols = sources[0].shape[1]
     return pl.pallas_call(
-        functools.partial(_order_kernel, n),
-        in_specs=[pl.BlockSpec(memory_space=pltpu.VMEM)] * (2 * n),
+        functools.partial(_order_kernel, moves, per),
+        in_specs=[pl.BlockSpec(memory_space=pltpu.VMEM)] * len(sources),
         out_specs=[pl.BlockSpec(memory_space=pltpu.VMEM)] * 2,
-        out_shape=[jax.ShapeDtypeStruct((rows * n, cols), BF16)] * 2,
-        cost_estimate=pl.CostEstimate(flops=2 * rows * n * cols, bytes_accessed=8 * rows * n * cols, transcendentals=0),
+        out_shape=[jax.ShapeDtypeStruct((total, cols), BF16)] * 2,
+        cost_estimate=pl.CostEstimate(flops=2 * total * cols, bytes_accessed=8 * total * cols, transcendentals=0),
         name="order",
-    )(*tops, *rests)
-
-
-def _unit_kernel(names, parts, n_lhs, n_out, index, *flat):
+    )(*sources)
+
+
+def _unit_kernel(names, parts, n_lhs, n_out, index, moves, picks, *flat):
     r = dict(zip(names, flat))
     lhs = [r[f"lhs{i}"] for i in range(n_lhs)]
     outs = [r[f"out{i}"] for i in range(n_out)]
@@ -171,15 +166,16 @@
             wo_copy(i, i).start()
     extra = []
     if do_o:
-        row, col = (lax.broadcasted_iota(jnp.int32, (rows, rows), d) for d in (0, 1))
-        mine = jnp.where(row == col, r["qpos"][index:index + 1, :], 0.0)
-        r["q_col"][...] = jnp.sum(mine, axis=1, keepdims=True)
-        for m in range(r["kv_sem"].shape[0]):
-            top, rest = r[f"k{m}"], r[f"v{m}"]
-            high, n = top.shape[0], (top.shape[0] + rest.shape[0]) // 2
-            moves = ((top, 0, high, "k_buf", 0), (rest, n, n - high, "k_buf", high), (rest, 0, n, "v_buf", 0))
-            for j, (src, first, count, buf, to) in enumerate(moves):
-                extra.append(pltpu.make_async_copy(src.at[pl.ds(first, count), :], r[buf].at[pl.ds(m * n + to, count), :], r["kv_sem"].at[m, j]))
+        block = r["qpos"].shape[1]
+        row, col = (lax.broadcasted_iota(jnp.int32, (block, block), d) for d in (0, 1))
+        for i in range(rows // block):
+            mine = jnp.where(row == col, r["qpos"][index + i:index + i + 1, :], 0.0)
+            r["q_col"][pl.ds(i * block, block), :] = jnp.sum(mine, axis=1, keepdims=True)
+        for i, (src, first, n, which, at_row) in enumerate(moves):
+            buf = r["v_buf"] if which else r["k_buf"]
+            extra.append(pltpu.make_async_copy(r[f"s{src}"].at[pl.ds(first, n), :], buf.at[pl.ds(at_row, n), :], r["kv_sem"].at[i]))
+        if not do_q:
+            extra.append(pltpu.make_async_copy(lhs[0], q_buf, r["kv_sem"].at[len(moves)]))
     for c in extra:
         c.start()
 
@@ -198,10 +194,9 @@
 
         lax.fori_loop(0, n_q, q_step, 0)
         if not do_o:
-            high, cols = outs[0].shape
-            outs[0][...] = acc[:high, :cols].astype(BF16)
-            outs[1][:rows, :] = acc[:, cols:].astype(BF16)
-            outs[1][rows:, :] = acc[high:, :cols].astype(BF16)
+            for out, to, first, n, left in picks:
+                cols = outs[out].shape[1]
+                outs[out][pl.ds(to, n), :] = acc[pl.ds(first, n), left:left + cols].astype(BF16)
             return
         q_buf[...] = acc[...].astype(BF16)
 
@@ -255,14 +250,14 @@
             c.wait()
 
 
-def unit_call(lhs, wq, wo, keys, values, qpos, kpos, index, splits, slots=7, chunk=None):
+def unit_call(lhs, wq, wo, keys, qpos, kpos, index, splits, picks=(), slots=7, chunk=None):
     parts = ("q" if wq is not None else "") + ("o" if wo is not None else "")
     rows = sum(h.shape[0] for h in lhs)
-    proj = wq.shape[1]
-    width = wq.shape[0]
+    proj, width = (wq.shape[1], wq.shape[0]) if wq is not None else wo.shape
     chunk = chunk or proj
     any_ = pl.BlockSpec(memory_space=pl.ANY)
     ins = [(f"lhs{i}", h, any_) for i, h in enumerate(lhs)]
+    moves = ()
     scratch = [("ring", pltpu.VMEM((slots, chunk, proj), BF16)), ("ring_sem", pltpu.SemaphoreType.DMA((slots,))), ("q_buf", pltpu.VMEM((rows, proj), BF16))]
     flops, moved = 0, 0
     if wq is not None:
@@ -271,23 +266,26 @@
         flops += 2 * rows * proj * width
         moved += 2 * (rows + proj) * width
     if wo is not None:
-        n_keys, head = kpos.shape[1], keys[0].shape[1]
+        sources, at = keys
+        n_keys, head = kpos.shape[1], sources[0].shape[1]
+        per = n_keys // (1 + max(m for _, _, _, _, m, _ in at))
+        moves = tuple((src, first, n, which, m * per + row) for src, first, n, which, m, row in at)
         ins.append(("wo", wo, any_))
-        ins += [(f"k{m}", k, any_) for m, k in enumerate(keys)] + [(f"v{m}", v, any_) for m, v in enumerate(values)]
+        ins += [(f"s{i}", a, any_) for i, a in enumerate(sources)]
         ins += [("qpos", qpos, pl.BlockSpec(qpos.shape, lambda i: (0, 0))), ("kpos", kpos, pl.BlockSpec((1, n_keys), lambda i: (0, 0)))]
         scratch += [
             ("o_buf", pltpu.VMEM((rows, proj), BF16)), ("y_buf", pltpu.VMEM((2, rows, chunk), BF16)), ("y_sem", pltpu.SemaphoreType.DMA((2, len(splits)))),
             ("q_col", pltpu.VMEM((rows, 1), F32)), ("s_a", pltpu.VMEM((rows // 2, n_keys), F32)), ("s_b", pltpu.VMEM((rows // 2, n_keys), F32)),
-            ("k_buf", pltpu.VMEM((n_keys, head), BF16)), ("v_buf", pltpu.VMEM((n_keys, head), BF16)), ("kv_sem", pltpu.SemaphoreType.DMA((len(keys), 3))),
+            ("k_buf", pltpu.VMEM((n_keys, head), BF16)), ("v_buf", pltpu.VMEM((n_keys, head), BF16)), ("kv_sem", pltpu.SemaphoreType.DMA((len(moves) + 1,))),
         ]
         flops += 2 * rows * proj * (width + 2 * n_keys)
         moved += 2 * (rows + proj) * width
         outs = [((n, width), any_) for n in splits]
     else:
-        outs = [((n, proj // 2), pl.BlockSpec((n, proj // 2), lambda i: (0, 0))) for n in splits]
+        outs = [(n, pl.BlockSpec(n, lambda i: (0, 0))) for n in splits]
     names = [i[0] for i in ins] + [f"out{i}" for i in range(len(outs))] + [s[0] for s in scratch]
     res = pl.pallas_call(
-        functools.partial(_unit_kernel, names, parts, len(lhs), len(outs), index),
+        functools.partial(_unit_kernel, names, parts, len(lhs), len(outs), index, moves, tuple(picks)),
         grid=(1,),
         in_specs=[i[2] for i in ins],
         out_specs=[o[1] for o in outs],
@@ -386,7 +384,7 @@
 
 
 CUTS = (16, 32, 16)
-UNITS = U1A, U1B, U2A, U2B, U3A, U3B, U0A, U0B = ("u1a", "u1b", "u2a", "u2b", "u3a", "u3b", "u0a", "u0b")
+UNITS = U1A, U1B, U2A, U3A, U3B, U2B, U0 = ("u1a", "u1b", "u2a", "u3a", "u3b", "u2b", "u0")
 
 
 def solution(mesh):
@@ -404,7 +402,7 @@
     def local_step(x_loc, ln_gain, wq_loc, w_kv, wo_loc, positions):
         me = lax.axis_index(AXIS)
         rows, width = x_loc.shape
-        seq = positions.shape[0]
+        seq, head = positions.shape[0], w_kv.shape[1] // 2
         piece = rows // 4
         gain = ln_gain.reshape(1, width)
 
@@ -412,14 +410,19 @@
             return [send(v, mask) for v in values]
 
         h, fx, fy, fd = [[] for _ in range(4)], [None] * 4, [None] * 4, [None] * 4
-        a, b, _ = CUTS
+        a, b, c = CUTS
         early = fetch_first(x_loc, a)
         middle, = norm_rows(x_loc, gain, a, b, 1, a)
         head_rows, tail_rows = norm_rows(x_loc, gain, 0, a, 2, a, (a + b) // a)
         h[0] = [head_rows, middle, tail_rows]
         for i, v in enumerate(norm_rows(x_loc, gain, piece, piece, 3, piece // 2)):
             h[i + 1].append(v)
-        k_own, v_own = unit_call(sum(h, []), w_kv, None, None, None, None, None, 0, [rows - piece, rows + piece], slots=4, chunk=2048)
+        low, t = rows - piece, piece
+        own_top, own_rest, own_first = unit_call(
+            sum(h, []), w_kv, None, None, None, None, 0, [(low - t, head), (low + t, head), (2 * piece, head)],
+            picks=((0, 0, piece, low - t, 0), (1, 0, piece, low, head), (1, low, rows - t, t, 0), (2, 0, 0, piece, 0), (2, piece, 0, piece, head)),
+            slots=4, chunk=2048,
+        )
         sent = [[early] + h[0][1:]] + h[1:]
         for i in range(4):
             fx[i], fy[i] = send_all(sent[i], XN), send_all(sent[i], YN)
@@ -429,33 +432,68 @@
             fd[i] = send_all(fy[i], XN)
         for far in (fx, fy, fd):
             far[0] = [*norm_rows(far[0][0], gain, 0, a, 1, a), *far[0][1:]]
-        k_m, v_m = {0: k_own}, {0: v_own}
+        swaps = {}
+
+        def swap(values, name):
+            if name not in swaps:
+                swaps[name] = send_all(values, CORE)
+            return swaps[name]
+
+        mine = fx[0] + fy[0]
+        near, near_k, near_v = unit_call(
+            mine + swap(mine, U1A), w_kv, None, None, None, None, 0, [(8 * piece, head), (piece, head), (piece, head)],
+            picks=((0, 0, 0, 4 * piece, 0), (0, 4 * piece, 0, 4 * piece, head), (1, 0, 0, piece, 0), (2, 0, piece, piece, head)),
+            slots=4, chunk=2048,
+        )
+        top, rest = {0: own_top}, {0: own_rest}
         for m in (XN, YN):
-            k_m[m], v_m[m] = send(k_own, m), send(v_own, m)
-        k_m[DIAG], v_m[DIAG] = send(k_m[XN], YN), send(v_m[YN], XN)
+            top[m], rest[m] = send(own_top, m), send(own_rest, m)
+        top[DIAG], rest[DIAG] = send(top[XN], YN), send(rest[YN], XN)
+        far_k, far_v = send(near_k, YN), send(near_v, XN)
+        sources, moves = [near], []
+
+        def found(array, *ranges):
+            moves.extend((len(sources),) + x for x in ranges)
+            sources.append(array)
+
         for m in (0, XN, YN, DIAG):
-            k_m[m | CORE], v_m[m | CORE] = send(k_m[m], CORE), send(v_m[m], CORE)
-        keys, values = [k_m[m] for m in range(n_dev)], [v_m[m] for m in range(n_dev)]
-        k_cache, v_cache = order_blocks(keys, values)
+            for c in (0, CORE):
+                far = m | c
+                upper, lower = (send(v, CORE) for v in (top[m], rest[m])) if c else (top[m], rest[m])
+                found(upper, (0, low - t, 0, far, piece))
+                found(lower, (0, low, 1, far, piece), (low, t, 0, far, rows - t))
+                if m == 0:
+                    found(send(own_first, CORE) if c else own_first, (0, piece, 0, far, 0), (piece, piece, 1, far, 0))
+                elif m == DIAG:
+                    found(send(far_k, CORE) if c else far_k, (0, piece, 0, far, 0))
+                    found(send(far_v, CORE) if c else far_v, (0, piece, 1, far, 0))
+                else:
+                    first = ((m == YN) + 2 * c) * piece
+                    moves.extend(((0, first, piece, 0, far, 0), (0, 4 * piece + first, piece, 1, far, 0)))
+        k_cache, v_cache = order_blocks(sources, tuple(moves), rows, seq)
 
         pos_m = by_mask(positions.reshape(n_dev, 4, piece), me)
         kpos = pos_m.reshape(1, seq)
         plan = {
-            U0A: [(0, 0, h[0]), (0, 1, h[1])], U0B: [(0, 2, h[2]), (0, 3, h[3])],
+            U0: [(0, i, h[i]) for i in range(4)],
             U1A: [(XN, 0, fx[0]), (YN, 0, fy[0])], U1B: [(XN, 1, fx[1]), (YN, 2, fy[2])],
             U2A: [(XN, 2, fx[2]), (YN, 3, fy[3])], U2B: [(XN, 3, fx[3]), (YN, 1, fy[1])],
             U3A: [(DIAG, 0, fd[0]), (DIAG, 2, fd[2])], U3B: [(DIAG, 1, fd[1]), (DIAG, 3, fd[3])],
         }
-        qpos = jnp.concatenate([pos_m[m | c, i] for u in UNITS for c in (0, CORE) for m, i, _ in plan[u]]).reshape(len(UNITS), -1)
+        qpos = jnp.concatenate([pos_m[m | c, i] for u in UNITS for c in (0, CORE) for m, i, _ in plan[u]]).reshape(-1, rows)
         qpos, kpos = as_float(qpos, kpos)
 
         parts = {}
         for index, name in enumerate(UNITS):
             blocks = plan[name]
             mine = sum((b for _, _, b in blocks), [])
-            lhs = mine + send_all(mine, CORE)
+            lhs, wq = mine + swap(mine, name), wq_loc
+            if name == U0:
+                total_rows, width_q = 2 * rows, wq_loc.shape[1]
+                lhs = unit_call(lhs, wq_loc, None, None, None, None, 0, [(total_rows, width_q)], picks=((0, 0, 0, total_rows, 0),), slots=4)
+                wq = None
             splits = [piece] * len(blocks) + [piece * len(blocks)]
-            *own, other = unit_call(lhs, wq_loc, wo_loc, keys, values, qpos, kpos, index, splits)
+            *own, other = unit_call(lhs, wq, wo_loc, (sources, moves), qpos, kpos, index, splits)
             back = send(other, CORE)
             for j, (m, i, _) in enumerate(blocks):
                 parts[m, i] = [(own[j], 0), (back, j * piece)]

time: 940 us -> 976 us (1.038)
  waiting for transfers between devices: 355 us -> 377 us
    ppermute x82 -> x86, waiting for transfers between devices: 355 us -> 377 us  [send(): return lax.ppermute(value, AXIS, [(i, i ^ mask) for i in range(n_dev)])]
    pallas_call x9 -> x10, Pallas kernels: 415 us -> 424 us  [unit_call(): pl.pallas_call(functools.partial(_unit_kernel, names, parts, len(lhs), le...]
    ppermute x82 -> x86, starting transfers between devices: 54 us -> 56.9 us  [send(): return lax.ppermute(value, AXIS, [(i, i ^ mask) for i in range(n_dev)])]
  transfers between devices with their start and end apart: 82 -> 86, of which waited for: 16 -> 21; matrix products, arithmetic and copies ran while one was open for 0% -> 0% of each run, Pallas kernels for 52% -> 51%
where the time goes in v3:
time: 976 us; the launch traced here: 975 us
  Pallas kernels  532 us (55%)
  waiting for transfers between devices  377 us (39%)
  starting transfers between devices  56.9 us (6%)
    pallas_call x10, Pallas kernels, unit_call(): pl.pallas_call(functools.partial(_unit_kernel, names, parts, len(lhs), le...  424 us
    ppermute x86, waiting for transfers between devices, send(): return lax.ppermute(value, AXIS, [(i, i ^ mask) for i in range(n_dev)])  377 us
    pallas_call x16, Pallas kernels, sums(): pl.pallas_call(functools.partial(_sums_kernel, tuple(spec), len(arrays)),...  76.1 us
    ppermute x86, starting transfers between devices, send(): return lax.ppermute(value, AXIS, [(i, i ^ mask) for i in range(n_dev)])  56.9 us
    pallas_call x6, Pallas kernels, norm_rows(): pl.pallas_call(functools.partial(_norm_kernel, 2048, steps), grid=(count...  27.2 us
  transfers between devices with their start and end apart: 86, of which 21 were waited for; matrix products, arithmetic and copies ran while one was open for 0% of the time, Pallas kernels for 51%

profile of v3, /device:TPU:0, one launch (start us, length us, event | category | flops | bytes accessed | tf_op | source)
XLA Modules:
  0.0 974.6 jit_solution(16086510025562609677)
XLA Ops:
  0.6 3.7 norm.6
  4.3 3.5 norm.7.flat_1_
  7.8 11.5 %norm.8 = (bf16[64,18432]{1,0:T(8,128)(2,1)}, bf16[64,18432]{1,0:T(8,128)(2,1)}, bf16[64,18432]{1,0:T(8,128)(2,1)}) custom-call(bf16[256,18432]{1,0:T(8,128)(2,1)} %x_hbm.1, f32[1,18432]{1,0:T(1,128)} %bitcast.68), custom_call_target="tpu_custom_call" | custom-call | flops 28311552 | bytes 14155776 | tf_op jit(solution)/shard_map/norm/pallas_call | solution.py:80
  19.3 11.1 %shard_map.87 = (bf16[128,256]{1,0:T(8,128)(2,1)}, bf16[256,256]{1,0:T(8,128)(2,1)}, bf16[128,256]{1,0:T(8,128)(2,1)}) custom-call(bf16[16,18432]{1,0:T(8,128)(2,1)} %get-tuple-element.57.flat_0_, bf16[32,18432]{1,0:T(8,128)(2,1)} %norm.7.flat_1_, bf16[16,18432]{1,0:T(8,128)(2,1)} %get-tuple-element.58.flat_2_, bf16[64,18432]{1,0:T(8,128)(2,1)} %get-tuple-element.59.flat_3_, ...), custom_call_target="tpu_custom_call" | custom-call | flops 4831838208 | bytes 28311552 | tf_op jit(solution)/shard_map/pallas_call | solution.py:287
  30.4 3.3 collective-permute-start.21
  51.4 25.3 %collective-permute-done.30.flat_18_.flat_30_.flat_22_.flat_26_.refs_16_ = bf16[256,256]{1,0:T(8,128)(2,1)S(1)} collective-permute-done((bf16[256,256]{1,0:T(8,128)(2,1)S(1)}, bf16[256,256]{1,0:T(8,128)(2,1)S(1)}, u32[]{:S(2)}, u32[]{:S(2)}) %collective-permute-start.30) | collective-permute-done | bytes 131104 | tf_op jit(solution)/shard_map/ppermute | solution.py:394
  80.3 13.9 %collective-permute-done.9.x_ref = bf16[16,18432]{1,0:T(8,128)(2,1)S(1)} collective-permute-done((bf16[16,18432]{1,0:T(8,128)(2,1)S(1)}, bf16[16,18432]{1,0:T(8,128)(2,1)S(1)}, u32[]{:S(2)}, u32[]{:S(2)}) %collective-permute-start.9) | collective-permute-done | bytes 589856 | tf_op jit(solution)/shard_map/ppermute | solution.py:394
  95.6 2.7 norm.9.flat_0_
  98.5 6.6 collective-permute-done.7.flat_1_
  105.1 3.1 norm.10.flat_3_
  108.8 10.0 %collective-permute-done.10.flat_4_ = bf16[32,18432]{1,0:T(8,128)(2,1)} collective-permute-done((bf16[32,18432]{1,0:T(8,128)(2,1)S(1)}, bf16[32,18432]{1,0:T(8,128)(2,1)}, u32[]{:S(2)}, u32[]{:S(2)}) %collective-permute-start.10) | collective-permute-done | bytes 1179680 | tf_op jit(solution)/shard_map/ppermute | solution.py:394
  121.2 7.6 collective-permute-done.16.flat_10_
  130.3 11.4 %shard_map.86 = (bf16[512,256]{1,0:T(8,128)(2,1)}, bf16[64,256]{1,0:T(8,128)(2,1)}, bf16[64,256]{1,0:T(8,128)(2,1)}) custom-call(bf16[16,18432]{1,0:T(8,128)(2,1)} %norm.9.flat_0_, bf16[32,18432]{1,0:T(8,128)(2,1)} %copy-done.8, bf16[16,18432]{1,0:T(8,128)(2,1)} %copy-done.17, bf16[16,18432]{1,0:T(8,128)(2,1)} %norm.10.flat_3_, ...), custom_call_target="tpu_custom_call" | custom-call | flops 4831838208 | bytes 28311552 | tf_op jit(solution)/shard_map/pallas_call | solution.py:287
  141.7 2.6 collective-permute-done.53.x_ref
  149.4 2.7 norm.11.flat_0_
  154.7 37.4 %shard_map.85.flat_0_ = bf16[512,1536]{1,0:T(8,128)(2,1)} custom-call(bf16[16,18432]{1,0:T(8,128)(2,1)} %get-tuple-element.57.flat_0_, bf16[32,18432]{1,0:T(8,128)(2,1)} %norm.7.flat_1_, bf16[16,18432]{1,0:T(8,128)(2,1)} %get-tuple-element.58.flat_2_, bf16[64,18432]{1,0:T(8,128)(2,1)} %get-tuple-element.59.flat_3_, ...), custom_call_target="tpu_custom_call" | custom-call | flops 28991029248 | bytes 75497472 | tf_op jit(solution)/shard_map/pallas_call | solution.py:287
  193.6 12.9 %collective-permute-done.66.flat_0_ = bf16[64,18432]{1,0:T(8,128)(2,1)} collective-permute-done((bf16[64,18432]{1,0:T(8,128)(2,1)}, bf16[64,18432]{1,0:T(8,128)(2,1)}, u32[]{:S(2)}, u32[]{:S(2)}) %collective-permute-start.66) | collective-permute-done | bytes 2359328 | tf_op jit(solution)/shard_map/ppermute | solution.py:394
  209.8 51.1 %shard_map.89 = (bf16[64,18432]{1,0:T(8,128)(2,1)}, bf16[64,18432]{1,0:T(8,128)(2,1)}, bf16[128,18432]{1,0:T(8,128)(2,1)}) custom-call(bf16[16,18432]{1,0:T(8,128)(2,1)} %norm.9.flat_0_, bf16[32,18432]{1,0:T(8,128)(2,1)} %copy-done.8, bf16[16,18432]{1,0:T(8,128)(2,1)} %copy-done.17, bf16[16,18432]{1,0:T(8,128)(2,1)} %norm.10.flat_3_, ...), custom_call_target="tpu_custom_call" | custom-call | flops 32212254720 | bytes 132120576 | tf_op jit(solution)/shard_map/pallas_call | solution.py:287
  262.2 43.2 %collective-permute-done.47.flat_0_ = bf16[64,18432]{1,0:T(8,128)(2,1)} collective-permute-done((bf16[64,18432]{1,0:T(8,128)(2,1)}, bf16[64,18432]{1,0:T(8,128)(2,1)}, u32[]{:S(2)}, u32[]{:S(2)}) %collective-permute-start.47) | collective-permute-done | bytes 2359328 | tf_op jit(solution)/shard_map/ppermute | solution.py:394
  307.0 50.7 %shard_map.93 = (bf16[64,18432]{1,0:T(8,128)(2,1)}, bf16[64,18432]{1,0:T(8,128)(2,1)}, bf16[128,18432]{1,0:T(8,128)(2,1)}) custom-call(bf16[64,18432]{1,0:T(8,128)(2,1)} %collective-permute-done.66.flat_0_, bf16[64,18432]{1,0:T(8,128)(2,1)} %collective-permute-done.67.flat_1_, bf16[64,18432]{1,0:T(8,128)(2,1)} %collective-permute-done.68.flat_2_, ...), custom_call_target="tpu_custom_call" | custom-call | flops 32212254720 | bytes 132120576 | tf_op jit(solution)/shard_map/pallas_call | solution.py:287
  360.4 50.5 %shard_map.91 = (bf16[64,18432]{1,0:T(8,128)(2,1)}, bf16[64,18432]{1,0:T(8,128)(2,1)}, bf16[128,18432]{1,0:T(8,128)(2,1)}) custom-call(bf16[64,18432]{1,0:T(8,128)(2,1)} %collective-permute-done.47.flat_0_, bf16[64,18432]{1,0:T(8,128)(2,1)} %collective-permute-done.48.flat_1_, bf16[64,18432]{1,0:T(8,128)(2,1)} %collective-permute-done.49.flat_2_, ...), custom_call_target="tpu_custom_call" | custom-call | flops 32212254720 | bytes 132120576 | tf_op jit(solution)/shard_map/pallas_call | solution.py:287
  414.4 50.5 %shard_map.90 = (bf16[64,18432]{1,0:T(8,128)(2,1)}, bf16[64,18432]{1,0:T(8,128)(2,1)}, bf16[128,18432]{1,0:T(8,128)(2,1)}) custom-call(bf16[64,18432]{1,0:T(8,128)(2,1)} %collective-permute-done.40.flat_0_, bf16[64,18432]{1,0:T(8,128)(2,1)} %collective-permute-done.41.flat_1_, bf16[64,18432]{1,0:T(8,128)(2,1)} %collective-permute-done.42.flat_2_, ...), custom_call_target="tpu_custom_call" | custom-call | flops 32212254720 | bytes 132120576 | tf_op jit(solution)/shard_map/pallas_call | solution.py:287
  466.0 50.8 %shard_map.94 = (bf16[64,18432]{1,0:T(8,128)(2,1)}, bf16[64,18432]{1,0:T(8,128)(2,1)}, bf16[128,18432]{1,0:T(8,128)(2,1)}) custom-call(bf16[64,18432]{1,0:T(8,128)(2,1)} %collective-permute-done.71.flat_0_, bf16[64,18432]{1,0:T(8,128)(2,1)} %collective-permute-done.72.flat_1_, bf16[64,18432]{1,0:T(8,128)(2,1)} %collective-permute-done.73.flat_2_, ...), custom_call_target="tpu_custom_call" | custom-call | flops 32212254720 | bytes 132120576 | tf_op jit(solution)/shard_map/pallas_call | solution.py:287
  517.9 50.8 %shard_map.92 = (bf16[64,18432]{1,0:T(8,128)(2,1)}, bf16[64,18432]{1,0:T(8,128)(2,1)}, bf16[128,18432]{1,0:T(8,128)(2,1)}) custom-call(bf16[16,18432]{1,0:T(8,128)(2,1)} %norm.11.flat_0_, bf16[32,18432]{1,0:T(8,128)(2,1)} %collective-permute-done.54.flat_1_, bf16[16,18432]{1,0:T(8,128)(2,1)} %collective-permute-done.55.flat_2_, ...), custom_call_target="tpu_custom_call" | custom-call | flops 32212254720 | bytes 132120576 | tf_op jit(solution)/shard_map/pallas_call | solution.py:287
  569.2 59.2 %shard_map.88 = (bf16[64,18432]{1,0:T(8,128)(2,1)}, bf16[64,18432]{1,0:T(8,128)(2,1)}, bf16[64,18432]{1,0:T(8,128)(2,1)}, bf16[64,18432]{1,0:T(8,128)(2,1)}, bf16[256,18432]{1,0:T(8,128)(2,1)}) custom-call(bf16[512,1536]{1,0:T(8,128)(2,1)} %shard_map.85.flat_0_, bf16[1536,18432]{1,0:T(8,128)(2,1)} %flat_5_.7, ...), custom_call_target="tpu_custom_call" | custom-call | flops 35433480192 | bytes 75497472 | tf_op jit(solution)/shard_map/pallas_call | solution.py:287
  628.5 3.8 sums.16
  633.5 3.8 sums.18
  638.5 6.0 sums.20
  646.3 6.1 sums.23
  652.4 34.4 %collective-permute-done.39.refs_2_ = bf16[64,18432]{1,0:T(8,128)(2,1)} collective-permute-done((bf16[64,18432]{1,0:T(8,128)(2,1)}, bf16[64,18432]{1,0:T(8,128)(2,1)}, u32[]{:S(2)}, u32[]{:S(2)}) %collective-permute-start.39) | collective-permute-done | bytes 2359328 | tf_op jit(solution)/shard_map/ppermute | solution.py:394
  688.0 3.8 collective-permute-done.52.refs_8_
  692.9 6.0 sums.17
  698.9 38.3 %collective-permute-done.62.refs_2_ = bf16[64,18432]{1,0:T(8,128)(2,1)} collective-permute-done((bf16[64,18432]{1,0:T(8,128)(2,1)}, bf16[64,18432]{1,0:T(8,128)(2,1)}, u32[]{:S(2)}, u32[]{:S(2)}) %collective-permute-start.62) | collective-permute-done | bytes 2359328 | tf_op jit(solution)/shard_map/ppermute | solution.py:394
  738.5 3.8 collective-permute-done.63.refs_5_
  743.5 7.6 sums.21
  751.0 36.8 %collective-permute-done.76.refs_2_ = bf16[64,18432]{1,0:T(8,128)(2,1)} collective-permute-done((bf16[64,18432]{1,0:T(8,128)(2,1)}, bf16[64,18432]{1,0:T(8,128)(2,1)}, u32[]{:S(2)}, u32[]{:S(2)}) %collective-permute-start.76) | collective-permute-done | bytes 2359328 | tf_op jit(solution)/shard_map/ppermute | solution.py:394
  788.9 4.0 collective-permute-done.77.refs_4_
  793.7 4.6 sums.24
  798.3 40.1 %collective-permute-done.45.refs_4_ = bf16[64,18432]{1,0:T(8,128)(2,1)} collective-permute-done((bf16[64,18432]{1,0:T(8,128)(2,1)}, bf16[64,18432]{1,0:T(8,128)(2,1)}, u32[]{:S(2)}, u32[]{:S(2)}) %collective-permute-start.45) | collective-permute-done | bytes 2359328 | tf_op jit(solution)/shard_map/ppermute | solution.py:394
  839.5 4.0 collective-permute-done.46.refs_6_
  844.3 3.0 sums.26
  848.4 82.8 %collective-permute-done.80.refs_1_ = bf16[16,18432]{1,0:T(8,128)(2,1)} collective-permute-done((bf16[16,18432]{1,0:T(8,128)(2,1)}, bf16[16,18432]{1,0:T(8,128)(2,1)}, u32[]{:S(2)}, u32[]{:S(2)}) %collective-permute-start.80) | collective-permute-done | bytes 589856 | tf_op jit(solution)/shard_map/ppermute | solution.py:394
  934.5 2.5 sums.28
  941.1 3.1 order.1
  944.1 13.5 %sums.19.refs_0_ = bf16[256,18432]{1,0:T(8,128)(2,1)} custom-call(bf16[64,18432]{1,0:T(8,128)(2,1)} %get-tuple-element.70.refs_0_, bf16[256,18432]{1,0:T(8,128)(2,1)} %collective-permute-done.37.refs_1_, bf16[64,18432]{1,0:T(8,128)(2,1)} %collective-permute-done.39.refs_2_, bf16[64,18432]{1,0:T(8,128)(2,1)} %get-tuple-element.74.refs_3_, ...), custom_call_target="tpu_custom_call" | custom-call | flops 14155776 | bytes 56623104 | tf_op jit(solution)/shard_map/sums/pallas_call | solution.py:357
  957.6 6.1 sums.22.refs_0_
  963.7 3.5 sums.25.refs_0_
  967.1 2.6 sums.27.refs_0_
  (236 shorter events, 76.8 us)
Async XLA Ops:
  79.6 39.2 %collective-permute-start.10 = (bf16[32,18432]{1,0:T(8,128)(2,1)S(1)}, bf16[32,18432]{1,0:T(8,128)(2,1)}, u32[]{:S(2)}, u32[]{:S(2)}) collective-permute-start(bf16[32,18432]{1,0:T(8,128)(2,1)S(1)} %copy-done.7), channel_id=1, source_target_pairs={{0,4},{1,5},{2,6},{3,7},{4,0},{5,1},{6,2},{7,3}} | collective-permute-start | bytes 3538952 | tf_op jit(solution)/shard_map/ppermute | solution.py:394
  108.3 43.7 %collective-permute-start.3 = (bf16[64,18432]{1,0:T(8,128)(2,1)}, bf16[64,18432]{1,0:T(8,128)(2,1)}, u32[]{:S(2)}, u32[]{:S(2)}) collective-permute-start(bf16[64,18432]{1,0:T(8,128)(2,1)} %get-tuple-element.59.flat_3_), channel_id=1, source_target_pairs={{0,1},{1,0},{2,3},{3,2},{4,5},{5,4},{6,7},{7,6}} | collective-permute-start | bytes 7077896 | tf_op jit(solution)/shard_map/ppermute | solution.py:394
  152.1 54.4 %collective-permute-start.66 = (bf16[64,18432]{1,0:T(8,128)(2,1)}, bf16[64,18432]{1,0:T(8,128)(2,1)}, u32[]{:S(2)}, u32[]{:S(2)}) collective-permute-start(bf16[64,18432]{1,0:T(8,128)(2,1)} %get-tuple-element.61.flat_5_), channel_id=1, source_target_pairs={{0,2},{1,3},{2,0},{3,1},{4,6},{5,7},{6,4},{7,5}} | collective-permute-start | bytes 7077896 | tf_op jit(solution)/shard_map/ppermute | solution.py:394
  153.3 54.0 %collective-permute-start.67 = (bf16[64,18432]{1,0:T(8,128)(2,1)}, bf16[64,18432]{1,0:T(8,128)(2,1)}, u32[]{:S(2)}, u32[]{:S(2)}) collective-permute-start(bf16[64,18432]{1,0:T(8,128)(2,1)} %get-tuple-element.59.flat_3_), channel_id=1, source_target_pairs={{0,4},{1,5},{2,6},{3,7},{4,0},{5,1},{6,2},{7,3}} | collective-permute-start | bytes 7077896 | tf_op jit(solution)/shard_map/ppermute | solution.py:394
  154.1 38.0 %collective-permute-start.34 = (bf16[256,256]{1,0:T(8,128)(2,1)S(1)}, bf16[256,256]{1,0:T(8,128)(2,1)S(1)}, u32[]{:S(2)}, u32[]{:S(2)}) collective-permute-start(bf16[256,256]{1,0:T(8,128)(2,1)S(1)} %collective-permute-done.30.flat_18_.flat_30_.flat_22_.flat_26_.refs_16_), channel_id=1, source_target_pairs={{0,1},{1,0},{2,3},{3,2},{4,5},{5,4},{6,7},{7,6}} | collective-permute-start | bytes 393224 | tf_op jit(solution)/shard_map/ppermute | solution.py:394
  154.1 54.4 %collective-permute-start.35 = (bf16[64,256]{1,0:T(8,128)(2,1)S(1)}, bf16[64,256]{1,0:T(8,128)(2,1)S(1)}, u32[]{:S(2)}, u32[]{:S(2)}) collective-permute-start(bf16[64,256]{1,0:T(8,128)(2,1)S(1)} %collective-permute-done.31.flat_19_.flat_31_.flat_23_.flat_27_.refs_17_), channel_id=1, source_target_pairs={{0,1},{1,0},{2,3},{3,2},{4,5},{5,4},{6,7},{7,6}} | collective-permute-start | bytes 98312 | tf_op jit(solution)/shard_map/ppermute | solution.py:394
  154.6 53.9 %collective-permute-start.36 = (bf16[64,256]{1,0:T(8,128)(2,1)S(1)}, bf16[64,256]{1,0:T(8,128)(2,1)S(1)}, u32[]{:S(2)}, u32[]{:S(2)}) collective-permute-start(bf16[64,256]{1,0:T(8,128)(2,1)S(1)} %collective-permute-done.32.flat_20_.flat_32_.flat_24_.flat_28_.refs_18_), channel_id=1, source_target_pairs={{0,1},{1,0},{2,3},{3,2},{4,5},{5,4},{6,7},{7,6}} | collective-permute-start | bytes 98312 | tf_op jit(solution)/shard_map/ppermute | solution.py:394
  192.8 164.9 %collective-permute-start.40 = (bf16[64,18432]{1,0:T(8,128)(2,1)}, bf16[64,18432]{1,0:T(8,128)(2,1)}, u32[]{:S(2)}, u32[]{:S(2)}) collective-permute-start(bf16[64,18432]{1,0:T(8,128)(2,1)} %get-tuple-element.59.flat_3_), channel_id=1, source_target_pairs={{0,2},{1,3},{2,0},{3,1},{4,6},{5,7},{6,4},{7,5}} | collective-permute-start | bytes 7077896 | tf_op jit(solution)/shard_map/ppermute | solution.py:394
  206.5 54.4 %collective-permute-start.48 = (bf16[64,18432]{1,0:T(8,128)(2,1)}, bf16[64,18432]{1,0:T(8,128)(2,1)}, u32[]{:S(2)}, u32[]{:S(2)}) collective-permute-start(bf16[64,18432]{1,0:T(8,128)(2,1)} %get-tuple-element.61.flat_5_), channel_id=1, source_target_pairs={{0,4},{1,5},{2,6},{3,7},{4,0},{5,1},{6,2},{7,3}} | collective-permute-start | bytes 7077896 | tf_op jit(solution)/shard_map/ppermute | solution.py:394
  207.3 98.1 %collective-permute-start.47 = (bf16[64,18432]{1,0:T(8,128)(2,1)}, bf16[64,18432]{1,0:T(8,128)(2,1)}, u32[]{:S(2)}, u32[]{:S(2)}) collective-permute-start(bf16[64,18432]{1,0:T(8,128)(2,1)} %get-tuple-element.60.flat_4_), channel_id=1, source_target_pairs={{0,2},{1,3},{2,0},{3,1},{4,6},{5,7},{6,4},{7,5}} | collective-permute-start | bytes 7077896 | tf_op jit(solution)/shard_map/ppermute | solution.py:394
  208.6 97.9 %collective-permute-start.68 = (bf16[64,18432]{1,0:T(8,128)(2,1)}, bf16[64,18432]{1,0:T(8,128)(2,1)}, u32[]{:S(2)}, u32[]{:S(2)}) collective-permute-start(bf16[64,18432]{1,0:T(8,128)(2,1)} %collective-permute-done.66.flat_0_), channel_id=1, source_target_pairs={{0,1},{1,0},{2,3},{3,2},{4,5},{5,4},{6,7},{7,6}} | collective-permute-start | bytes 7077896 | tf_op jit(solution)/shard_map/ppermute | solution.py:394
  209.2 97.3 %collective-permute-start.69 = (bf16[64,18432]{1,0:T(8,128)(2,1)}, bf16[64,18432]{1,0:T(8,128)(2,1)}, u32[]{:S(2)}, u32[]{:S(2)}) collective-permute-start(bf16[64,18432]{1,0:T(8,128)(2,1)} %collective-permute-done.67.flat_1_), channel_id=1, source_target_pairs={{0,1},{1,0},{2,3},{3,2},{4,5},{5,4},{6,7},{7,6}} | collective-permute-start | bytes 7077896 | tf_op jit(solution)/shard_map/ppermute | solution.py:394
  260.9 98.0 %collective-permute-start.41 = (bf16[64,18432]{1,0:T(8,128)(2,1)}, bf16[64,18432]{1,0:T(8,128)(2,1)}, u32[]{:S(2)}, u32[]{:S(2)}) collective-permute-start(bf16[64,18432]{1,0:T(8,128)(2,1)} %get-tuple-element.60.flat_4_), channel_id=1, source_target_pairs={{0,4},{1,5},{2,6},{3,7},{4,0},{5,1},{6,2},{7,3}} | collective-permute-start | bytes 7077896 | tf_op jit(solution)/shard_map/ppermute | solution.py:394
  305.4 159.6 %collective-permute-start.55 = (bf16[16,18432]{1,0:T(8,128)(2,1)}, bf16[16,18432]{1,0:T(8,128)(2,1)}, u32[]{:S(2)}, u32[]{:S(2)}) collective-permute-start(bf16[16,18432]{1,0:T(8,128)(2,1)} %copy-done.17), channel_id=1, source_target_pairs={{0,4},{1,5},{2,6},{3,7},{4,0},{5,1},{6,2},{7,3}} | collective-permute-start | bytes 1769480 | tf_op jit(solution)/shard_map/ppermute | solution.py:394
  306.5 53.4 %collective-permute-start.50 = (bf16[64,18432]{1,0:T(8,128)(2,1)}, bf16[64,18432]{1,0:T(8,128)(2,1)}, u32[]{:S(2)}, u32[]{:S(2)}) collective-permute-start(bf16[64,18432]{1,0:T(8,128)(2,1)} %collective-permute-done.48.flat_1_), channel_id=1, source_target_pairs={{0,1},{1,0},{2,3},{3,2},{4,5},{5,4},{6,7},{7,6}} | collective-permute-start | bytes 7077896 | tf_op jit(solution)/shard_map/ppermute | solution.py:394
  306.5 53.4 %collective-permute-start.49 = (bf16[64,18432]{1,0:T(8,128)(2,1)}, bf16[64,18432]{1,0:T(8,128)(2,1)}, u32[]{:S(2)}, u32[]{:S(2)}) collective-permute-start(bf16[64,18432]{1,0:T(8,128)(2,1)} %collective-permute-done.47.flat_0_), channel_id=1, source_target_pairs={{0,1},{1,0},{2,3},{3,2},{4,5},{5,4},{6,7},{7,6}} | collective-permute-start | bytes 7077896 | tf_op jit(solution)/shard_map/ppermute | solution.py:394
  357.7 55.4 %collective-permute-start.72 = (bf16[64,18432]{1,0:T(8,128)(2,1)}, bf16[64,18432]{1,0:T(8,128)(2,1)}, u32[]{:S(2)}, u32[]{:S(2)}) collective-permute-start(bf16[64,18432]{1,0:T(8,128)(2,1)} %collective-permute-done.48.flat_1_), channel_id=1, source_target_pairs={{0,2},{1,3},{2,0},{3,1},{4,6},{5,7},{6,4},{7,5}} | collective-permute-start | bytes 7077896 | tf_op jit(solution)/shard_map/ppermute | solution.py:394
  358.9 53.2 %collective-permute-start.71 = (bf16[64,18432]{1,0:T(8,128)(2,1)}, bf16[64,18432]{1,0:T(8,128)(2,1)}, u32[]{:S(2)}, u32[]{:S(2)}) collective-permute-start(bf16[64,18432]{1,0:T(8,128)(2,1)} %collective-permute-done.40.flat_0_), channel_id=1, source_target_pairs={{0,4},{1,5},{2,6},{3,7},{4,0},{5,1},{6,2},{7,3}} | collective-permute-start | bytes 7077896 | tf_op jit(solution)/shard_map/ppermute | solution.py:394
  359.9 54.0 %collective-permute-start.42 = (bf16[64,18432]{1,0:T(8,128)(2,1)}, bf16[64,18432]{1,0:T(8,128)(2,1)}, u32[]{:S(2)}, u32[]{:S(2)}) collective-permute-start(bf16[64,18432]{1,0:T(8,128)(2,1)} %collective-permute-done.40.flat_0_), channel_id=1, source_target_pairs={{0,1},{1,0},{2,3},{3,2},{4,5},{5,4},{6,7},{7,6}} | collective-permute-start | bytes 7077896 | tf_op jit(solution)/shard_map/ppermute | solution.py:394
  359.9 54.0 %collective-permute-start.43 = (bf16[64,18432]{1,0:T(8,128)(2,1)}, bf16[64,18432]{1,0:T(8,128)(2,1)}, u32[]{:S(2)}, u32[]{:S(2)}) collective-permute-start(bf16[64,18432]{1,0:T(8,128)(2,1)} %collective-permute-done.41.flat_1_), channel_id=1, source_target_pairs={{0,1},{1,0},{2,3},{3,2},{4,5},{5,4},{6,7},{7,6}} | collective-permute-start | bytes 7077896 | tf_op jit(solution)/shard_map/ppermute | solution.py:394
  412.2 52.8 %collective-permute-start.54 = (bf16[32,18432]{1,0:T(8,128)(2,1)}, bf16[32,18432]{1,0:T(8,128)(2,1)}, u32[]{:S(2)}, u32[]{:S(2)}) collective-permute-start(bf16[32,18432]{1,0:T(8,128)(2,1)} %copy-done.8), channel_id=1, source_target_pairs={{0,4},{1,5},{2,6},{3,7},{4,0},{5,1},{6,2},{7,3}} | collective-permute-start | bytes 3538952 | tf_op jit(solution)/shard_map/ppermute | solution.py:394
  413.1 52.4 %collective-permute-start.56 = (bf16[64,18432]{1,0:T(8,128)(2,1)}, bf16[64,18432]{1,0:T(8,128)(2,1)}, u32[]{:S(2)}, u32[]{:S(2)}) collective-permute-start(bf16[64,18432]{1,0:T(8,128)(2,1)} %collective-permute-done.41.flat_1_), channel_id=1, source_target_pairs={{0,2},{1,3},{2,0},{3,1},{4,6},{5,7},{6,4},{7,5}} | collective-permute-start | bytes 7077896 | tf_op jit(solution)/shard_map/ppermute | solution.py:394
  413.9 51.6 %collective-permute-start.73 = (bf16[64,18432]{1,0:T(8,128)(2,1)}, bf16[64,18432]{1,0:T(8,128)(2,1)}, u32[]{:S(2)}, u32[]{:S(2)}) collective-permute-start(bf16[64,18432]{1,0:T(8,128)(2,1)} %collective-permute-done.71.flat_0_), channel_id=1, source_target_pairs={{0,1},{1,0},{2,3},{3,2},{4,5},{5,4},{6,7},{7,6}} | collective-permute-start | bytes 7077896 | tf_op jit(solution)/shard_map/ppermute | solution.py:394
  413.9 52.1 %collective-permute-start.74 = (bf16[64,18432]{1,0:T(8,128)(2,1)}, bf16[64,18432]{1,0:T(8,128)(2,1)}, u32[]{:S(2)}, u32[]{:S(2)}) collective-permute-start(bf16[64,18432]{1,0:T(8,128)(2,1)} %collective-permute-done.72.flat_1_), channel_id=1, source_target_pairs={{0,1},{1,0},{2,3},{3,2},{4,5},{5,4},{6,7},{7,6}} | collective-permute-start | bytes 7077896 | tf_op jit(solution)/shard_map/ppermute | solution.py:394
  464.9 52.4 %collective-permute-start.57 = (bf16[16,18432]{1,0:T(8,128)(2,1)}, bf16[16,18432]{1,0:T(8,128)(2,1)}, u32[]{:S(2)}, u32[]{:S(2)}) collective-permute-start(bf16[16,18432]{1,0:T(8,128)(2,1)} %norm.11.flat_0_), channel_id=1, source_target_pairs={{0,1},{1,0},{2,3},{3,2},{4,5},{5,4},{6,7},{7,6}} | collective-permute-start | bytes 1769480 | tf_op jit(solution)/shard_map/ppermute | solution.py:394
  465.0 51.8 %collective-permute-start.59 = (bf16[16,18432]{1,0:T(8,128)(2,1)}, bf16[16,18432]{1,0:T(8,128)(2,1)}, u32[]{:S(2)}, u32[]{:S(2)}) collective-permute-start(bf16[16,18432]{1,0:T(8,128)(2,1)} %collective-permute-done.55.flat_2_), channel_id=1, source_target_pairs={{0,1},{1,0},{2,3},{3,2},{4,5},{5,4},{6,7},{7,6}} | collective-permute-start | bytes 1769480 | tf_op jit(solution)/shard_map/ppermute | solution.py:394
  465.5 51.9 %collective-permute-start.58 = (bf16[32,18432]{1,0:T(8,128)(2,1)}, bf16[32,18432]{1,0:T(8,128)(2,1)}, u32[]{:S(2)}, u32[]{:S(2)}) collective-permute-start(bf16[32,18432]{1,0:T(8,128)(2,1)} %collective-permute-done.54.flat_1_), channel_id=1, source_target_pairs={{0,1},{1,0},{2,3},{3,2},{4,5},{5,4},{6,7},{7,6}} | collective-permute-start | bytes 3538952 | tf_op jit(solution)/shard_map/ppermute | solution.py:394
  465.5 103.2 %collective-permute-start.38 = (bf16[128,18432]{1,0:T(8,128)(2,1)}, bf16[128,18432]{1,0:T(8,128)(2,1)}, u32[]{:S(2)}, u32[]{:S(2)}) collective-permute-start(bf16[128,18432]{1,0:T(8,128)(2,1)} %get-tuple-element.73), channel_id=1, source_target_pairs={{0,1},{1,0},{2,3},{3,2},{4,5},{5,4},{6,7},{7,6}} | collective-permute-start | bytes 14155784 | tf_op jit(solution)/shard_map/ppermute | solution.py:394
  466.0 51.8 %collective-permute-start.60 = (bf16[64,18432]{1,0:T(8,128)(2,1)}, bf16[64,18432]{1,0:T(8,128)(2,1)}, u32[]{:S(2)}, u32[]{:S(2)}) collective-permute-start(bf16[64,18432]{1,0:T(8,128)(2,1)} %collective-permute-done.56.flat_3_), channel_id=1, source_target_pairs={{0,1},{1,0},{2,3},{3,2},{4,5},{5,4},{6,7},{7,6}} | collective-permute-start | bytes 7077896 | tf_op jit(solution)/shard_map/ppermute | solution.py:394
  516.8 111.6 %collective-permute-start.70 = (bf16[128,18432]{1,0:T(8,128)(2,1)}, bf16[128,18432]{1,0:T(8,128)(2,1)}, u32[]{:S(2)}, u32[]{:S(2)}) collective-permute-start(bf16[128,18432]{1,0:T(8,128)(2,1)} %get-tuple-element.94), channel_id=1, source_target_pairs={{0,1},{1,0},{2,3},{3,2},{4,5},{5,4},{6,7},{7,6}} | collective-permute-start | bytes 14155784 | tf_op jit(solution)/shard_map/ppermute | solution.py:394
  517.3 115.0 %collective-permute-start.51 = (bf16[128,18432]{1,0:T(8,128)(2,1)}, bf16[128,18432]{1,0:T(8,128)(2,1)}, u32[]{:S(2)}, u32[]{:S(2)}) collective-permute-start(bf16[128,18432]{1,0:T(8,128)(2,1)} %get-tuple-element.83), channel_id=1, source_target_pairs={{0,1},{1,0},{2,3},{3,2},{4,5},{5,4},{6,7},{7,6}} | collective-permute-start | bytes 14155784 | tf_op jit(solution)/shard_map/ppermute | solution.py:394
  517.4 127.2 %collective-permute-start.44 = (bf16[128,18432]{1,0:T(8,128)(2,1)}, bf16[128,18432]{1,0:T(8,128)(2,1)}, u32[]{:S(2)}, u32[]{:S(2)}) collective-permute-start(bf16[128,18432]{1,0:T(8,128)(2,1)} %get-tuple-element.76), channel_id=1, source_target_pairs={{0,1},{1,0},{2,3},{3,2},{4,5},{5,4},{6,7},{7,6}} | collective-permute-start | bytes 14155784 | tf_op jit(solution)/shard_map/ppermute | solution.py:394
  517.8 127.5 %collective-permute-start.75 = (bf16[128,18432]{1,0:T(8,128)(2,1)}, bf16[128,18432]{1,0:T(8,128)(2,1)}, u32[]{:S(2)}, u32[]{:S(2)}) collective-permute-start(bf16[128,18432]{1,0:T(8,128)(2,1)} %get-tuple-element.96), channel_id=1, source_target_pairs={{0,1},{1,0},{2,3},{3,2},{4,5},{5,4},{6,7},{7,6}} | collective-permute-start | bytes 14155784 | tf_op jit(solution)/shard_map/ppermute | solution.py:394
  568.7 68.6 %collective-permute-start.61 = (bf16[128,18432]{1,0:T(8,128)(2,1)}, bf16[128,18432]{1,0:T(8,128)(2,1)}, u32[]{:S(2)}, u32[]{:S(2)}) collective-permute-start(bf16[128,18432]{1,0:T(8,128)(2,1)} %get-tuple-element.86), channel_id=1, source_target_pairs={{0,1},{1,0},{2,3},{3,2},{4,5},{5,4},{6,7},{7,6}} | collective-permute-start | bytes 14155784 | tf_op jit(solution)/shard_map/ppermute | solution.py:394
  628.4 218.9 %collective-permute-start.37 = (bf16[256,18432]{1,0:T(8,128)(2,1)}, bf16[256,18432]{1,0:T(8,128)(2,1)}, u32[]{:S(2)}, u32[]{:S(2)}) collective-permute-start(bf16[256,18432]{1,0:T(8,128)(2,1)} %get-tuple-element.71), channel_id=1, source_target_pairs={{0,1},{1,0},{2,3},{3,2},{4,5},{5,4},{6,7},{7,6}} | collective-permute-start | bytes 28311560 | tf_op jit(solution)/shard_map/ppermute | solution.py:394
  632.3 54.5 %collective-permute-start.39 = (bf16[64,18432]{1,0:T(8,128)(2,1)}, bf16[64,18432]{1,0:T(8,128)(2,1)}, u32[]{:S(2)}, u32[]{:S(2)}) collective-permute-start(bf16[64,18432]{1,0:T(8,128)(2,1)} %sums.16), channel_id=1, source_target_pairs={{0,2},{1,3},{2,0},{3,1},{4,6},{5,7},{6,4},{7,5}} | collective-permute-start | bytes 7077896 | tf_op jit(solution)/shard_map/ppermute | solution.py:394
  637.3 54.5 %collective-permute-start.52 = (bf16[64,18432]{1,0:T(8,128)(2,1)}, bf16[64,18432]{1,0:T(8,128)(2,1)}, u32[]{:S(2)}, u32[]{:S(2)}) collective-permute-start(bf16[64,18432]{1,0:T(8,128)(2,1)} %sums.18), channel_id=1, source_target_pairs={{0,4},{1,5},{2,6},{3,7},{4,0},{5,1},{6,2},{7,3}} | collective-permute-start | bytes 7077896 | tf_op jit(solution)/shard_map/ppermute | solution.py:394
  644.5 92.8 %collective-permute-start.62 = (bf16[64,18432]{1,0:T(8,128)(2,1)}, bf16[64,18432]{1,0:T(8,128)(2,1)}, u32[]{:S(2)}, u32[]{:S(2)}) collective-permute-start(bf16[64,18432]{1,0:T(8,128)(2,1)} %get-tuple-element.88), channel_id=1, source_target_pairs={{0,2},{1,3},{2,0},{3,1},{4,6},{5,7},{6,4},{7,5}} | collective-permute-start | bytes 7077896 | tf_op jit(solution)/shard_map/ppermute | solution.py:394
  645.3 97.0 %collective-permute-start.63 = (bf16[64,18432]{1,0:T(8,128)(2,1)}, bf16[64,18432]{1,0:T(8,128)(2,1)}, u32[]{:S(2)}, u32[]{:S(2)}) collective-permute-start(bf16[64,18432]{1,0:T(8,128)(2,1)} %get-tuple-element.90), channel_id=1, source_target_pairs={{0,4},{1,5},{2,6},{3,7},{4,0},{5,1},{6,2},{7,3}} | collective-permute-start | bytes 7077896 | tf_op jit(solution)/shard_map/ppermute | solution.py:394
  686.7 101.1 %collective-permute-start.76 = (bf16[64,18432]{1,0:T(8,128)(2,1)}, bf16[64,18432]{1,0:T(8,128)(2,1)}, u32[]{:S(2)}, u32[]{:S(2)}) collective-permute-start(bf16[64,18432]{1,0:T(8,128)(2,1)} %get-tuple-element.98), channel_id=1, source_target_pairs={{0,2},{1,3},{2,0},{3,1},{4,6},{5,7},{6,4},{7,5}} | collective-permute-start | bytes 7077896 | tf_op jit(solution)/shard_map/ppermute | solution.py:394
  691.8 101.1 %collective-permute-start.77 = (bf16[64,18432]{1,0:T(8,128)(2,1)}, bf16[64,18432]{1,0:T(8,128)(2,1)}, u32[]{:S(2)}, u32[]{:S(2)}) collective-permute-start(bf16[64,18432]{1,0:T(8,128)(2,1)} %get-tuple-element.100), channel_id=1, source_target_pairs={{0,4},{1,5},{2,6},{3,7},{4,0},{5,1},{6,2},{7,3}} | collective-permute-start | bytes 7077896 | tf_op jit(solution)/shard_map/ppermute | solution.py:394
  737.3 101.1 %collective-permute-start.45 = (bf16[64,18432]{1,0:T(8,128)(2,1)}, bf16[64,18432]{1,0:T(8,128)(2,1)}, u32[]{:S(2)}, u32[]{:S(2)}) collective-permute-start(bf16[64,18432]{1,0:T(8,128)(2,1)} %get-tuple-element.78), channel_id=1, source_target_pairs={{0,2},{1,3},{2,0},{3,1},{4,6},{5,7},{6,4},{7,5}} | collective-permute-start | bytes 7077896 | tf_op jit(solution)/shard_map/ppermute | solution.py:394
  742.4 101.1 %collective-permute-start.46 = (bf16[64,18432]{1,0:T(8,128)(2,1)}, bf16[64,18432]{1,0:T(8,128)(2,1)}, u32[]{:S(2)}, u32[]{:S(2)}) collective-permute-start(bf16[64,18432]{1,0:T(8,128)(2,1)} %get-tuple-element.80), channel_id=1, source_target_pairs={{0,4},{1,5},{2,6},{3,7},{4,0},{5,1},{6,2},{7,3}} | collective-permute-start | bytes 7077896 | tf_op jit(solution)/shard_map/ppermute | solution.py:394
  787.8 151.5 %collective-permute-start.64 = (bf16[64,18432]{1,0:T(8,128)(2,1)}, bf16[64,18432]{1,0:T(8,128)(2,1)}, u32[]{:S(2)}, u32[]{:S(2)}) collective-permute-start(bf16[64,18432]{1,0:T(8,128)(2,1)} %get-tuple-element.91), channel_id=1, source_target_pairs={{0,4},{1,5},{2,6},{3,7},{4,0},{5,1},{6,2},{7,3}} | collective-permute-start | bytes 7077896 | tf_op jit(solution)/shard_map/ppermute | solution.py:394
  792.9 147.4 %collective-permute-start.65 = (bf16[64,18432]{1,0:T(8,128)(2,1)}, bf16[64,18432]{1,0:T(8,128)(2,1)}, u32[]{:S(2)}, u32[]{:S(2)}) collective-permute-start(bf16[64,18432]{1,0:T(8,128)(2,1)} %get-tuple-element.92), channel_id=1, source_target_pairs={{0,2},{1,3},{2,0},{3,1},{4,6},{5,7},{6,4},{7,5}} | collective-permute-start | bytes 7077896 | tf_op jit(solution)/shard_map/ppermute | solution.py:394
  838.4 98.6 %collective-permute-start.78 = (bf16[32,18432]{1,0:T(8,128)(2,1)}, bf16[32,18432]{1,0:T(8,128)(2,1)}, u32[]{:S(2)}, u32[]{:S(2)}) collective-permute-start(bf16[32,18432]{1,0:T(8,128)(2,1)} %get-tuple-element.101), channel_id=1, source_target_pairs={{0,4},{1,5},{2,6},{3,7},{4,0},{5,1},{6,2},{7,3}} | collective-permute-start | bytes 3538952 | tf_op jit(solution)/shard_map/ppermute | solution.py:394
  843.5 94.6 %collective-permute-start.79 = (bf16[32,18432]{1,0:T(8,128)(2,1)}, bf16[32,18432]{1,0:T(8,128)(2,1)}, u32[]{:S(2)}, u32[]{:S(2)}) collective-permute-start(bf16[32,18432]{1,0:T(8,128)(2,1)} %get-tuple-element.102), channel_id=1, source_target_pairs={{0,2},{1,3},{2,0},{3,1},{4,6},{5,7},{6,4},{7,5}} | collective-permute-start | bytes 3538952 | tf_op jit(solution)/shard_map/ppermute | solution.py:394
  847.3 83.9 %collective-permute-start.80 = (bf16[16,18432]{1,0:T(8,128)(2,1)}, bf16[16,18432]{1,0:T(8,128)(2,1)}, u32[]{:S(2)}, u32[]{:S(2)}) collective-permute-start(bf16[16,18432]{1,0:T(8,128)(2,1)} %get-tuple-element.103), channel_id=1, source_target_pairs={{0,4},{1,5},{2,6},{3,7},{4,0},{5,1},{6,2},{7,3}} | collective-permute-start | bytes 1769480 | tf_op jit(solution)/shard_map/ppermute | solution.py:394
  (72 other events, 1346.7 us)
